TPU v7x, 16 devices: a whole 2x2x2 slice. The times are simulated.
16 devices in a mesh: tp: 2 (over z), dp: 8 (over y, x, core).
Axes of the slice: x: 2, y: 2, z: 2, core: 2. Of those that a mesh axis runs over, the one named last changes fastest.
Arguments:
- hid_q: bfloat16 [256, 512, 2048], P('dp')
- hid_d: bfloat16 [16, 512, 2048], P('dp')
- len_q: int32 [256], P('dp')
- len_d: int32 [16], P('dp')
- pos_doc: int32 [256], P('dp')
- w_q: bfloat16 [2048, 2048], P(None, 'tp')
- w_k: bfloat16 [2048, 1024], P(None, 'tp')
- w_v: bfloat16 [2048, 1024], P(None, 'tp')
- w_o: bfloat16 [2048, 2048], P('tp')
- w_gate: bfloat16 [2048, 6144], P(None, 'tp')
- w_up: bfloat16 [2048, 6144], P(None, 'tp')
- w_down: bfloat16 [6144, 2048], P('tp')
- g_in: bfloat16 [2048], replicated
- g_q: bfloat16 [128], replicated
- g_k: bfloat16 [128], replicated
- g_post: bfloat16 [2048], replicated
- g_final: bfloat16 [2048], replicated
Outputs:
- output 1: float32 [256], P('dp')
- output 2: bfloat16 [256, 512, 2048], P('dp')
- output 3: bfloat16 [16, 512, 2048], P('dp')
- output 4: float32 [2048, 2048], P(None, 'tp')
- output 5: float32 [2048, 1024], P(None, 'tp')
- output 6: float32 [2048, 1024], P(None, 'tp')
- output 7: float32 [2048, 2048], P('tp')
- output 8: float32 [2048, 6144], P(None, 'tp')
- output 9: float32 [2048, 6144], P(None, 'tp')
- output 10: float32 [6144, 2048], P('tp')
- output 11: float32 [2048], replicated
- output 12: float32 [128], replicated
- output 13: float32 [128], replicated
- output 14: float32 [2048], replicated
- output 15: float32 [2048], replicated
All inputs are finite; a program needn't handle non-finite values.
Results may differ from a plain program's by a relative error of at most 0.02.
Values sent between devices are 32-bit elements.
A program may use at most 1.25 GiB of HBM per device.

v0:
```python
import functools
import jax
import jax.numpy as jnp
from jax import lax
from jax.sharding import PartitionSpec as P

NORM_EPS = 1e-6
ROPE_THETA = 1000000.0
value_a11 = 0.05


def norm_rows(values, gain_vec):
    return values * lax.rsqrt(jnp.mean(values * values, axis=-1, keepdims=True) + NORM_EPS) * gain_vec


def norm_back(values, gain_vec, d_out):
    scale = lax.rsqrt(jnp.mean(values * values, axis=-1, keepdims=True) + NORM_EPS)
    g_dout = d_out * gain_vec
    d_values = scale * g_dout - values * scale ** 3 * jnp.mean(values * g_dout, axis=-1, keepdims=True)
    d_gain = jnp.sum((d_out * values * scale).reshape(-1, values.shape[-1]), axis=0)
    return d_values, d_gain


def rotate(values, angles):
    half_dim = values.shape[-1] // 2
    first_half = values[..., :half_dim]
    second_half = values[..., half_dim:]
    cos_a = jnp.cos(angles)
    sin_a = jnp.sin(angles)
    return jnp.concatenate([first_half * cos_a - second_half * sin_a, second_half * cos_a + first_half * sin_a], axis=-1)


def attend(q_raw, k_raw, v_raw, g_q, g_k, lens):
    head_dim = g_q.shape[0]
    n_seq, seq_len, kv_width = k_raw.shape
    n_kv = kv_width // head_dim
    group_size = q_raw.shape[1] // kv_width
    inv_freq = ROPE_THETA ** (-jnp.arange(0, head_dim, 2, dtype=jnp.float32) / head_dim)
    key_angle = jnp.arange(seq_len, dtype=jnp.float32)[:, None] * inv_freq
    key_rot = norm_rows(k_raw.reshape(n_seq, seq_len, n_kv, head_dim).astype(jnp.float32), g_k)
    key_rot = rotate(key_rot, key_angle[None, :, None, :]).astype(jnp.bfloat16)
    q_angle = (lens - 1).astype(jnp.float32)[:, None] * inv_freq
    query_rot = norm_rows(q_raw.reshape(n_seq, n_kv, group_size, head_dim).astype(jnp.float32), g_q)
    query_rot = rotate(query_rot, q_angle[:, None, None, :]).astype(jnp.bfloat16)
    scores = jnp.einsum('nkgd,nskd->nkgs', query_rot, key_rot, preferred_element_type=jnp.float32) * head_dim ** -0.5
    key_valid = jnp.arange(seq_len)[None, :] < lens[:, None]
    scores = jnp.where(key_valid[:, None, None, :], scores, -1e30)
    attn_prob = jax.nn.softmax(scores, axis=-1).astype(jnp.bfloat16)
    val_heads = v_raw.reshape(n_seq, seq_len, n_kv, head_dim)
    attn_mix = jnp.einsum('nkgs,nskd->nkgd', attn_prob, val_heads, preferred_element_type=jnp.float32)
    return attn_mix.astype(jnp.bfloat16).reshape(n_seq, q_raw.shape[1])


def swiglu(gate_in, up_in):
    return jax.nn.silu(gate_in) * up_in


def final_head(h_out, g_final):
    z_norm = norm_rows(h_out, g_final)
    return z_norm * lax.rsqrt(jnp.sum(z_norm * z_norm, axis=-1, keepdims=True))


def embed_fwd(hidden, lens, weights):
    w_q, w_k, w_v, w_o, w_gate, w_up, w_down, g_in, g_q, g_k, g_post, g_final = weights
    seq_len = hidden.shape[1]
    x_norm = norm_rows(hidden.astype(jnp.float32), g_in).astype(jnp.bfloat16)
    k_raw = jnp.einsum('nsd,de->nse', x_norm, w_k, preferred_element_type=jnp.float32).astype(jnp.bfloat16)
    v_raw = jnp.einsum('nsd,de->nse', x_norm, w_v, preferred_element_type=jnp.float32).astype(jnp.bfloat16)
    at_last = jnp.arange(seq_len)[None, :] == (lens - 1)[:, None]
    last_idx = (lens - 1)[:, None, None]
    x_last = jnp.take_along_axis(x_norm, last_idx, axis=1)[:, 0]
    h_last = jnp.take_along_axis(hidden, last_idx, axis=1)[:, 0].astype(jnp.float32)
    q_raw = jnp.dot(x_last, w_q, preferred_element_type=jnp.float32).astype(jnp.bfloat16)
    attn_out, attn_pull = jax.vjp(functools.partial(attend, lens=lens), q_raw, k_raw, v_raw, g_q, g_k)
    h_mid = h_last + lax.psum(jnp.dot(attn_out, w_o, preferred_element_type=jnp.float32), 'tp')
    y_norm = norm_rows(h_mid, g_post).astype(jnp.bfloat16)
    gate_val = jnp.dot(y_norm, w_gate, preferred_element_type=jnp.float32).astype(jnp.bfloat16)
    up_val = jnp.dot(y_norm, w_up, preferred_element_type=jnp.float32).astype(jnp.bfloat16)
    hidden_act, act_pull = jax.vjp(swiglu, gate_val.astype(jnp.float32), up_val.astype(jnp.float32))
    hidden_act = hidden_act.astype(jnp.bfloat16)
    h_out = h_mid + lax.psum(jnp.dot(hidden_act, w_down, preferred_element_type=jnp.float32), 'tp')
    emb_out, head_pull = jax.vjp(final_head, h_out, g_final)
    saved = (hidden, x_norm, at_last, x_last, attn_out, attn_pull, h_mid, y_norm, act_pull, hidden_act, head_pull)
    return emb_out, saved


def embed_bwd(saved, d_emb, weights):
    w_q, w_k, w_v, w_o, w_gate, w_up, w_down, g_in, g_q, g_k, g_post, g_final = weights
    hidden, x_norm, at_last, x_last, attn_out, attn_pull, h_mid, y_norm, act_pull, hidden_act, head_pull = saved
    d_hout, d_gfinal = head_pull(d_emb)
    d_hout_b = d_hout.astype(jnp.bfloat16)
    d_act = jnp.einsum('nd,fd->nf', d_hout_b, w_down, preferred_element_type=jnp.float32).astype(jnp.bfloat16)
    d_wdown = jnp.einsum('nf,nd->fd', hidden_act, d_hout_b, preferred_element_type=jnp.float32)
    d_gate, d_up = act_pull(d_act.astype(jnp.float32))
    d_gate = d_gate.astype(jnp.bfloat16)
    d_up = d_up.astype(jnp.bfloat16)
    d_wgate = jnp.einsum('nd,nf->df', y_norm, d_gate, preferred_element_type=jnp.float32)
    d_wup = jnp.einsum('nd,nf->df', y_norm, d_up, preferred_element_type=jnp.float32)
    d_y = lax.psum(jnp.einsum('nf,df->nd', d_gate, w_gate, preferred_element_type=jnp.float32) + jnp.einsum('nf,df->nd', d_up, w_up, preferred_element_type=jnp.float32), 'tp')
    d_ymid, d_gpost = norm_back(h_mid, g_post, d_y)
    d_hmid = d_hout + d_ymid
    d_hmid_b = d_hmid.astype(jnp.bfloat16)
    d_attn = jnp.einsum('nd,ed->ne', d_hmid_b, w_o, preferred_element_type=jnp.float32).astype(jnp.bfloat16)
    d_wo = jnp.einsum('ne,nd->ed', attn_out, d_hmid_b, preferred_element_type=jnp.float32)
    d_qraw, d_kraw, d_vraw, d_gq, d_gk = attn_pull(d_attn)
    d_wq = jnp.einsum('nd,ne->de', x_last, d_qraw, preferred_element_type=jnp.float32)
    d_wk = jnp.einsum('nsd,nse->de', x_norm, d_kraw, preferred_element_type=jnp.float32)
    d_wv = jnp.einsum('nsd,nse->de', x_norm, d_vraw, preferred_element_type=jnp.float32)
    d_xlast = jnp.einsum('ne,de->nd', d_qraw, w_q, preferred_element_type=jnp.float32)
    d_x = jnp.einsum('nse,de->nsd', d_kraw, w_k, preferred_element_type=jnp.float32) + jnp.einsum('nse,de->nsd', d_vraw, w_v, preferred_element_type=jnp.float32)
    d_x = lax.psum(jnp.where(at_last[:, :, None], d_x + d_xlast[:, None, :], d_x), 'tp')
    d_hid, d_gin = norm_back(hidden.astype(jnp.float32), g_in, d_x)
    d_hid = jnp.where(at_last[:, :, None], d_hid + d_hmid[:, None, :], d_hid)
    return d_hid.astype(jnp.bfloat16), (d_wq, d_wk, d_wv, d_wo, d_wgate, d_wup, d_wdown, d_gin, d_gq, d_gk, d_gpost, d_gfinal)


def solution(mesh):
    dp_size = mesh.shape['dp']

    def device_step(hid_q, hid_d, len_q, len_d, pos_doc, w_q, w_k, w_v, w_o, w_gate, w_up, w_down, g_in, g_q, g_k, g_post, g_final):
        weights = (w_q, w_k, w_v, w_o, w_gate, w_up, w_down) + tuple(gain_vec.astype(jnp.float32) for gain_vec in (g_in, g_q, g_k, g_post, g_final))
        n_query = hid_q.shape[0] * dp_size
        emb_q, saved_q = embed_fwd(hid_q, len_q, weights)
        emb_d, saved_d = embed_fwd(hid_d, len_d, weights)
        all_docs = lax.all_gather(emb_d, 'dp', axis=0, tiled=True)
        logits = jnp.einsum('qd,kd->qk', emb_q, all_docs, precision=lax.Precision.HIGHEST) / value_a11
        log_norm = jax.nn.logsumexp(logits, axis=1)
        is_pos = jnp.arange(all_docs.shape[0])[None, :] == pos_doc[:, None]
        pos_logit = jnp.sum(jnp.where(is_pos, logits, 0.0), axis=1)
        loss_rows = log_norm - pos_logit
        d_logits = (jnp.exp(logits - log_norm[:, None]) - is_pos.astype(jnp.float32)) / (n_query * value_a11)
        d_emb_q = jnp.einsum('qk,kd->qd', d_logits, all_docs, precision=lax.Precision.HIGHEST)
        d_docs = jnp.einsum('qk,qd->kd', d_logits, emb_q, precision=lax.Precision.HIGHEST)
        d_emb_d = lax.psum_scatter(d_docs, 'dp', scatter_dimension=0, tiled=True)
        d_hid_q, grads_q = embed_bwd(saved_q, d_emb_q, weights)
        d_hid_d, grads_d = embed_bwd(saved_d, d_emb_d, weights)
        grads = [grad_a + grad_b for grad_a, grad_b in zip(grads_q, grads_d)]
        head_grads = lax.psum((grads[8], grads[9]), ('tp', 'dp'))
        dp_grads = lax.psum(tuple(grads[:8]) + (grads[10], grads[11]), 'dp')
        return (loss_rows, d_hid_q, d_hid_d) + tuple(dp_grads[:8]) + tuple(head_grads) + tuple(dp_grads[8:])

    col_split = P(None, 'tp')
    row_split = P('tp', None)
    in_specs = (P('dp'), P('dp'), P('dp'), P('dp'), P('dp'), col_split, col_split, col_split, row_split, col_split, col_split, row_split, P(), P(), P(), P(), P())
    out_specs = (P('dp'), P('dp'), P('dp'), col_split, col_split, col_split, row_split, col_split, col_split, row_split, P(), P(), P(), P(), P())
    return jax.shard_map(device_step, mesh=mesh, in_specs=in_specs, out_specs=out_specs, check_vma=False)
```

profile of v0, /device:TPU:0, one launch (start us, length us, event | category | flops | bytes accessed | tf_op | source)
XLA Modules:
  0.0 5020.1 jit_solution(13885734717212642548)
XLA Ops:
  16.8 20.9 fusion.3
  39.0 44.7 fusion.5
  90.4 42.1 convolution_convert_fusion.1
  132.5 42.4 multiply_reduce_fusion.2
  175.6 23.7 copy.159
  199.9 23.2 multiply_multiply_fusion
  223.1 33.7 subtract_convert_fusion
  256.9 16.0 fusion.132
  272.9 8.3 convolution_convert_fusion.14
  293.1 5.2 fusion.15
  300.5 6.4 fusion.45
  333.0 10.2 psum.142
  345.3 6.5 fusion.26
  351.8 7.1 multiply_convert_fusion.4
  360.7 6.7 psum.143
  373.9 7.0 fusion.23
  380.9 7.8 multiply_convert_fusion.1
  393.1 9.9 all-gather
  405.6 7.6 all-reduce.22.cloned.1.call-done
  425.8 8.9 multiply_convert_fusion
  435.5 8.5 fusion.138
  444.0 4.5 convolution_add_fusion.5
  448.8 19.9 all-reduce.30.cloned.1.call-done
  473.4 8.1 multiply_convert_fusion.3
  481.5 8.1 fusion.127
  493.6 9.5 psum.146
  506.0 4.0 convolution_convert_fusion.17
  528.4 4.1 fusion.140
  544.9 9.5 add_select_fusion.3
  561.8 8.7 convolution_convert_fusion
  570.5 8.2 multiply_reduce_fusion.6
  578.7 15.6 fusion.53
  594.4 13.9 convert_bitcast_fusion
  610.2 4.3 fusion.139
  614.5 44.7 multiply_add_fusion.1
  659.2 36.5 multiply_reduce_fusion
  696.0 37.2 fusion.11
  733.1 22.6 copy.172
  755.7 52.5 %fusion.37 = f32[32,512,2048]{2,1,0:T(8,128)} fusion(bf16[32,512,512]{1,2,0:T(8,128)(2,1)} %bitcast.212, bf16[2048,512]{1,0:T(8,128)(2,1)S(1)} %copy-done), kind=kOutput, calls=%fused_computation.86 | convolution fusion | flops 34359738368 | bytes 153092096 | tf_op jit(solution)/shard_map/nse,de->nsd/dot_general | solution.py:110
  808.3 113.8 %add_select_fusion.1 = f32[32,512,2048]{2,1,0:T(8,128)} fusion(f32[32,512,2048]{2,1,0:T(8,128)} %fusion.37, f32[32,2048]{1,0:T(8,128)S(1)} %copy-done.75, pred[32,512]{1,0:T(8,128)(4,1)S(1)} %copy-done.101, bf16[32,512,512]{1,2,0:T(8,128)(2,1)} %bitcast.210, bf16[2048,512]{1,0:T(8,128)(2,1)} %param.28), kind=kOutput, calls=%fused_computation.12 | convolution fusion | flops 34460401664 | bytes 287588352 | tf_op jit(solution)/shard_map/nse,de->nsd/dot_general | solution.py:110
  923.1 11.1 fusion.144
  934.3 10.8 fusion.143
  945.1 10.8 fusion.85
  955.9 4.5 fusion.141
  960.5 4.5 fusion.142
  965.0 16.5 convolution_add_fusion.1
  981.6 16.8 convolution_add_fusion.2
  998.4 16.6 convolution_add_fusion
  1017.8 4.8 convolution_add_fusion.4
  1022.5 4.7 convolution_add_fusion.3
  1027.2 47.0 bitcast_add_fusion
  1074.1 47.0 bitcast_add_fusion.1
  1122.0 32.1 all-reduce.9
  1154.1 6.1 fusion.20
  1162.4 4.1 fusion.12
  1166.5 2656.1 %all-reduce.26.cloned.1.call-done = f32[32,512,2048]{2,1,0:T(8,128)} async-done(((f32[32,512,2048]{2,1,0:T(8,128)}), f32[32,512,2048]{2,1,0:T(8,128)}) %all-reduce.26.cloned.1.call-update) | async-done | bytes 134217744 | tf_op jit(solution)/shard_map/psum | solution.py:111
  3822.6 60.5 %fusion.10 = (f32[2048]{0:T(1024)S(1)}, f32[32,512]{1,0:T(8,128)S(1)}) fusion(f32[32,512,2048]{2,1,0:T(8,128)} %all-reduce.26.cloned.1.call-done, bf16[32,512,2048]{2,1,0:T(8,128)(2,1)} %param.21, f32[32,512]{1,0:T(8,128)S(1)} %copy-done.47, f32[2048]{0:T(1024)S(1)} %copy-done.64), kind=kLoop, calls=%fused_computation.21 | loop fusion | flops 234862592 | bytes 201474048 | tf_op jit(solution)/shard_map/reduce_sum | solution.py:20
  3883.1 25.3 all-reduce.10
  3908.4 83.6 %fusion.2 = bf16[32,512,2048]{2,1,0:T(8,128)(2,1)} fusion(bf16[32,512,2048]{2,1,0:T(8,128)(2,1)} %param.21, f32[32,512,2048]{2,1,0:T(8,128)} %all-reduce.26.cloned.1.call-done, f32[32,2048]{1,0:T(8,128)S(1)} %copy-done.26, f32[32,512]{1,0:T(8,128)S(1)} %broadcast_multiply_fusion, f32[32,512]{1,0:T(8,128)S(1)} %copy-done.72, f32[2048]{0:T(1024)S(1)} %copy-done.64, ...), kind=kLoop, calls=%fused_computation.13 | loop fusion | flops 301989888 | bytes 268918784 | tf_op jit(solution)/shard_map/convert_element_type | solution.py:114
  3992.0 954.0 %all-reduce.32.cloned.1.call-done = (f32[2048,1024]{1,0:T(8,128)}, f32[2048,512]{1,0:T(8,128)}, f32[2048,512]{1,0:T(8,128)}, f32[1024,2048]{1,0:T(8,128)}, f32[2...) async-done(((f32[2048,1024]{1,0:T(8,128)}, f32[2048,512]{1,0:T(8,128)}, f32[2048,512]{1,0:T(8,128)}, f32[1024,2048]{1,0:T(8,128)}, ...) | async-done | bytes 100663312 | tf_op jit(solution)/shard_map/psum | solution.py:139
  4946.0 8.6 copy.231
  4964.7 19.6 copy.235
  4984.3 19.6 copy.236
  5004.0 9.0 copy.237
  (522 shorter events, 157.0 us)
Async XLA Ops:
  7.2 125.3 %copy-start = (bf16[2048,512]{1,0:T(8,128)(2,1)S(1)}, bf16[2048,512]{1,0:T(8,128)(2,1)}, u32[]{:S(2)}) copy-start(bf16[2048,512]{1,0:T(8,128)(2,1)} %param.27) | copy-start | bytes 6291460
  7.2 364.7 %all-reduce.20.cloned.1.call-start = ((), (), s32[]{:S(2)}) async-start(), calls=%async_computation | async-start | bytes 524288 | tf_op jit(solution)/shard_map/psum | solution.py:75
  8.1 77.3 %copy-start.131 = (pred[32]{0:T(512)(128)(4,1)}, pred[32]{0:T(512)(128)(4,1)S(1)}, u32[]{:S(2)}) copy-start(pred[32]{0:T(512)(128)(4,1)S(1)} %and_bitcast_fusion.1) | copy-start | bytes 100
  13.6 70.1 %copy-start.36 = (s32[32]{0:T(128)}, s32[32]{0:T(128)S(1)}, u32[]{:S(2)}) copy-start(s32[32]{0:T(128)S(1)} %or_bitcast_fusion) | copy-start | bytes 388
  14.3 24.0 copy-start.62
  89.2 43.2 copy-start.31
  89.6 42.9 copy-start.108
  175.0 24.9 copy-start.22
  175.6 23.8 copy-start.32
  175.6 23.8 copy-start.51
  175.6 23.8 copy-start.126
  175.6 24.0 copy-start.89
  175.6 24.0 copy-start.91
  175.6 24.2 copy-start.122
  199.9 57.0 %copy-start.57 = (bf16[32,4,2,64]{3,2,1,0:T(2,128)(2,1)}, bf16[32,4,2,64]{3,2,1,0:T(2,128)(2,1)S(1)}, u32[]{:S(2)}) copy-start(bf16[32,4,2,64]{3,2,1,0:T(2,128)(2,1)S(1)} %get-tuple-element.79) | copy-start | bytes 98308
  199.9 23.2 copy-start.12
  199.9 23.2 copy-start.14
  223.1 33.8 copy-start.68
  272.9 17.6 copy-start.8
  272.9 20.2 copy-start.63
  281.3 19.2 copy-start.53
  285.0 128.2 %all-reduce.22.cloned.1.call-start = ((), (), s32[]{:S(2)}) async-start(), calls=%async_computation.1 | async-start | bytes 524288 | tf_op jit(solution)/shard_map/psum | solution.py:81
  310.6 245.6 %copy-start.44 = (f32[2048]{0:T(1024)}, f32[2048]{0:T(1024)S(1)}, u32[]{:S(2)}) copy-start(f32[2048]{0:T(1024)S(1)} %convert_element_type.286) | copy-start | bytes 24580
  324.5 20.2 copy-start.87
  324.5 20.2 copy-start.88
  327.1 41.3 copy-start.93
  344.1 23.2 copy-start.61
  392.4 76.3 %all-reduce.30.cloned.1.call-start = ((), (), s32[]{:S(2)}) async-start(), calls=%async_computation.5 | async-start | bytes 262144
  414.4 141.8 %copy-start.6 = (f32[32,2048]{1,0:T(8,128)}, f32[32,2048]{1,0:T(8,128)S(1)}, u32[]{:S(2)}) copy-start(f32[32,2048]{1,0:T(8,128)S(1)} %get-tuple-element.55) | copy-start | bytes 786436
  422.7 131.8 %all-reduce.24.cloned.1.call-start = ((), (), s32[]{:S(2)}) async-start(), calls=%async_computation.2 | async-start | bytes 524288 | tf_op jit(solution)/shard_map/psum | solution.py:99
  425.8 18.2 slice-start.6
  425.8 18.2 slice-start.7
  448.6 705.5 %all-reduce.28.cloned.1.call-start = ((), (), s32[]{:S(2)}) async-start(), calls=%async_computation.4 | async-start | bytes 16777216 | tf_op jit(solution)/shard_map/psum | solution.py:111
  544.9 16.8 copy-start.9
  554.5 3268.1 %all-reduce.26.cloned.1.call-start = ((), (), s32[]{:S(2)}) async-start(), calls=%async_computation.3 | async-start | bytes 268435456 | tf_op jit(solution)/shard_map/psum | solution.py:111
  594.4 20.1 copy-start.13
  594.4 20.1 copy-start.15
  610.2 49.0 copy-start.55
  614.5 44.7 copy-start.23
  614.5 44.7 copy-start.125
  659.2 36.5 copy-start.49
  755.7 52.5 %copy-start.75 = (f32[32,2048]{1,0:T(8,128)S(1)}, f32[32,2048]{1,0:T(8,128)}, u32[]{:S(2)}) copy-start(f32[32,2048]{1,0:T(8,128)} %fusion.139) | copy-start | bytes 786436
  755.7 52.5 %copy-start.101 = (pred[32,512]{1,0:T(8,128)(4,1)S(1)}, pred[32,512]{1,0:T(8,128)(4,1)}, u32[]{:S(2)}) copy-start(pred[32,512]{1,0:T(8,128)(4,1)} %iota_compare_fusion) | copy-start | bytes 49156
  922.1 4023.9 %all-reduce.32.cloned.1.call-start = ((), (), s32[]{:S(2)}) async-start(), calls=%async_computation.6 | async-start | bytes 201326592 | tf_op jit(solution)/shard_map/psum | solution.py:139
  981.6 16.8 copy-start.74
  981.6 16.8 copy-start.82
  998.3 16.7 copy-start.43
  998.3 16.7 copy-start.56
  998.4 16.6 copy-start.133
  1121.2 32.8 copy-start.64
  1121.2 32.8 copy-start.100
  1121.3 38.9 copy-start.80
  1121.3 38.9 copy-start.119
  1121.3 38.9 copy-start.128
  1154.1 2668.5 %copy-start.47 = (f32[32,512]{1,0:T(8,128)S(1)}, f32[32,512]{1,0:T(8,128)}, u32[]{:S(2)}) copy-start(f32[32,512]{1,0:T(8,128)} %copy-done.46) | copy-start | bytes 196612
  1166.5 2741.9 %copy-start.26 = (f32[32,2048]{1,0:T(8,128)S(1)}, f32[32,2048]{1,0:T(8,128)}, u32[]{:S(2)}) copy-start(f32[32,2048]{1,0:T(8,128)} %copy-done.24) | copy-start | bytes 786436
  1166.5 2741.9 %copy-start.72 = (f32[32,512]{1,0:T(8,128)S(1)}, f32[32,512]{1,0:T(8,128)}, u32[]{:S(2)}) copy-start(f32[32,512]{1,0:T(8,128)} %get-tuple-element.80) | copy-start | bytes 196612
  1166.5 2741.9 %copy-start.102 = (pred[32,512]{1,0:T(8,128)(4,1)S(1)}, pred[32,512]{1,0:T(8,128)(4,1)}, u32[]{:S(2)}) copy-start(pred[32,512]{1,0:T(8,128)(4,1)} %iota_compare_fusion) | copy-start | bytes 49156
  4964.6 39.3 slice-start.12
  4964.6 39.3 slice-start.13
  4964.6 39.3 slice-start.14
  4984.3 19.7 slice-start.15
  4984.3 19.7 slice-start.16
  4984.3 19.7 slice-start.17
  (122 other events, 928.5 us)
Sparse Core Ops, SparseCore 0:
  285.2 22.1 all-reduce.19
  392.5 20.7 all-reduce.21
  422.9 45.7 all-reduce.29
  470.8 18.6 all-reduce.23
  554.6 192.5 all-reduce.27
  922.2 2900.3 all-reduce.25
  3828.9 1117.0 all-reduce.31
where the time goes:
time: 5030 us; the launch traced here: 5020 us
  waiting for transfers between devices  3640 us (72%)
  matrix products  667 us (13%)
  other arithmetic  462 us (9%)
  local copies, waits for them, and re-layouts  142 us (3%)
  blocking collectives  93.7 us (2%)
    psum x2, waiting for transfers between devices, embed_bwd(): lax.psum(jnp.where(at_last[:, :, None], d_x + d_xlast[:, None, :], d_x),...  2660 us
    psum x1, waiting for transfers between devices, device_step(): dp_grads = lax.psum(tuple(grads[:8]) + (grads[10], grads[11]), 'dp')  954 us
    dot_general x2, matrix products, embed_bwd(): jnp.einsum('nse,de->nsd', d_vraw, w_v, preferred_element_type=jnp.float32)  123 us
  transfers between devices with their start and end apart: 7, of which 4 were waited for; matrix products, arithmetic and copies ran while one was open for 18% of the time, Pallas kernels for 0%

commit v1 on v0

v1 whole, which is shorter than its diff:
```python
import functools
import jax
import jax.numpy as jnp
from jax import lax
from jax.experimental import pallas as pl
from jax.experimental.pallas import tpu as pltpu
from jax.sharding import PartitionSpec as P

NORM_EPS = 1e-6
ROPE_THETA = 1000000.0
TEMPERATURE = 0.05
HEAD = 128
Q_MAX = 128
BF = jnp.bfloat16
F32 = jnp.float32
SWAP = [(0, 1), (1, 0)]
VMEM = 60 * 1024 * 1024


def norm_rows(values, gain_vec):
    return values * lax.rsqrt(jnp.mean(values * values, axis=-1, keepdims=True) + NORM_EPS) * gain_vec


def norm_back(values, gain_vec, d_out):
    scale = lax.rsqrt(jnp.mean(values * values, axis=-1, keepdims=True) + NORM_EPS)
    g_dout = d_out * gain_vec
    d_values = scale * g_dout - values * scale ** 3 * jnp.mean(values * g_dout, axis=-1, keepdims=True)
    d_gain = jnp.sum((d_out * values * scale).reshape(-1, values.shape[-1]), axis=0)
    return d_values, d_gain


def rope_tables(positions):
    inv_freq = ROPE_THETA ** (-jnp.arange(0, HEAD, 2, dtype=F32) / HEAD)
    angles = positions.astype(F32)[:, None] * inv_freq
    cos_a, sin_a = jnp.cos(angles), jnp.sin(angles)
    return jnp.concatenate([cos_a, cos_a], axis=-1), jnp.concatenate([-sin_a, sin_a], axis=-1)


def rotate_query(q_raw, g_q, cos_t, sin_t):
    n_seq = q_raw.shape[0]
    normed = norm_rows(q_raw.reshape(n_seq, -1, HEAD).astype(F32), g_q)
    half = HEAD // 2
    swapped = jnp.concatenate([normed[..., half:], normed[..., :half]], axis=-1)
    return (normed * cos_t[:, None, :] + swapped * sin_t[:, None, :]).astype(BF)


def head_mask(n_rows, width):
    row_head = lax.broadcasted_iota(jnp.int32, (n_rows, width), 0) // 2
    lane_head = lax.broadcasted_iota(jnp.int32, (n_rows, width), 1) // HEAD
    return row_head == lane_head


def block_diag(per_head):
    n_seq, n_q, _ = per_head.shape
    n_kv = n_q // 2
    wide = jnp.tile(per_head, (1, 1, n_kv))
    wide = jnp.where(head_mask(n_q, n_kv * HEAD)[None], wide, jnp.zeros_like(wide))
    return jnp.pad(wide, ((0, 0), (0, 16 - n_q), (0, 0)))


def take_diag(wide):
    kept = jnp.where(head_mask(wide.shape[0], wide.shape[1]), wide, 0.0)
    total = kept[:, :HEAD]
    for head in range(1, wide.shape[1] // HEAD):
        total = total + kept[:, head * HEAD:(head + 1) * HEAD]
    return total


def key_stats(k_raw):
    k_f = k_raw.astype(F32)
    scale = lax.rsqrt(jnp.mean(k_f * k_f, axis=-1, keepdims=True) + NORM_EPS)
    return k_f * scale, scale


def turn(values, cos_t, sin_t):
    return values * cos_t + pltpu.roll(values, HEAD // 2, 1) * sin_t


def variants(max_len, sizes, body):
    low = 0
    for size in sizes:
        pl.when(jnp.logical_and(max_len > low, max_len <= size))(functools.partial(body, size))
        low = size


NT = (((1,), (1,)), ((), ()))
TN = (((0,), (0,)), ((), ()))


def fwd_body(do_norm, group, sizes, order_ref, lens_ref, *refs):
    h_refs, refs = refs[:group if do_norm else 1], refs[group if do_norm else 1:]
    if do_norm:
        gin_ref, w_ref, qbd_ref, gk_ref, cos_ref, sin_ref, x_ref, kv_ref, p_ref, o_ref = refs
        for g in range(group):
            hid = h_refs[g][0].astype(F32)
            scale = lax.rsqrt(jnp.mean(hid * hid, axis=-1, keepdims=True) + NORM_EPS)
            x_ref[g] = (hid * scale * gin_ref[...]).astype(BF)
    else:
        w_ref, qbd_ref, gk_ref, cos_ref, sin_ref, kv_ref, p_ref, o_ref = refs
        x_ref = h_refs[0]
    width = w_ref.shape[1]
    kv_half = width // 2
    step = pl.program_id(0)

    def run(size):
        def project(j, carry):
            cols = pl.ds(pl.multiple_of(j * 256, 256), 256)
            x_val = x_ref[:, :size, :].reshape(group * size, x_ref.shape[2])
            out = jnp.dot(x_val, w_ref[:, cols], preferred_element_type=F32)
            kv_ref[:, :size, cols] = out.astype(BF).reshape(group, size, 256)
            return carry

        lax.fori_loop(0, width // 256, project, 0)
        cos_t, sin_t = cos_ref[:size], sin_ref[:size]
        for g in range(group):
            length = lens_ref[step * group + g]
            k_rot = []
            for head in range(kv_half // HEAD):
                k_hat, _ = key_stats(kv_ref[g, :size, head * HEAD:(head + 1) * HEAD])
                k_rot.append(turn(k_hat * gk_ref[...], cos_t, sin_t).astype(BF))
            k_rot = jnp.concatenate(k_rot, axis=-1)
            scores = lax.dot_general(qbd_ref[g], k_rot, NT, preferred_element_type=F32) * HEAD ** -0.5
            valid = lax.broadcasted_iota(jnp.int32, scores.shape, 1) < length
            scores = jnp.where(valid, scores, -1e30)
            expd = jnp.exp(scores - jnp.max(scores, axis=-1, keepdims=True))
            prob = expd / jnp.sum(expd, axis=-1, keepdims=True)
            p_ref[g, :, :size] = prob
            mix = jnp.dot(prob.astype(BF), kv_ref[g, :size, kv_half:], preferred_element_type=F32)
            o_ref[g] = take_diag(mix)

    variants(lens_ref[step * group + group - 1], sizes, run)


def attn_fwd(hid_or_x, order, lens, rows, group, sizes, w_kv, qbd, g_k, cos_t, sin_t, g_in=None):
    n_seq, width = order.shape[0], w_kv.shape[1]
    model = w_kv.shape[0]
    do_norm = g_in is not None
    once = dict(pipeline_mode=pl.Buffered(buffer_count=1))
    by_group = lambda *shape: pl.BlockSpec((group,) + shape, lambda i, o, l: (i,) + (0,) * len(shape))
    whole = lambda arr: pl.BlockSpec(arr.shape, lambda i, o, l: (0,) * arr.ndim, **once)
    if do_norm:
        in_specs = [pl.BlockSpec((1, rows, model), lambda i, o, l, g=g: (o[i * group + g], 0, 0)) for g in range(group)]
        operands = [hid_or_x] * group + [g_in]
        in_specs.append(whole(g_in))
    else:
        in_specs, operands = [by_group(rows, model)], [hid_or_x]
    in_specs += [whole(w_kv), by_group(16, width // 2), whole(g_k), whole(cos_t), whole(sin_t)]
    operands += [w_kv, qbd, g_k, cos_t, sin_t]
    out_specs = [by_group(rows, width), by_group(16, rows), by_group(16, HEAD)]
    out_shape = [jax.ShapeDtypeStruct((n_seq, rows, width), BF), jax.ShapeDtypeStruct((n_seq, 16, rows), F32), jax.ShapeDtypeStruct((n_seq, 16, HEAD), F32)]
    if do_norm:
        out_specs.insert(0, by_group(rows, model))
        out_shape.insert(0, jax.ShapeDtypeStruct((n_seq, rows, model), BF))
    return pl.pallas_call(
        functools.partial(fwd_body, do_norm, group, sizes),
        grid_spec=pltpu.PrefetchScalarGridSpec(num_scalar_prefetch=2, grid=(n_seq // group,), in_specs=in_specs, out_specs=out_specs),
        out_shape=out_shape,
        compiler_params=pltpu.CompilerParams(dimension_semantics=("arbitrary",), vmem_limit_bytes=VMEM),
        cost_estimate=pl.CostEstimate(flops=2 * n_seq * rows * model * width, bytes_accessed=n_seq * rows * model * 4, transcendentals=0),
        name="attn_fwd" + ("_norm" if do_norm else "") + str(rows),
    )(order, lens, *operands)


def bwd_body(group, sizes, lens_ref, kv_ref, p_ref, qbd_ref, dobd_ref, gk_ref, cos_ref, sin_ref, dkv_ref, dq_ref, dgk_ref):
    step = pl.program_id(0)
    rows, width = kv_ref.shape[1], kv_ref.shape[2]
    kv_half = width // 2

    @pl.when(step == 0)
    def _():
        dgk_ref[...] = jnp.zeros_like(dgk_ref)

    def run(size):
        cos_t, sin_t = cos_ref[:size], sin_ref[:size]
        gk = gk_ref[...]
        for g in range(group):
            prob = p_ref[g, :, :size]
            qbd, dobd = qbd_ref[g], dobd_ref[g]
            d_prob = lax.dot_general(dobd, kv_ref[g, :size, kv_half:], NT, preferred_element_type=F32)
            d_prob = d_prob.astype(BF).astype(F32)
            d_score = prob * (d_prob - jnp.sum(prob * d_prob, axis=-1, keepdims=True))
            d_score = (d_score * HEAD ** -0.5).astype(BF)
            d_key = lax.dot_general(d_score, qbd, TN, preferred_element_type=F32)
            d_val = lax.dot_general(prob.astype(BF), dobd, TN, preferred_element_type=F32)
            dkv_ref[g, :size, kv_half:] = d_val.astype(BF)
            k_rot = []
            d_gain = jnp.zeros((size, HEAD), F32)
            for head in range(kv_half // HEAD):
                lanes = slice(head * HEAD, (head + 1) * HEAD)
                k_hat, scale = key_stats(kv_ref[g, :size, lanes])
                k_rot.append(turn(k_hat * gk, cos_t, sin_t).astype(BF))
                d_norm = turn(d_key[:, lanes].astype(BF).astype(F32), cos_t, -sin_t)
                d_gain = d_gain + d_norm * k_hat
                d_hat = d_norm * gk
                d_raw = scale * (d_hat - k_hat * jnp.mean(k_hat * d_hat, axis=-1, keepdims=True))
                dkv_ref[g, :size, lanes] = d_raw.astype(BF)
            d_query = jnp.dot(d_score, jnp.concatenate(k_rot, axis=-1), preferred_element_type=F32)
            dq_ref[g] = take_diag(d_query)
            dgk_ref[...] += jnp.sum(d_gain.reshape(size // 8, 8, HEAD), axis=0)
            if size < rows:
                dkv_ref[g, size:, :] = jnp.zeros((rows - size, width), BF)

    variants(lens_ref[step * group + group - 1], sizes, run)


def attn_bwd(lens, group, sizes, kv, prob, qbd, dobd, g_k, cos_t, sin_t):
    n_seq, rows, width = kv.shape
    once = dict(pipeline_mode=pl.Buffered(buffer_count=1))
    by_group = lambda *shape: pl.BlockSpec((group,) + shape, lambda i, l: (i,) + (0,) * len(shape))
    whole = lambda arr: pl.BlockSpec(arr.shape, lambda i, l: (0,) * arr.ndim, **once)
    return pl.pallas_call(
        functools.partial(bwd_body, group, sizes),
        grid_spec=pltpu.PrefetchScalarGridSpec(
            num_scalar_prefetch=1, grid=(n_seq // group,),
            in_specs=[by_group(rows, width), by_group(16, rows), by_group(16, width // 2), by_group(16, width // 2), whole(g_k), whole(cos_t), whole(sin_t)],
            out_specs=[by_group(rows, width), by_group(16, HEAD), pl.BlockSpec((8, HEAD), lambda i, l: (0, 0))]),
        out_shape=[jax.ShapeDtypeStruct(kv.shape, BF), jax.ShapeDtypeStruct((n_seq, 16, HEAD), F32), jax.ShapeDtypeStruct((8, HEAD), F32)],
        compiler_params=pltpu.CompilerParams(dimension_semantics=("arbitrary",), vmem_limit_bytes=VMEM),
        cost_estimate=pl.CostEstimate(flops=20 * 1000 * n_seq * rows * width // 8, bytes_accessed=n_seq * rows * width * 4, transcendentals=0),
        name="attn_bwd" + str(rows),
    )(lens, kv, prob, qbd, dobd, g_k, cos_t, sin_t)


def dx_body(group, sizes, order_ref, lens_ref, dkv_ref, dkv2_ref, w_ref, w2_ref, h_ref, gin_ref, dxl_ref, dhm_ref, out_ref, dgin_ref, dx_ref):
    step = pl.program_id(0)
    rows, model = h_ref.shape[1], h_ref.shape[2]
    width = w_ref.shape[1]
    length = lens_ref[step]
    inner = lax.rem(step, group)

    @pl.when(step == 0)
    def _():
        dgin_ref[...] = jnp.zeros_like(dgin_ref)

    def run(size):
        @pl.when(inner == 0)
        def _():
            def project(j, carry):
                cols = pl.ds(pl.multiple_of(j * 256, 256), 256)
                d_own = dkv_ref[:, :size, :].reshape(group * size, width)
                part = lax.dot_general(d_own, w_ref[cols, :], NT, preferred_element_type=F32)
                dx_ref[:, :size, cols] = part.reshape(group, size, 256)
                return carry

            def project_other(j, carry):
                cols = pl.ds(pl.multiple_of(j * 256, 256), 256)
                d_oth = dkv2_ref[:, :size, :].reshape(group * size, width)
                part = lax.dot_general(d_oth, w2_ref[cols, :], NT, preferred_element_type=F32)
                dx_ref[:, :size, cols] += part.reshape(group, size, 256)
                return carry

            lax.fori_loop(0, model // 256, project, 0)
            lax.fori_loop(0, model // 256, project_other, 0)

        chunk = 32
        gin = gin_ref[...]

        def finish(c, carry):
            start = pl.multiple_of(c * chunk, chunk)
            here = pl.ds(start, chunk)
            hid = h_ref[0, here, :].astype(F32)
            at_last = lax.broadcasted_iota(jnp.int32, (chunk, 1), 0) + start == length - 1
            d_x = dx_ref[inner, here, :] + jnp.where(at_last, dxl_ref[0], 0.0)
            scale = lax.rsqrt(jnp.mean(hid * hid, axis=-1, keepdims=True) + NORM_EPS)
            h_hat = hid * scale
            dgin_ref[...] += jnp.sum((d_x * h_hat).reshape(chunk // 8, 8, model), axis=0)
            g_dx = d_x * gin
            d_hid = scale * (g_dx - h_hat * jnp.mean(h_hat * g_dx, axis=-1, keepdims=True))
            out_ref[0, here, :] = (d_hid + jnp.where(at_last, dhm_ref[0], 0.0)).astype(BF)
            return carry

        lax.fori_loop(0, size // chunk, finish, 0)
        if size < out_ref.shape[1]:
            out_ref[0, size:, :] = jnp.zeros((out_ref.shape[1] - size, model), BF)

    variants(lens_ref[step - inner + group - 1], sizes, run)


def attn_dx(hid, order, lens, rows, group, sizes, dkv, dkv2, w_kv, w_kv2, g_in, d_xlast, d_hmid):
    n_seq, seq_len, model = hid.shape
    width = w_kv.shape[1]
    once = dict(pipeline_mode=pl.Buffered(buffer_count=1))
    by_group = lambda *shape: pl.BlockSpec((group,) + shape, lambda i, o, l: (i // group,) + (0,) * len(shape))
    whole = lambda arr: pl.BlockSpec(arr.shape, lambda i, o, l: (0,) * arr.ndim, **once)
    one_row = pl.BlockSpec((1, 1, model), lambda i, o, l: (i, 0, 0))
    return pl.pallas_call(
        functools.partial(dx_body, group, sizes),
        grid_spec=pltpu.PrefetchScalarGridSpec(
            num_scalar_prefetch=2, grid=(n_seq,),
            in_specs=[by_group(rows, width), by_group(rows, width), whole(w_kv), whole(w_kv2),
                      pl.BlockSpec((1, rows, model), lambda i, o, l: (o[i], 0, 0)), whole(g_in), one_row, one_row],
            out_specs=[pl.BlockSpec((1, seq_len, model), lambda i, o, l: (o[i], 0, 0)), pl.BlockSpec((8, model), lambda i, o, l: (0, 0))],
            scratch_shapes=[pltpu.VMEM((group, rows, model), F32)]),
        out_shape=[jax.ShapeDtypeStruct(hid.shape, BF), jax.ShapeDtypeStruct((8, model), F32)],
        compiler_params=pltpu.CompilerParams(dimension_semantics=("arbitrary",), vmem_limit_bytes=VMEM),
        cost_estimate=pl.CostEstimate(flops=4 * n_seq * rows * model * width, bytes_accessed=hid.size * 4, transcendentals=0),
        name="attn_dx" + str(rows),
    )(order, lens, dkv, dkv2, w_kv, w_kv2, hid, g_in, d_xlast[:, None, :], d_hmid[:, None, :])


def wide(values):
    return values.astype(F32)


def narrow(values, unit):
    return (values * unit).astype(BF)


def swap_tp(values):
    return lax.ppermute(values, 'tp', SWAP)


def psum_tp(values):
    return values + swap_tp(values)


def swiglu(gate_in, up_in):
    return jax.nn.silu(gate_in) * up_in


def final_head(h_out, g_final):
    z_norm = norm_rows(h_out, g_final)
    return z_norm * lax.rsqrt(jnp.sum(z_norm * z_norm, axis=-1, keepdims=True))


def dot(a, b):
    return jnp.dot(a, b, preferred_element_type=F32)


def dot_nt(a, b):
    return lax.dot_general(a, b, NT, preferred_element_type=F32)


def dot_tn(a, b):
    return lax.dot_general(a, b, TN, preferred_element_type=F32)


Q_SIZES = (32, 64, 96, 128)
D_SIZES = (128, 256, 384, 512)


def solution(mesh):
    dp_size = mesh.shape['dp']

    def device_step(hid_q, hid_d, len_q, len_d, pos_doc, w_q, w_k, w_v, w_o, w_gate, w_up, w_down, g_in, g_q, g_k, g_post, g_final):
        g_in, g_q, g_k, g_post, g_final = (gain.astype(F32) for gain in (g_in, g_q, g_k, g_post, g_final))
        n_q, n_d = hid_q.shape[0], hid_d.shape[0]
        seq_len = hid_q.shape[1]
        n_query = n_q * dp_size

        ids = jnp.arange(n_q)
        before = (len_q[None, :] < len_q[:, None]) | ((len_q[None, :] == len_q[:, None]) & (ids[None, :] < ids[:, None]))
        rank = jnp.sum(before, axis=1)
        is_rank = rank[None, :] == ids[:, None]
        order_q = jnp.sum(jnp.where(is_rank, ids[None, :], 0), axis=1).astype(jnp.int32)
        lens_q = jnp.sum(jnp.where(is_rank, len_q[None, :], 0), axis=1).astype(jnp.int32)
        pos_sorted = jnp.sum(jnp.where(is_rank, pos_doc[None, :], 0), axis=1).astype(jnp.int32)
        order_d = jnp.arange(n_d, dtype=jnp.int32)
        lens = jnp.concatenate([lens_q, len_d])
        unit = jnp.minimum(len_d[0], 1).astype(F32)

        w_kv = jnp.concatenate([w_k, w_v], axis=1)
        slab_rows = w_kv.shape[0] // dp_size
        slab = lax.dynamic_slice_in_dim(w_kv, lax.axis_index('dp') * slab_rows, slab_rows, axis=0)
        w_kv2 = narrow(lax.all_gather(swap_tp(wide(slab)), 'dp', axis=0, tiled=True), unit)

        h_last = jnp.concatenate([hid_q[order_q, lens_q - 1], hid_d[order_d, len_d - 1]], axis=0).astype(F32)
        x_last = norm_rows(h_last, g_in).astype(BF)
        q_raw = dot(x_last, w_q).astype(BF)
        q_cos, q_sin = rope_tables(lens - 1)
        q_rot, q_pull = jax.vjp(lambda raw, gain: rotate_query(raw, gain, q_cos, q_sin), q_raw, g_q)
        q_rot2 = narrow(swap_tp(wide(q_rot)), unit)
        qbd, qbd2 = block_diag(q_rot), block_diag(q_rot2)

        cos_t, sin_t = rope_tables(jnp.arange(seq_len))
        cos_q, sin_q = cos_t[:Q_MAX], sin_t[:Q_MAX]
        gin_row, gk_row = g_in[None, :], g_k[None, :]
        x_q, kv_q, p_q, o_q = attn_fwd(hid_q, order_q, lens_q, Q_MAX, 4, Q_SIZES, w_kv, qbd[:n_q], gk_row, cos_q, sin_q, gin_row)
        x_d, kv_d, p_d, o_d = attn_fwd(hid_d, order_d, len_d, seq_len, 1, D_SIZES, w_kv, qbd[n_q:], gk_row, cos_t, sin_t, gin_row)
        attn_out = jnp.concatenate([o_q, o_d], axis=0)[:, :q_rot.shape[1]].astype(BF).reshape(n_q + n_d, -1)

        h_mid = h_last + psum_tp(dot(attn_out, w_o))
        y_norm = norm_rows(h_mid, g_post).astype(BF)
        gate_val = dot(y_norm, w_gate).astype(BF)
        up_val = dot(y_norm, w_up).astype(BF)
        hidden_act, act_pull = jax.vjp(swiglu, gate_val.astype(F32), up_val.astype(F32))
        h_out = h_mid + psum_tp(dot(hidden_act.astype(BF), w_down))
        emb, head_pull = jax.vjp(final_head, h_out, g_final)
        emb_q, emb_d = emb[:n_q], emb[n_q:]

        all_docs = lax.all_gather(emb_d, 'dp', axis=0, tiled=True)
        logits = jnp.einsum('qd,kd->qk', emb_q, all_docs, precision=lax.Precision.HIGHEST) / TEMPERATURE
        log_norm = jax.nn.logsumexp(logits, axis=1)
        is_pos = jnp.arange(all_docs.shape[0])[None, :] == pos_sorted[:, None]
        loss_sorted = log_norm - jnp.sum(jnp.where(is_pos, logits, 0.0), axis=1)
        loss_rows = jnp.sum(jnp.where(is_rank, loss_sorted[:, None], 0.0), axis=0)
        d_logits = (jnp.exp(logits - log_norm[:, None]) - is_pos.astype(F32)) / (n_query * TEMPERATURE)
        d_emb_q = jnp.einsum('qk,kd->qd', d_logits, all_docs, precision=lax.Precision.HIGHEST)
        d_docs = jnp.einsum('qk,qd->kd', d_logits, emb_q, precision=lax.Precision.HIGHEST)
        d_emb_d = lax.psum_scatter(d_docs, 'dp', scatter_dimension=0, tiled=True)

        d_hout, d_gfinal = head_pull(jnp.concatenate([d_emb_q, d_emb_d], axis=0))
        d_hout_b = d_hout.astype(BF)
        d_act = dot_nt(d_hout_b, w_down).astype(BF)
        d_gate, d_up = act_pull(d_act.astype(F32))
        d_y = psum_tp(dot_nt(d_gate.astype(BF), w_gate) + dot_nt(d_up.astype(BF), w_up))
        d_ymid, d_gpost = norm_back(h_mid, g_post, d_y)
        d_hmid = d_hout + d_ymid
        d_hmid_b = d_hmid.astype(BF)
        d_attn = dot_nt(d_hmid_b, w_o).astype(BF).reshape(q_rot.shape)
        d_attn2 = narrow(swap_tp(wide(d_attn)), unit)
        dobd, dobd2 = block_diag(d_attn), block_diag(d_attn2)

        dkv_q, dq_q, dgk_q = attn_bwd(lens_q, 4, Q_SIZES, kv_q, p_q, qbd[:n_q], dobd[:n_q], gk_row, cos_q, sin_q)
        dkv_d, dq_d, dgk_d = attn_bwd(len_d, 1, D_SIZES, kv_d, p_d, qbd[n_q:], dobd[n_q:], gk_row, cos_t, sin_t)
        flat = lambda arr: arr.reshape(-1, arr.shape[-1])
        d_wkv = lax.psum(dot_tn(flat(x_q), flat(dkv_q)) + dot_tn(flat(x_d), flat(dkv_d)), 'dp')
        d_qrot = jnp.concatenate([dq_q, dq_d], axis=0)[:, :q_rot.shape[1]].astype(BF)
        d_qraw, d_gq = q_pull(d_qrot)
        d_xlast = psum_tp(dot_nt(d_qraw, w_q))

        kv2_q, p2_q, _ = attn_fwd(x_q, order_q, lens_q, Q_MAX, 4, Q_SIZES, w_kv2, qbd2[:n_q], gk_row, cos_q, sin_q)
        kv2_d, p2_d, _ = attn_fwd(x_d, order_d, len_d, seq_len, 1, D_SIZES, w_kv2, qbd2[n_q:], gk_row, cos_t, sin_t)
        dkv2_q, _, _ = attn_bwd(lens_q, 4, Q_SIZES, kv2_q, p2_q, qbd2[:n_q], dobd2[:n_q], gk_row, cos_q, sin_q)
        dkv2_d, _, _ = attn_bwd(len_d, 1, D_SIZES, kv2_d, p2_d, qbd2[n_q:], dobd2[n_q:], gk_row, cos_t, sin_t)
        d_hid_q, dgin_q = attn_dx(hid_q, order_q, lens_q, Q_MAX, 4, Q_SIZES, dkv_q, dkv2_q, w_kv, w_kv2, gin_row, d_xlast[:n_q], d_hmid[:n_q])
        d_hid_d, dgin_d = attn_dx(hid_d, order_d, len_d, seq_len, 1, D_SIZES, dkv_d, dkv2_d, w_kv, w_kv2, gin_row, d_xlast[n_q:], d_hmid[n_q:])

        gather = lambda arr: narrow(lax.all_gather(wide(arr), 'dp', axis=0, tiled=True), unit)
        width = h_last.shape[1]
        x_last_all = gather(x_last)
        y_attn = gather(jnp.concatenate([y_norm, attn_out], axis=1))
        y_all, attn_all = y_attn[:, :width], y_attn[:, width:]
        d_both = gather(jnp.concatenate([d_hout_b, d_hmid_b], axis=1))
        d_hout_all, d_hmid_all = d_both[:, :width], d_both[:, width:]
        d_qraw_all = gather(d_qraw)
        act_all, act_all_pull = jax.vjp(swiglu, dot(y_all, w_gate).astype(BF).astype(F32), dot(y_all, w_up).astype(BF).astype(F32))
        d_gate_all, d_up_all = act_all_pull(dot_nt(d_hout_all, w_down).astype(BF).astype(F32))
        d_wdown = dot_tn(act_all.astype(BF), d_hout_all)
        d_wgate = dot_tn(y_all, d_gate_all.astype(BF))
        d_wup = dot_tn(y_all, d_up_all.astype(BF))
        d_wo = dot_tn(attn_all, d_hmid_all)
        d_wq = dot_tn(x_last_all, d_qraw_all)

        d_gk = jnp.sum(dgk_q + dgk_d, axis=0)
        d_gin = jnp.sum(dgin_q + dgin_d, axis=0)
        gains = lax.psum(jnp.concatenate([d_gin * 0.5, d_gpost * 0.5, d_gfinal * 0.5, d_gq, d_gk]), ('tp', 'dp'))
        d_gin, d_gpost, d_gfinal = gains[:width], gains[width:2 * width], gains[2 * width:3 * width]
        d_gq, d_gk = gains[3 * width:3 * width + HEAD], gains[3 * width + HEAD:]
        kv_half = w_k.shape[1]
        return (loss_rows, d_hid_q, d_hid_d, d_wq, d_wkv[:, :kv_half], d_wkv[:, kv_half:], d_wo, d_wgate, d_wup, d_wdown,
                d_gin, d_gq, d_gk, d_gpost, d_gfinal)

    col_split = P(None, 'tp')
    row_split = P('tp', None)
    in_specs = (P('dp'), P('dp'), P('dp'), P('dp'), P('dp'), col_split, col_split, col_split, row_split, col_split, col_split, row_split, P(), P(), P(), P(), P())
    out_specs = (P('dp'), P('dp'), P('dp'), col_split, col_split, col_split, row_split, col_split, col_split, row_split, P(), P(), P(), P(), P())
    return jax.shard_map(device_step, mesh=mesh, in_specs=in_specs, out_specs=out_specs, check_vma=False)
```

time: 5030 us -> 839 us (0.17)
  waiting for transfers between devices: 3640 us -> 222 us
  matrix products: 667 us -> 161 us
  other arithmetic: 462 us -> 37.8 us
  Pallas kernels: 0 us -> 292 us
  local copies, waits for them, and re-layouts: 142 us -> 35.1 us
    psum x6 -> x1, waiting for transfers between devices: 3620 us -> 91.7 us  [device_step(): lax.psum(dot_tn(flat(x_q), flat(dkv_q)) + dot_tn(flat(x_d), flat(dkv_d)),...]
    dot_general x52 -> x20, matrix products: 643 us -> 159 us  [the longest x7 81.1 us: dot_tn(): return lax.dot_general(a, b, TN, preferred_element_type=F32)]
    pallas_call x0 -> x10, Pallas kernels: none -> 292 us  [the longest x2 131 us: attn_dx(): pl.pallas_call(functools.partial(dx_body, group, sizes), grid_spec=pltpu....]
    convert_element_type x15 -> x20, other arithmetic: 181 us -> 19.5 us  [the longest x7 15.4 us: narrow(): return (values * unit).astype(BF)]
    unnamed x367 -> x82, local copies, waits for them, and re-layouts: 81.1 us -> 5.9 us
    reduce_sum x4 -> x1, other arithmetic: 69.6 us -> 0.77 us  [norm_back(): jnp.sum((d_out * values * scale).reshape(-1, values.shape[-1]), axis=0)]
  transfers between devices with their start and end apart: 7 -> 14, of which waited for: 4 -> 10; matrix products, arithmetic and copies ran while one was open for 18% -> 18% of each run, Pallas kernels for 0% -> 0%
where the time goes in v1:
time: 839 us; the launch traced here: 830 us
  Pallas kernels  292 us (35%)
  waiting for transfers between devices  222 us (26%)
  matrix products  161 us (19%)
  blocking collectives  53.2 us (6%)
  other arithmetic  37.8 us (5%)
  local copies, waits for them, and re-layouts  35.1 us (4%)
  between operations  16.2 us (2%)
  starting transfers between devices  12.2 us (1%)
    pallas_call x2, Pallas kernels, attn_dx(): pl.pallas_call(functools.partial(dx_body, group, sizes), grid_spec=pltpu....  131 us
    pallas_call x4, Pallas kernels, attn_fwd(): pl.pallas_call(functools.partial(fwd_body, do_norm, group, sizes), grid_s...  106 us
    psum x1, waiting for transfers between devices, device_step(): lax.psum(dot_tn(flat(x_q), flat(dkv_q)) + dot_tn(flat(x_d), flat(dkv_d)),...  91.7 us
    dot_general x7, matrix products, dot_tn(): return lax.dot_general(a, b, TN, preferred_element_type=F32)  81.1 us
    pallas_call x4, Pallas kernels, attn_bwd(): pl.pallas_call(functools.partial(bwd_body, group, sizes), grid_spec=pltpu...  54.8 us
    unnamed x8, waiting for transfers between devices  46.2 us
    all_gather x4, waiting for transfers between devices, device_step(): lax.all_gather(wide(arr), 'dp', axis=0, tiled=True)  42.2 us
    ppermute x7, waiting for transfers between devices, swap_tp(): return lax.ppermute(values, 'tp', SWAP)  42 us
  transfers between devices with their start and end apart: 14, of which 10 were waited for; matrix products, arithmetic and copies ran while one was open for 18% of the time, Pallas kernels for 0%

profile of v1, /device:TPU:0, one launch (start us, length us, event | category | flops | bytes accessed | tf_op | source)
XLA Modules:
  0.0 829.6 jit_solution(6341068511299467294)
XLA Ops:
  11.2 1.5 gather_fusion.1
  12.7 1.7 gather_fusion
  14.6 3.1 fusion.18
  20.8 1.0 fusion.52
  21.9 1.0 pad_maximum_fusion.1
  23.6 3.1 constant_dynamic-update-slice_fusion.1
  27.2 1.6 constant_dynamic-update-slice_fusion.refs_5_.refs_2_.w_ref
  29.3 14.1 %attn_fwd_norm512.1 = (bf16[2,512,2048]{2,1,0:T(8,128)(2,1)}, bf16[2,512,1024]{2,1,0:T(8,128)(2,1)}, f32[2,16,512]{2,1,0:T(8,128)}, f32[2,16,128]{2,1,0:T(8,128)}) custom-call(s32[2]{0:T(128)} %iota.137.order_ref, s32[2]{0:T(128)} %lens_ref.9, bf16[2,512,2048]{2,1,0:T(8,128)(2,1)} %h_ref.3, f32[1,2048]{1,0:T(1,128)} %bitcast.122, ...), custom_call_target="tpu_custom_call" | custom-call | flops 4294967296 | bytes 8388608 | tf_op jit(solution)/shard_map/attn_fwd_norm512/pallas_call | solution.py:154
  44.1 44.1 %attn_fwd_norm128.1 = (bf16[32,128,2048]{2,1,0:T(8,128)(2,1)}, bf16[32,128,1024]{2,1,0:T(8,128)(2,1)}, f32[32,16,128]{2,1,0:T(8,128)}, f32[32,16,128]{2,1,0:T(8,128)}) custom-call(s32[32]{0:T(128)} %copy-done.17, s32[32]{0:T(128)} %copy-done.16, bf16[32,512,2048]{2,1,0:T(8,128)(2,1)} %h_ref.2, bf16[32,512,2048]{2,1,0:T(8,128)(2,1)} %h_ref.2, ...), custom_call_target="tpu_custom_call" | custom-call | flops 17179869184 | bytes 33554432 | tf_op jit(solution)/shard_map/attn_fwd_norm128/pallas_call | solution.py:154
  89.3 3.0 fusion.99
  92.3 3.3 collective-permute-start
  95.6 5.8 collective-permute-done
  102.5 7.0 fusion.1
  109.5 7.0 fusion.2
  116.6 2.2 fusion.39
  118.9 1.8 collective-permute-start.1
  121.9 4.1 collective-permute-done.1
  126.5 14.6 %all-gather = f32[8,2,2048]{2,1,0:T(2,128)S(1)} all-gather(f32[1,2,2048]{2,1,0:T(2,128)S(1)} %slice_bitcast_fusion.2), channel_id=1, replica_groups=mesh['tp'=2,'dp'=8] {'dp'}, dimensions={0}, use_global_device_ids=true | all-gather | bytes 147456 | tf_op jit(solution)/shard_map/all_gather | solution.py:391
  143.2 45.4 %all-reduce.12.cloned.1.call-done = f32[16,2048]{1,0:T(8,128)} async-done(((f32[16,2048]{1,0:T(8,128)}), f32[16,2048]{1,0:T(8,128)}) %all-reduce.12.cloned.1.call-update) | async-done | bytes 131088
  190.7 8.5 %fusion = f32[34,3072]{1,0:T(8,128)S(1)} fusion(bf16[34,2048]{1,0:T(8,128)(2,1)S(1)} %get-tuple-element.79, bf16[3072,2048]{1,0:T(8,128)(2,1)} %param.28), kind=kOutput, calls=%fused_computation.17 | convolution fusion | flops 428027904 | bytes 13139968 | tf_op jit(solution)/shard_map/dot_general | solution.py:331
  199.3 8.6 %fusion.40 = f32[34,2048]{1,0:T(8,128)S(1)} fusion(bf16[2048,3072]{1,0:T(8,128)(2,1)} %param.26, f32[34,3072]{1,0:T(8,128)S(1)} %fusion.2, f32[34,3072]{1,0:T(8,128)S(1)} %fusion, f32[34,3072]{1,0:T(8,128)S(1)} %fusion.1), kind=kOutput, calls=%fused_computation.108 | convolution fusion | flops 428967936 | bytes 14114816 | tf_op jit(solution)/shard_map/dot_general | solution.py:331
  208.0 3.9 convolution_add_fusion
  211.9 1.5 collective-permute-start.2
  214.0 8.1 collective-permute-done.2
  223.0 3.5 convolution_convert_fusion.6
  226.6 1.5 collective-permute-start.5
  228.1 3.6 collective-permute-done.5
  233.2 6.3 attn_bwd512.2
  240.2 21.1 %attn_bwd128.2 = (bf16[32,128,1024]{2,1,0:T(8,128)(2,1)}, f32[32,16,128]{2,1,0:T(8,128)}, f32[8,128]{1,0:T(8,128)}) custom-call(s32[32]{0:T(128)} %copy-done.16, bf16[32,128,1024]{2,1,0:T(8,128)(2,1)} %get-tuple-element.41.kv_ref, f32[32,16,128]{2,1,0:T(8,128)} %get-tuple-element.42.p_ref, bf16[32,16,512]{2,1,0:T(8,128)(2,1)} %pad_slice_fusion.7.refs_6_.qbd_ref, ...), custom_call_target="tpu_custom_call" | custom-call | flops 10485760000 | bytes 16777216 | tf_op jit(solution)/shard_map/attn_bwd128/pallas_call | solution.py:211
  265.0 22.9 %fusion.102 = f32[2048,1024,1]{1,0,2:T(8,128)S(1)} fusion(bf16[32,128,2048]{2,1,0:T(8,128)(2,1)} %get-tuple-element.44.refs_0_, bf16[32,128,1024]{2,1,0:T(8,128)(2,1)} %get-tuple-element.43.dkv_ref), kind=kOutput, calls=%fused_computation.236 | convolution fusion | flops 17179869184 | bytes 33554432 | tf_op jit(solution)/shard_map/dot_general | solution.py:335
  287.9 7.2 bitcast_add_fusion
  297.0 1.1 dynamic-slice_convert_fusion
  298.2 1.5 collective-permute-start.3
  299.7 18.4 %collective-permute-done.3 = f32[256,1024]{1,0:T(8,128)S(1)} collective-permute-done((f32[256,1024]{1,0:T(8,128)S(1)}, f32[256,1024]{1,0:T(8,128)S(1)}, u32[]{:S(2)}, u32[]{:S(2)}) %collective-permute-start.3) | collective-permute-done | bytes 1048608 | tf_op jit(solution)/shard_map/ppermute | solution.py:310
  321.3 3.5 fusion.100
  324.8 1.5 collective-permute-start.6
  329.8 2.1 collective-permute-done.6
  332.0 1.0 copy.58.dxl_ref
  333.6 1.4 multiply_convert_fusion.4
  335.2 2.0 multiply_convert_fusion.3
  337.8 5.8 fusion.101
  343.6 91.7 %all-reduce.10.cloned.1.call-done = f32[2048,1024]{1,0:T(8,128)} async-done(((f32[2048,1024]{1,0:T(8,128)}), f32[2048,1024]{1,0:T(8,128)}) %all-reduce.10.cloned.1.call-update) | async-done | bytes 8388624 | tf_op jit(solution)/shard_map/psum | solution.py:417
  435.3 7.8 fusion.93
  443.2 26.0 %all-gather.17.cloned.1.call-done = f32[8,34,3072]{2,1,0:T(8,128)} async-done(((f32[1,34,3072]{2,1,0:T(8,128)}), f32[8,34,3072]{2,1,0:T(8,128)}) %all-gather.17.cloned.1.call-update) | async-done | bytes 3342352 | tf_op jit(solution)/shard_map/all_gather | solution.py:429
  469.2 2.4 multiply_convert_fusion.2
  471.6 1.4 reshape.370
  473.1 9.8 %convolution_convert_fusion = bf16[272,3072]{1,0:T(8,128)(2,1)} fusion(bf16[2048,3072]{1,0:T(8,128)(2,1)} %param.26, bf16[272,3072]{1,0:T(8,128)(2,1)} %reshape.370), kind=kOutput, calls=%fused_computation.12 | convolution fusion | flops 3423387648 | bytes 15368192 | tf_op jit(solution)/shard_map/dot_general | solution.py:327
  482.9 9.3 %convolution_convert_fusion.1 = bf16[272,3072]{1,0:T(8,128)(2,1)} fusion(bf16[2048,3072]{1,0:T(8,128)(2,1)} %param.27, bf16[272,3072]{1,0:T(8,128)(2,1)S(1)} %copy-done), kind=kOutput, calls=%fused_computation.13 | convolution fusion | flops 3423387648 | bytes 15368192 | tf_op jit(solution)/shard_map/dot_general | solution.py:327
  492.2 16.2 %all-gather.19.cloned.1.call-done = f32[8,34,4096]{2,1,0:T(8,128)} async-done(((f32[1,34,4096]{2,1,0:T(8,128)}), f32[8,34,4096]{2,1,0:T(8,128)}) %all-gather.19.cloned.1.call-update) | async-done | bytes 4456464 | tf_op jit(solution)/shard_map/all_gather | solution.py:429
  508.4 2.9 multiply_convert_fusion.1
  511.4 2.1 reshape.371
  513.5 7.4 fusion.19
  520.8 8.4 %convolution_convert_fusion.2 = bf16[272,3072]{1,0:T(8,128)(2,1)S(1)} fusion(bf16[3072,2048]{1,0:T(8,128)(2,1)} %param.28, bf16[272,4096]{1,0:T(8,128)(2,1)S(1)} %copy-done.2), kind=kOutput, calls=%fused_computation.14 | convolution fusion | flops 3423387648 | bytes 15368192 | tf_op jit(solution)/shard_map/dot_general | solution.py:331
  529.2 12.5 %fusion.15 = f32[2048,3072]{1,0:T(8,128)} fusion(bf16[272,3072]{1,0:T(8,128)(2,1)S(1)} %convolution_convert_fusion.2, bf16[272,3072]{1,0:T(8,128)(2,1)S(1)} %copy-done.4, bf16[272,3072]{1,0:T(8,128)(2,1)S(1)} %copy-done.1), kind=kOutput, calls=%fused_computation.34 | convolution fusion | flops 3429236736 | bytes 29622272 | tf_op jit(solution)/shard_map/dot_general | solution.py:335
  541.8 12.7 %fusion.13 = f32[3072,2048]{1,0:T(8,128)} fusion(bf16[272,3072]{1,0:T(8,128)(2,1)S(1)} %copy-done.26, bf16[272,3072]{1,0:T(8,128)(2,1)S(1)} %copy-done.4, bf16[272,4096]{1,0:T(8,128)(2,1)S(1)} %copy-done.2), kind=kOutput, calls=%fused_computation.33 | convolution fusion | flops 3429236736 | bytes 29622272 | tf_op jit(solution)/shard_map/dot_general | solution.py:335
  554.5 12.6 %fusion.11 = f32[2048,3072]{1,0:T(8,128)} fusion(bf16[272,3072]{1,0:T(8,128)(2,1)S(1)} %copy-done.4, bf16[272,3072]{1,0:T(8,128)(2,1)S(1)} %copy-done.26, bf16[272,3072]{1,0:T(8,128)(2,1)S(1)} %convolution_convert_fusion.2, bf16[272,3072]{1,0:T(8,128)(2,1)S(1)} %copy-done.1), kind=kOutput, calls=%fused_computation.32 | convolution fusion | flops 3434250240 | bytes 31293440 | tf_op jit(solution)/shard_map/dot_general | solution.py:335
  567.1 6.6 multiply_convert_fusion.refs_1_.w2_ref
  573.8 36.9 %attn_fwd128.1 = (bf16[32,128,1024]{2,1,0:T(8,128)(2,1)}, f32[32,16,128]{2,1,0:T(8,128)}, f32[32,16,128]{2,1,0:T(8,128)}) custom-call(s32[32]{0:T(128)} %copy-done.17, s32[32]{0:T(128)} %copy-done.16, bf16[32,128,2048]{2,1,0:T(8,128)(2,1)} %get-tuple-element.44.refs_0_, bf16[2048,1024]{1,0:T(8,128)(2,1)} %multiply_convert_fusion.refs_1_.w2_ref, ...), custom_call_target="tpu_custom_call" | custom-call | flops 17179869184 | bytes 33554432 | tf_op jit(solution)/shard_map/attn_fwd128/pallas_call | solution.py:154
  611.2 11.3 %attn_fwd512.1 = (bf16[2,512,1024]{2,1,0:T(8,128)(2,1)}, f32[2,16,512]{2,1,0:T(8,128)}, f32[2,16,128]{2,1,0:T(8,128)}) custom-call(s32[2]{0:T(128)} %iota.139.order_ref, s32[2]{0:T(128)} %lens_ref.9, bf16[2,512,2048]{2,1,0:T(8,128)(2,1)} %get-tuple-element.54.refs_0_, bf16[2048,1024]{1,0:T(8,128)(2,1)} %multiply_convert_fusion.refs_1_.w2_ref, ...), custom_call_target="tpu_custom_call" | custom-call | flops 4294967296 | bytes 8388608 | tf_op jit(solution)/shard_map/attn_fwd512/pallas_call | solution.py:154
  622.4 21.3 %attn_bwd128.3 = (bf16[32,128,1024]{2,1,0:T(8,128)(2,1)}, f32[32,16,128]{2,1,0:T(8,128)}, f32[8,128]{1,0:T(8,128)}) custom-call(s32[32]{0:T(128)} %copy-done.16, bf16[32,128,1024]{2,1,0:T(8,128)(2,1)} %get-tuple-element.45.kv_ref, f32[32,16,128]{2,1,0:T(8,128)} %get-tuple-element.46.p_ref, bf16[32,16,512]{2,1,0:T(8,128)(2,1)} %pad_slice_fusion.3.refs_2_.qbd_ref, ...), custom_call_target="tpu_custom_call" | custom-call | flops 10485760000 | bytes 16777216 | tf_op jit(solution)/shard_map/attn_bwd128/pallas_call | solution.py:211
  643.7 105.8 %attn_dx128.1 = (bf16[32,512,2048]{2,1,0:T(8,128)(2,1)}, f32[8,2048]{1,0:T(8,128)}) custom-call(s32[32]{0:T(128)} %copy-done.17, s32[32]{0:T(128)} %copy-done.16, bf16[32,128,1024]{2,1,0:T(8,128)(2,1)} %get-tuple-element.43.dkv_ref, bf16[32,128,1024]{2,1,0:T(8,128)(2,1)} %get-tuple-element.47.dkv2_ref, ...), custom_call_target="tpu_custom_call" | custom-call | flops 34359738368 | bytes 134217728 | tf_op jit(solution)/shard_map/attn_dx128/pallas_call | solution.py:286
  749.4 6.2 attn_bwd512.3
  756.2 25.4 %attn_dx512.1 = (bf16[2,512,2048]{2,1,0:T(8,128)(2,1)}, f32[8,2048]{1,0:T(8,128)}) custom-call(s32[2]{0:T(128)} %iota.138.order_ref, s32[2]{0:T(128)} %lens_ref.9, bf16[2,512,1024]{2,1,0:T(8,128)(2,1)} %get-tuple-element.53.dkv_ref, bf16[2,512,1024]{2,1,0:T(8,128)(2,1)} %get-tuple-element.57.dkv2_ref, ...), custom_call_target="tpu_custom_call" | custom-call | flops 8589934592 | bytes 8388608 | tf_op jit(solution)/shard_map/attn_dx512/pallas_call | solution.py:286
  782.5 38.6 %psum.15 = f32[6400]{0:T(1024)S(1)} all-reduce(f32[6400]{0:T(1024)S(1)} %constant_dynamic-update-slice_fusion.3), channel_id=1, replica_groups=mesh['tp'=2,'dp'=8] {'tp','dp'}, use_global_device_ids=true, to_apply=%region_24.25 | all-reduce | flops 6400 | bytes 51200 | tf_op jit(solution)/shard_map/psum | solution.py:447
  (203 shorter events, 37.6 us)
Async XLA Ops:
  7.2 10.5 %copy-start.22 = (bf16[128]{0:T(256)(128)(2,1)S(1)}, bf16[128]{0:T(256)(128)(2,1)}, u32[]{:S(2)}) copy-start(bf16[128]{0:T(256)(128)(2,1)} %param.30) | copy-start | bytes 772
  7.2 181.4 %all-reduce.12.cloned.1.call-start = ((), (), s32[]{:S(2)}) async-start(), calls=%async_computation.6 | async-start | bytes 262144
  8.0 10.1 %copy-start.7 = (f32[2048]{0:T(1024)}, f32[2048]{0:T(1024)S(1)}, u32[]{:S(2)}) copy-start(f32[2048]{0:T(1024)S(1)} %convert_element_type.194) | copy-start | bytes 24580
  8.9 1.5 copy-start.20
  10.4 7.7 copy-start.16
  10.4 7.7 copy-start.17
  21.8 4.9 copy-start.23
  21.8 5.4 copy-start.3
  88.2 7.4 copy-start.12
  88.3 13.2 %copy-start.8 = (f32[2048]{0:T(1024)S(1)}, f32[2048]{0:T(1024)}, u32[]{:S(2)}) copy-start(f32[2048]{0:T(1024)} %copy-done.7) | copy-start | bytes 24580
  92.3 9.1 %collective-permute-start = (f32[34,2048]{1,0:T(8,128)S(1)}, f32[34,2048]{1,0:T(8,128)S(1)}, u32[]{:S(2)}, u32[]{:S(2)}) collective-permute-start(f32[34,2048]{1,0:T(8,128)S(1)} %fusion.99), channel_id=1, source_target_pairs={{0,8},{8,0},{1,9},{9,1},{2,10},{10,2},{3,11},{11,3},{4,12},{12,4},... | collective-permute-start | bytes 835592 | tf_op jit(solution)/shard_map/ppermute | solution.py:310
  102.5 14.0 %slice-start = ((s8[12582912]{0:T(1024)(128)(4,1)}), s8[4194304]{0:T(1024)(128)(4,1)S(1)}, s32[]{:S(2)}) async-start(s8[12582912]{0:T(1024)(128)(4,1)} %bitcast.104), calls=%async_computation.7 | async-start | bytes 8388608
  102.5 14.0 %slice-start.1 = ((s8[12582912]{0:T(1024)(128)(4,1)}), s8[4194304]{0:T(1024)(128)(4,1)S(1)}, s32[]{:S(2)}) async-start(s8[12582912]{0:T(1024)(128)(4,1)} %bitcast.104), calls=%async_computation.8 | async-start | bytes 8388608
  109.5 7.0 slice-start.2
  116.6 4.0 copy-start.13
  116.6 4.0 copy-start.25
  118.9 7.1 collective-permute-start.1
  142.5 191.1 %all-gather.15.cloned.1.call-start = ((), (), s32[]{:S(2)}) async-start(), calls=%async_computation.3 | async-start | bytes 1474560 | tf_op jit(solution)/shard_map/all_gather | solution.py:429
  190.7 17.2 %slice-start.3 = ((s8[12582912]{0:T(1024)(128)(4,1)}), s8[4194304]{0:T(1024)(128)(4,1)S(1)}, s32[]{:S(2)}) async-start(s8[12582912]{0:T(1024)(128)(4,1)} %bitcast.106), calls=%async_computation.10 | async-start | bytes 8388608
  190.7 17.2 %slice-start.4 = ((s8[12582912]{0:T(1024)(128)(4,1)}), s8[4194304]{0:T(1024)(128)(4,1)S(1)}, s32[]{:S(2)}) async-start(s8[12582912]{0:T(1024)(128)(4,1)} %bitcast.106), calls=%async_computation.11 | async-start | bytes 8388608
  199.3 8.6 %slice-start.5 = ((s8[12582912]{0:T(1024)(128)(4,1)}), s8[4194304]{0:T(1024)(128)(4,1)S(1)}, s32[]{:S(2)}) async-start(s8[12582912]{0:T(1024)(128)(4,1)} %bitcast.106), calls=%async_computation.12 | async-start | bytes 8388608
  207.9 5.4 copy-start.6
  208.0 6.0 copy-start.24
  211.9 10.2 %collective-permute-start.2 = (f32[34,2048]{1,0:T(8,128)S(1)}, f32[34,2048]{1,0:T(8,128)S(1)}, u32[]{:S(2)}, u32[]{:S(2)}) collective-permute-start(f32[34,2048]{1,0:T(8,128)S(1)} %convolution_add_fusion), channel_id=1, source_target_pairs={{0,8},{8,0},{1,9},{9,1},{2,10},{10,2},{3,11},{11,3},{4,12},{12,4},... | collective-permute-start | bytes 835592 | tf_op jit(solution)/shard_map/ppermute | solution.py:310
  213.4 14.7 %collective-permute-start.4 = (f32[34,8,128]{2,1,0:T(8,128)S(1)}, f32[34,8,128]{2,1,0:T(8,128)S(1)}, u32[]{:S(2)}, u32[]{:S(2)}) collective-permute-start(f32[34,8,128]{2,1,0:T(8,128)S(1)} %copy-done.6), channel_id=1, source_target_pairs={{0,8},{8,0},{1,9},{9,1},{2,10},{10,2},{3,11},{11,3},{4,12},{12,4},... | collective-permute-start | bytes 417800 | tf_op jit(solution)/shard_map/ppermute | solution.py:310
  226.6 5.1 collective-permute-start.5
  264.2 71.1 %all-gather.13.cloned.1.call-start = ((), (), s32[]{:S(2)}) async-start(), calls=%async_computation.2 | async-start | bytes 2949120 | tf_op jit(solution)/shard_map/all_gather | solution.py:429
  264.9 170.4 %all-reduce.10.cloned.1.call-start = ((), (), s32[]{:S(2)}) async-start(), calls=%async_computation.1 | async-start | bytes 16777216 | tf_op jit(solution)/shard_map/psum | solution.py:417
  264.9 23.0 %copy-start.27 = (bf16[2,512,2048]{2,1,0:T(8,128)(2,1)S(1)}, bf16[2,512,2048]{2,1,0:T(8,128)(2,1)}, u32[]{:S(2)}) copy-start(bf16[2,512,2048]{2,1,0:T(8,128)(2,1)} %get-tuple-element.54.refs_0_) | copy-start | bytes 12582916
  265.0 23.0 %copy-start.28 = (bf16[2,512,1024]{2,1,0:T(8,128)(2,1)S(1)}, bf16[2,512,1024]{2,1,0:T(8,128)(2,1)}, u32[]{:S(2)}) copy-start(bf16[2,512,1024]{2,1,0:T(8,128)(2,1)} %get-tuple-element.53.dkv_ref) | copy-start | bytes 6291460
  295.1 23.9 %copy-start.21 = (s32[32]{0:T(128)S(1)}, s32[32]{0:T(128)}, u32[]{:S(2)}) copy-start(s32[32]{0:T(128)} %copy-done.20) | copy-start | bytes 388
  295.1 174.0 %all-gather.17.cloned.1.call-start = ((), (), s32[]{:S(2)}) async-start(), calls=%async_computation.4 | async-start | bytes 4423680 | tf_op jit(solution)/shard_map/all_gather | solution.py:429
  296.0 212.4 %all-gather.19.cloned.1.call-start = ((), (), s32[]{:S(2)}) async-start(), calls=%async_computation.5 | async-start | bytes 5898240 | tf_op jit(solution)/shard_map/all_gather | solution.py:429
  297.0 270.1 %all-gather.11.cloned.1.call-start = ((), (), s32[]{:S(2)}) async-start(), calls=%async_computation | async-start | bytes 9437184 | tf_op jit(solution)/shard_map/all_gather | solution.py:365
  298.2 19.9 %collective-permute-start.3 = (f32[256,1024]{1,0:T(8,128)S(1)}, f32[256,1024]{1,0:T(8,128)S(1)}, u32[]{:S(2)}, u32[]{:S(2)}) collective-permute-start(f32[256,1024]{1,0:T(8,128)S(1)} %dynamic-slice_convert_fusion), channel_id=1, source_target_pairs={{0,8},{8,0},{1,9},{9,1},{2,10},{10,2},{3,11},{11,3},{4,12},{12,4},... | collective-permute-start | bytes 3145736 | tf_op jit(solution)/shard_map/ppermute | solution.py:310
  318.0 1.0 copy-start.5
  319.0 8.5 %copy-start.14 = (f32[8,128]{1,0:T(8,128)S(1)}, f32[8,128]{1,0:T(8,128)}, u32[]{:S(2)}) copy-start(f32[8,128]{1,0:T(8,128)} %get-tuple-element.62) | copy-start | bytes 12292
  319.0 8.5 %copy-start.15 = (f32[8,128]{1,0:T(8,128)S(1)}, f32[8,128]{1,0:T(8,128)}, u32[]{:S(2)}) copy-start(f32[8,128]{1,0:T(8,128)} %get-tuple-element.61) | copy-start | bytes 12292
  324.8 7.1 collective-permute-start.6
  473.1 9.8 %copy-start = (bf16[272,3072]{1,0:T(8,128)(2,1)S(1)}, bf16[272,3072]{1,0:T(8,128)(2,1)}, u32[]{:S(2)}) copy-start(bf16[272,3072]{1,0:T(8,128)(2,1)} %reshape.370) | copy-start | bytes 5013508
  513.5 7.4 copy-start.2
  520.8 8.4 %copy-start.1 = (bf16[272,3072]{1,0:T(8,128)(2,1)S(1)}, bf16[272,3072]{1,0:T(8,128)(2,1)}, u32[]{:S(2)}) copy-start(bf16[272,3072]{1,0:T(8,128)(2,1)} %reshape.370) | copy-start | bytes 5013508
  520.8 8.4 %copy-start.4 = (bf16[272,3072]{1,0:T(8,128)(2,1)S(1)}, bf16[272,3072]{1,0:T(8,128)(2,1)}, u32[]{:S(2)}) copy-start(bf16[272,3072]{1,0:T(8,128)(2,1)} %convolution_convert_fusion) | copy-start | bytes 5013508
  529.2 12.6 %copy-start.26 = (bf16[272,3072]{1,0:T(8,128)(2,1)S(1)}, bf16[272,3072]{1,0:T(8,128)(2,1)}, u32[]{:S(2)}) copy-start(bf16[272,3072]{1,0:T(8,128)(2,1)} %convolution_convert_fusion.1) | copy-start | bytes 5013508
  756.1 25.4 %copy-start.9 = (f32[8,2048]{1,0:T(8,128)S(1)}, f32[8,2048]{1,0:T(8,128)}, u32[]{:S(2)}) copy-start(f32[8,2048]{1,0:T(8,128)} %get-tuple-element.59) | copy-start | bytes 196612
  756.1 26.3 %copy-start.11 = (f32[2048]{0:T(1024)S(1)}, f32[2048]{0:T(1024)}, u32[]{:S(2)}) copy-start(f32[2048]{0:T(1024)} %get-tuple-element.63) | copy-start | bytes 24580
  756.1 26.3 %copy-start.10 = (f32[2048]{0:T(1024)S(1)}, f32[2048]{0:T(1024)}, u32[]{:S(2)}) copy-start(f32[2048]{0:T(1024)} %get-tuple-element.65) | copy-start | bytes 24580
  756.1 26.3 %copy-start.18 = (f32[128]{0:T(128)S(1)}, f32[128]{0:T(128)}, u32[]{:S(2)}) copy-start(f32[128]{0:T(128)} %get-tuple-element.67) | copy-start | bytes 1540
  756.1 26.3 %copy-start.19 = (f32[128]{0:T(128)S(1)}, f32[128]{0:T(128)}, u32[]{:S(2)}) copy-start(f32[128]{0:T(128)} %add_reduce_fusion.1) | copy-start | bytes 1540
Sparse Core Ops, SparseCore 0:
  142.6 45.9 all-reduce.11
  264.3 20.4 all-gather.14
  287.2 25.9 all-gather.12
  317.1 118.2 all-reduce.9
  437.6 31.5 all-gather.16
  471.4 36.9 all-gather.18
  510.3 50.1 all-gather.10

commit v2 on v1

v2 whole, which is shorter than its diff:
```python
import functools
import jax
import jax.numpy as jnp
from jax import lax
from jax.experimental import pallas as pl
from jax.experimental.pallas import tpu as pltpu
from jax.sharding import PartitionSpec as P

NORM_EPS = 1e-6
ROPE_THETA = 1000000.0
TEMPERATURE = 0.05
HEAD = 128
Q_MAX = 128
BF = jnp.bfloat16
F32 = jnp.float32
SWAP = [(0, 1), (1, 0)]
VMEM = 60 * 1024 * 1024


def norm_rows(values, gain_vec):
    return values * lax.rsqrt(jnp.mean(values * values, axis=-1, keepdims=True) + NORM_EPS) * gain_vec


def norm_back(values, gain_vec, d_out):
    scale = lax.rsqrt(jnp.mean(values * values, axis=-1, keepdims=True) + NORM_EPS)
    g_dout = d_out * gain_vec
    d_values = scale * g_dout - values * scale ** 3 * jnp.mean(values * g_dout, axis=-1, keepdims=True)
    d_gain = jnp.sum((d_out * values * scale).reshape(-1, values.shape[-1]), axis=0)
    return d_values, d_gain


def rope_tables(positions):
    inv_freq = ROPE_THETA ** (-jnp.arange(0, HEAD, 2, dtype=F32) / HEAD)
    angles = positions.astype(F32)[:, None] * inv_freq
    cos_a, sin_a = jnp.cos(angles), jnp.sin(angles)
    return jnp.concatenate([cos_a, cos_a], axis=-1), jnp.concatenate([-sin_a, sin_a], axis=-1)


def rotate_query(q_raw, g_q, cos_t, sin_t):
    n_seq = q_raw.shape[0]
    normed = norm_rows(q_raw.reshape(n_seq, -1, HEAD).astype(F32), g_q)
    half = HEAD // 2
    swapped = jnp.concatenate([normed[..., half:], normed[..., :half]], axis=-1)
    return (normed * cos_t[:, None, :] + swapped * sin_t[:, None, :]).astype(BF)


def head_mask(n_rows, width):
    row_head = lax.rem(lax.broadcasted_iota(jnp.int32, (n_rows, width), 0), 16) // 2
    lane_head = lax.broadcasted_iota(jnp.int32, (n_rows, width), 1) // HEAD
    return row_head == lane_head


def block_diag(per_head):
    n_seq, n_q, _ = per_head.shape
    n_kv = n_q // 2
    wide = jnp.tile(per_head, (1, 1, n_kv))
    wide = jnp.where(head_mask(n_q, n_kv * HEAD)[None], wide, jnp.zeros_like(wide))
    return jnp.pad(wide, ((0, 0), (0, 16 - n_q), (0, 0)))


def take_diag(wide):
    kept = jnp.where(head_mask(wide.shape[0], wide.shape[1]), wide, 0.0)
    total = kept[:, :HEAD]
    for head in range(1, wide.shape[1] // HEAD):
        total = total + kept[:, head * HEAD:(head + 1) * HEAD]
    return total


def key_stats(k_raw):
    k_f = k_raw.astype(F32)
    scale = lax.rsqrt(jnp.mean(k_f * k_f, axis=-1, keepdims=True) + NORM_EPS)
    return k_f * scale, scale


def turn(values, cos_t, sin_t):
    return values * cos_t + pltpu.roll(values, HEAD // 2, 1) * sin_t


def variants(max_len, sizes, body):
    low = 0
    for size in sizes:
        pl.when(jnp.logical_and(max_len > low, max_len <= size))(functools.partial(body, size))
        low = size


NT = (((1,), (1,)), ((), ()))
TN = (((0,), (0,)), ((), ()))


def stacked(parts):
    return parts[0] if len(parts) == 1 else jnp.concatenate(parts, axis=0)


def row_lengths(lens_ref, first, group, shape):
    row_seq = lax.broadcasted_iota(jnp.int32, shape, 0) // 16
    lengths = jnp.full(shape, lens_ref[first], jnp.int32)
    for g in range(1, group):
        lengths = jnp.where(row_seq == g, lens_ref[first + g], lengths)
    return lengths


def fwd_body(do_norm, group, sizes, order_ref, lens_ref, *refs):
    h_refs, refs = refs[:group if do_norm else 1], refs[group if do_norm else 1:]
    if do_norm:
        gin_ref, wk_ref, wv_ref, qbd_ref, gk_ref, cos_ref, sin_ref, x_ref, kv_ref, p_ref, o_ref, rot_ref = refs
        for g in range(group):
            def norm_chunk(c, carry, g=g):
                here = pl.ds(pl.multiple_of(c * 32, 32), 32)
                hid = h_refs[g][0, here, :].astype(F32)
                scale = lax.rsqrt(jnp.mean(hid * hid, axis=-1, keepdims=True) + NORM_EPS)
                x_ref[g, here, :] = (hid * scale * gin_ref[...]).astype(BF)
                return carry

            lax.fori_loop(0, x_ref.shape[1] // 32, norm_chunk, 0)
    else:
        wk_ref, wv_ref, qbd_ref, gk_ref, cos_ref, sin_ref, kv_ref, p_ref, o_ref, rot_ref = refs
        x_ref = h_refs[0]
    kv_half = wk_ref.shape[1]
    step = pl.program_id(0)

    def run(size):
        for at, w_ref in ((0, wk_ref), (kv_half, wv_ref)):
            x_val = x_ref[:, :size, :].reshape(group * size, x_ref.shape[2])
            out = jnp.dot(x_val, w_ref[...], preferred_element_type=F32)
            kv_ref[:, :size, at:at + kv_half] = out.astype(BF).reshape(group, size, kv_half)
        cos_t, sin_t = cos_ref[:size], sin_ref[:size]
        for g in range(group):
            for head in range(kv_half // HEAD):
                lanes = slice(head * HEAD, (head + 1) * HEAD)
                k_hat, _ = key_stats(kv_ref[g, :size, lanes])
                rot_ref[g, :size, lanes] = turn(k_hat * gk_ref[...], cos_t, sin_t).astype(BF)
        scores = stacked([lax.dot_general(qbd_ref[g], rot_ref[g, :size, :], NT, preferred_element_type=F32) for g in range(group)])
        valid = lax.broadcasted_iota(jnp.int32, scores.shape, 1) < row_lengths(lens_ref, step * group, group, scores.shape)
        scores = jnp.where(valid, scores * HEAD ** -0.5, -1e30)
        expd = jnp.exp(scores - jnp.max(scores, axis=-1, keepdims=True))
        prob = expd / jnp.sum(expd, axis=-1, keepdims=True)
        p_ref[:, :, :size] = prob.reshape(group, 16, size)
        prob = prob.astype(BF)
        mix = stacked([jnp.dot(prob[g * 16:(g + 1) * 16], kv_ref[g, :size, kv_half:], preferred_element_type=F32) for g in range(group)])
        o_ref[...] = take_diag(mix).reshape(group, 16, HEAD)

    variants(lens_ref[step * group + group - 1], sizes, run)


def attn_fwd(hid_or_x, order, lens, rows, group, sizes, w_k, w_v, qbd, g_k, cos_t, sin_t, g_in=None):
    n_seq, width = order.shape[0], 2 * w_k.shape[1]
    model = w_k.shape[0]
    do_norm = g_in is not None
    once = dict(pipeline_mode=pl.Buffered(buffer_count=1))
    by_group = lambda *shape: pl.BlockSpec((group,) + shape, lambda i, o, l: (i,) + (0,) * len(shape))
    whole = lambda arr: pl.BlockSpec(arr.shape, lambda i, o, l: (0,) * arr.ndim, **once)
    if do_norm:
        in_specs = [pl.BlockSpec((1, rows, model), lambda i, o, l, g=g: (o[i * group + g], 0, 0)) for g in range(group)]
        operands = [hid_or_x] * group + [g_in]
        in_specs.append(whole(g_in))
    else:
        in_specs, operands = [by_group(rows, model)], [hid_or_x]
    in_specs += [whole(w_k), whole(w_v), by_group(16, width // 2), whole(g_k), whole(cos_t), whole(sin_t)]
    operands += [w_k, w_v, qbd, g_k, cos_t, sin_t]
    out_specs = [by_group(rows, width), by_group(16, rows), by_group(16, HEAD)]
    out_shape = [jax.ShapeDtypeStruct((n_seq, rows, width), BF), jax.ShapeDtypeStruct((n_seq, 16, rows), F32), jax.ShapeDtypeStruct((n_seq, 16, HEAD), F32)]
    if do_norm:
        out_specs.insert(0, by_group(rows, model))
        out_shape.insert(0, jax.ShapeDtypeStruct((n_seq, rows, model), BF))
    return pl.pallas_call(
        functools.partial(fwd_body, do_norm, group, sizes),
        grid_spec=pltpu.PrefetchScalarGridSpec(num_scalar_prefetch=2, grid=(n_seq // group,), in_specs=in_specs, out_specs=out_specs,
                                              scratch_shapes=[pltpu.VMEM((group, rows, width // 2), BF)]),
        out_shape=out_shape,
        compiler_params=pltpu.CompilerParams(dimension_semantics=("arbitrary",), vmem_limit_bytes=VMEM),
        cost_estimate=pl.CostEstimate(flops=2 * n_seq * rows * model * width, bytes_accessed=n_seq * rows * model * 4, transcendentals=0),
        name="attn_fwd" + ("_norm" if do_norm else "") + str(rows),
    )(order, lens, *operands)


def bwd_body(group, sizes, lens_ref, kv_ref, p_ref, qbd_ref, dobd_ref, gk_ref, cos_ref, sin_ref, dkv_ref, dq_ref, dgk_ref, rot_ref, dkey_ref):
    step = pl.program_id(0)
    rows, width = kv_ref.shape[1], kv_ref.shape[2]
    kv_half = width // 2

    @pl.when(step == 0)
    def _():
        dgk_ref[...] = jnp.zeros_like(dgk_ref)

    def run(size):
        cos_t, sin_t = cos_ref[:size], sin_ref[:size]
        gk = gk_ref[...]
        prob = p_ref[:, :, :size].reshape(group * 16, size)
        d_prob = stacked([lax.dot_general(dobd_ref[g], kv_ref[g, :size, kv_half:], NT, preferred_element_type=F32) for g in range(group)])
        d_prob = d_prob.astype(BF).astype(F32)
        d_score = prob * (d_prob - jnp.sum(prob * d_prob, axis=-1, keepdims=True))
        d_score = (d_score * HEAD ** -0.5).astype(BF)
        prob = prob.astype(BF)
        for g in range(group):
            d_key = lax.dot_general(d_score[g * 16:(g + 1) * 16], qbd_ref[g], TN, preferred_element_type=F32)
            dkey_ref[g, :size, :] = d_key.astype(BF)
            d_val = lax.dot_general(prob[g * 16:(g + 1) * 16], dobd_ref[g], TN, preferred_element_type=F32)
            dkv_ref[g, :size, kv_half:] = d_val.astype(BF)
        d_gain = jnp.zeros((8, HEAD), F32)
        for g in range(group):
            for head in range(kv_half // HEAD):
                lanes = slice(head * HEAD, (head + 1) * HEAD)
                k_hat, scale = key_stats(kv_ref[g, :size, lanes])
                rot_ref[g, :size, lanes] = turn(k_hat * gk, cos_t, sin_t).astype(BF)
                d_norm = turn(dkey_ref[g, :size, lanes].astype(F32), cos_t, -sin_t)
                d_gain = d_gain + jnp.sum((d_norm * k_hat).reshape(size // 8, 8, HEAD), axis=0)
                d_hat = d_norm * gk
                d_raw = scale * (d_hat - k_hat * jnp.mean(k_hat * d_hat, axis=-1, keepdims=True))
                dkv_ref[g, :size, lanes] = d_raw.astype(BF)
        dgk_ref[...] += d_gain
        d_query = stacked([jnp.dot(d_score[g * 16:(g + 1) * 16], rot_ref[g, :size, :], preferred_element_type=F32) for g in range(group)])
        dq_ref[...] = take_diag(d_query).reshape(group, 16, HEAD)
        if size < rows:
            dkv_ref[:, size:, :] = jnp.zeros((group, rows - size, width), BF)

    variants(lens_ref[step * group + group - 1], sizes, run)


def attn_bwd(lens, group, sizes, kv, prob, qbd, dobd, g_k, cos_t, sin_t):
    n_seq, rows, width = kv.shape
    once = dict(pipeline_mode=pl.Buffered(buffer_count=1))
    by_group = lambda *shape: pl.BlockSpec((group,) + shape, lambda i, l: (i,) + (0,) * len(shape))
    whole = lambda arr: pl.BlockSpec(arr.shape, lambda i, l: (0,) * arr.ndim, **once)
    return pl.pallas_call(
        functools.partial(bwd_body, group, sizes),
        grid_spec=pltpu.PrefetchScalarGridSpec(
            num_scalar_prefetch=1, grid=(n_seq // group,),
            in_specs=[by_group(rows, width), by_group(16, rows), by_group(16, width // 2), by_group(16, width // 2), whole(g_k), whole(cos_t), whole(sin_t)],
            out_specs=[by_group(rows, width), by_group(16, HEAD), pl.BlockSpec((8, HEAD), lambda i, l: (0, 0))],
            scratch_shapes=[pltpu.VMEM((group, rows, width // 2), BF)] * 2),
        out_shape=[jax.ShapeDtypeStruct(kv.shape, BF), jax.ShapeDtypeStruct((n_seq, 16, HEAD), F32), jax.ShapeDtypeStruct((8, HEAD), F32)],
        compiler_params=pltpu.CompilerParams(dimension_semantics=("arbitrary",), vmem_limit_bytes=VMEM),
        cost_estimate=pl.CostEstimate(flops=20 * 1000 * n_seq * rows * width // 8, bytes_accessed=n_seq * rows * width * 4, transcendentals=0),
        name="attn_bwd" + str(rows),
    )(lens, kv, prob, qbd, dobd, g_k, cos_t, sin_t)


def dx_body(group, sizes, order_ref, lens_ref, dkv_ref, dkv2_ref, wk_ref, wv_ref, wk2_ref, wv2_ref, h_ref, gin_ref, dxl_ref, dhm_ref, out_ref, dgin_ref, dx_ref):
    step = pl.program_id(0)
    rows, model = h_ref.shape[1], h_ref.shape[2]
    kv_half = wk_ref.shape[1]
    last = lens_ref[step] - 1
    inner = lax.rem(step, group)
    wide_cols = 512

    @pl.when(step == 0)
    def _():
        dgin_ref[...] = jnp.zeros_like(dgin_ref)

    def run(size):
        @pl.when(inner == 0)
        def _():
            def project(d_ref, w_refs, add, j, carry):
                cols = pl.ds(pl.multiple_of(j * wide_cols, wide_cols), wide_cols)
                part = None
                for half, w_ref in enumerate(w_refs):
                    d_half = d_ref[:, :size, half * kv_half:(half + 1) * kv_half].reshape(group * size, kv_half)
                    term = lax.dot_general(d_half, w_ref[cols, :], NT, preferred_element_type=F32)
                    part = term if part is None else part + term
                part = part.reshape(group, size, wide_cols)
                dx_ref[:, :size, cols] = dx_ref[:, :size, cols] + part if add else part
                return carry

            lax.fori_loop(0, model // wide_cols, functools.partial(project, dkv_ref, (wk_ref, wv_ref), False), 0)
            lax.fori_loop(0, model // wide_cols, functools.partial(project, dkv2_ref, (wk2_ref, wv2_ref), True), 0)

        dx_ref[inner, pl.ds(last, 1), :] += dxl_ref[0]
        chunk = 32
        tiles = [slice(t, t + HEAD) for t in range(0, model, HEAD)]

        def finish(c, carry):
            start = pl.multiple_of(c * chunk, chunk)
            here = pl.ds(start, chunk)
            at_last = lax.broadcasted_iota(jnp.int32, (chunk, HEAD), 0) + start == last
            squares, cross = jnp.zeros((chunk, HEAD), F32), jnp.zeros((chunk, HEAD), F32)
            for t in tiles:
                hid = h_ref[0, here, t].astype(F32)
                squares = squares + hid * hid
                cross = cross + hid * (dx_ref[inner, here, t] * gin_ref[:, t])
            scale = lax.rsqrt(jnp.sum(squares, axis=-1, keepdims=True) / model + NORM_EPS)
            slope = scale * scale * scale * (jnp.sum(cross, axis=-1, keepdims=True) / model)
            for t in tiles:
                hid = h_ref[0, here, t].astype(F32)
                d_x = dx_ref[inner, here, t] * scale
                dgin_ref[:, t] += jnp.sum((d_x * hid).reshape(chunk // 8, 8, HEAD), axis=0)
                d_hid = d_x * gin_ref[:, t] - hid * slope
                out_ref[0, here, t] = (d_hid + jnp.where(at_last, dhm_ref[0][:, t], 0.0)).astype(BF)
            return carry

        lax.fori_loop(0, size // chunk, finish, 0)
        if size < out_ref.shape[1]:
            out_ref[0, size:, :] = jnp.zeros((out_ref.shape[1] - size, model), BF)

    variants(lens_ref[step - inner + group - 1], sizes, run)


def attn_dx(hid, order, lens, rows, group, sizes, dkv, dkv2, w_own, w_oth, g_in, d_xlast, d_hmid):
    n_seq, seq_len, model = hid.shape
    width = dkv.shape[-1]
    once = dict(pipeline_mode=pl.Buffered(buffer_count=1))
    by_group = lambda *shape: pl.BlockSpec((group,) + shape, lambda i, o, l: (i // group,) + (0,) * len(shape))
    whole = lambda arr: pl.BlockSpec(arr.shape, lambda i, o, l: (0,) * arr.ndim, **once)
    one_row = pl.BlockSpec((1, 1, model), lambda i, o, l: (i, 0, 0))
    weights = tuple(w_own) + tuple(w_oth)
    return pl.pallas_call(
        functools.partial(dx_body, group, sizes),
        grid_spec=pltpu.PrefetchScalarGridSpec(
            num_scalar_prefetch=2, grid=(n_seq,),
            in_specs=[by_group(rows, width), by_group(rows, width)] + [whole(w) for w in weights] +
                     [pl.BlockSpec((1, rows, model), lambda i, o, l: (o[i], 0, 0)), whole(g_in), one_row, one_row],
            out_specs=[pl.BlockSpec((1, seq_len, model), lambda i, o, l: (o[i], 0, 0)), pl.BlockSpec((8, model), lambda i, o, l: (0, 0))],
            scratch_shapes=[pltpu.VMEM((group, rows, model), F32)]),
        out_shape=[jax.ShapeDtypeStruct(hid.shape, BF), jax.ShapeDtypeStruct((8, model), F32)],
        compiler_params=pltpu.CompilerParams(dimension_semantics=("arbitrary",), vmem_limit_bytes=VMEM),
        cost_estimate=pl.CostEstimate(flops=4 * n_seq * rows * model * width, bytes_accessed=hid.size * 4, transcendentals=0),
        name="attn_dx" + str(rows),
    )(order, lens, dkv, dkv2, *weights, hid, g_in, d_xlast[:, None, :], d_hmid[:, None, :])


def wide(values):
    return values.astype(F32)


def narrow(values, unit):
    return (values * unit).astype(BF)


def swap_tp(values):
    return lax.ppermute(values, 'tp', SWAP)


def psum_tp(values):
    return values + swap_tp(values)


def swiglu(gate_in, up_in):
    return jax.nn.silu(gate_in) * up_in


def final_head(h_out, g_final):
    z_norm = norm_rows(h_out, g_final)
    return z_norm * lax.rsqrt(jnp.sum(z_norm * z_norm, axis=-1, keepdims=True))


def dot(a, b):
    return jnp.dot(a, b, preferred_element_type=F32)


def dot_nt(a, b):
    return lax.dot_general(a, b, NT, preferred_element_type=F32)


def dot_tn(a, b):
    return lax.dot_general(a, b, TN, preferred_element_type=F32)


Q_SIZES = (32, 64, 96, 128)
D_SIZES = (128, 256, 384, 512)


def solution(mesh):
    dp_size = mesh.shape['dp']

    def device_step(hid_q, hid_d, len_q, len_d, pos_doc, w_q, w_k, w_v, w_o, w_gate, w_up, w_down, g_in, g_q, g_k, g_post, g_final):
        g_in, g_q, g_k, g_post, g_final = (gain.astype(F32) for gain in (g_in, g_q, g_k, g_post, g_final))
        n_q, n_d = hid_q.shape[0], hid_d.shape[0]
        seq_len = hid_q.shape[1]
        n_query = n_q * dp_size

        ids = jnp.arange(n_q)
        before = (len_q[None, :] < len_q[:, None]) | ((len_q[None, :] == len_q[:, None]) & (ids[None, :] < ids[:, None]))
        rank = jnp.sum(before, axis=1)
        is_rank = rank[None, :] == ids[:, None]
        order_q = jnp.sum(jnp.where(is_rank, ids[None, :], 0), axis=1).astype(jnp.int32)
        lens_q = jnp.sum(jnp.where(is_rank, len_q[None, :], 0), axis=1).astype(jnp.int32)
        pos_sorted = jnp.sum(jnp.where(is_rank, pos_doc[None, :], 0), axis=1).astype(jnp.int32)
        order_d = jnp.arange(n_d, dtype=jnp.int32)
        lens = jnp.concatenate([lens_q, len_d])
        unit = jnp.minimum(len_d[0], 1).astype(F32)

        kv_half = w_k.shape[1]
        slab_rows = w_k.shape[0] // dp_size
        my_slab = lambda arr: lax.dynamic_slice_in_dim(arr, lax.axis_index('dp') * slab_rows, slab_rows, axis=0)
        slab = jnp.concatenate([my_slab(w_k), my_slab(w_v)], axis=1)
        w_kv2 = narrow(lax.all_gather(swap_tp(wide(slab)), 'dp', axis=0, tiled=True), unit)
        w_k2, w_v2 = w_kv2[:, :kv_half], w_kv2[:, kv_half:]

        h_last = jnp.concatenate([hid_q[order_q, lens_q - 1], hid_d[order_d, len_d - 1]], axis=0).astype(F32)
        x_last = norm_rows(h_last, g_in).astype(BF)
        q_raw = dot(x_last, w_q).astype(BF)
        q_cos, q_sin = rope_tables(lens - 1)
        q_rot, q_pull = jax.vjp(lambda raw, gain: rotate_query(raw, gain, q_cos, q_sin), q_raw, g_q)
        q_rot2 = narrow(swap_tp(wide(q_rot)), unit)
        qbd, qbd2 = block_diag(q_rot), block_diag(q_rot2)

        cos_t, sin_t = rope_tables(jnp.arange(seq_len))
        cos_q, sin_q = cos_t[:Q_MAX], sin_t[:Q_MAX]
        gin_row, gk_row = g_in[None, :], g_k[None, :]
        x_q, kv_q, p_q, o_q = attn_fwd(hid_q, order_q, lens_q, Q_MAX, 4, Q_SIZES, w_k, w_v, qbd[:n_q], gk_row, cos_q, sin_q, gin_row)
        x_d, kv_d, p_d, o_d = attn_fwd(hid_d, order_d, len_d, seq_len, 1, D_SIZES, w_k, w_v, qbd[n_q:], gk_row, cos_t, sin_t, gin_row)
        attn_out = jnp.concatenate([o_q, o_d], axis=0)[:, :q_rot.shape[1]].astype(BF).reshape(n_q + n_d, -1)
        attn_out, w_k2, w_v2 = lax.optimization_barrier((attn_out, w_k2, w_v2))

        h_mid = h_last + psum_tp(dot(attn_out, w_o))
        y_norm = norm_rows(h_mid, g_post).astype(BF)
        width = h_last.shape[1]
        gather = lambda arr: narrow(lax.all_gather(wide(arr), 'dp', axis=0, tiled=True), unit)
        early = gather(jnp.concatenate([x_last, y_norm, attn_out], axis=1))
        gate_val = dot(y_norm, w_gate).astype(BF)
        up_val = dot(y_norm, w_up).astype(BF)
        hidden_act, act_pull = jax.vjp(swiglu, gate_val.astype(F32), up_val.astype(F32))
        h_out = h_mid + psum_tp(dot(hidden_act.astype(BF), w_down))
        emb, head_pull = jax.vjp(final_head, h_out, g_final)
        emb_q, emb_d = emb[:n_q], emb[n_q:]

        all_docs = lax.all_gather(emb_d, 'dp', axis=0, tiled=True)
        logits = jnp.einsum('qd,kd->qk', emb_q, all_docs, precision=lax.Precision.HIGHEST) / TEMPERATURE
        log_norm = jax.nn.logsumexp(logits, axis=1)
        is_pos = jnp.arange(all_docs.shape[0])[None, :] == pos_sorted[:, None]
        loss_sorted = log_norm - jnp.sum(jnp.where(is_pos, logits, 0.0), axis=1)
        loss_rows = jnp.sum(jnp.where(is_rank, loss_sorted[:, None], 0.0), axis=0)
        d_logits = (jnp.exp(logits - log_norm[:, None]) - is_pos.astype(F32)) / (n_query * TEMPERATURE)
        d_emb_q = jnp.einsum('qk,kd->qd', d_logits, all_docs, precision=lax.Precision.HIGHEST)
        d_docs = jnp.einsum('qk,qd->kd', d_logits, emb_q, precision=lax.Precision.HIGHEST)
        d_docs = lax.all_to_all(d_docs, 'dp', 0, 0, tiled=True)
        d_emb_d = jnp.sum(d_docs.reshape(dp_size, n_d, width), axis=0)

        d_hout, d_gfinal = head_pull(jnp.concatenate([d_emb_q, d_emb_d], axis=0))
        d_hout_b = d_hout.astype(BF)
        d_act = dot_nt(d_hout_b, w_down).astype(BF)
        d_gate, d_up = act_pull(d_act.astype(F32))
        d_y = psum_tp(dot_nt(d_gate.astype(BF), w_gate) + dot_nt(d_up.astype(BF), w_up))
        d_ymid, d_gpost = norm_back(h_mid, g_post, d_y)
        d_hmid = d_hout + d_ymid
        d_hmid_b = d_hmid.astype(BF)
        d_hmid_b, early = lax.optimization_barrier((d_hmid_b, early))
        d_both = gather(jnp.concatenate([d_hout_b, d_hmid_b], axis=1))
        d_attn = dot_nt(d_hmid_b, w_o).astype(BF).reshape(q_rot.shape)
        d_attn2 = narrow(swap_tp(wide(d_attn)), unit)
        dobd, dobd2 = block_diag(d_attn), block_diag(d_attn2)

        dkv_q, dq_q, dgk_q = attn_bwd(lens_q, 4, Q_SIZES, kv_q, p_q, qbd[:n_q], dobd[:n_q], gk_row, cos_q, sin_q)
        dkv_d, dq_d, dgk_d = attn_bwd(len_d, 1, D_SIZES, kv_d, p_d, qbd[n_q:], dobd[n_q:], gk_row, cos_t, sin_t)
        d_qrot = jnp.concatenate([dq_q, dq_d], axis=0)[:, :q_rot.shape[1]].astype(BF)
        d_qrot, d_both = lax.optimization_barrier((d_qrot, d_both))
        d_qraw, d_gq = q_pull(d_qrot)
        d_xlast = psum_tp(dot_nt(d_qraw, w_q))
        d_qraw_all = gather(d_qraw)
        flat = lambda arr: arr.reshape(-1, arr.shape[-1])
        d_wkv = dot_tn(flat(x_q), flat(dkv_q)) + dot_tn(flat(x_d), flat(dkv_d))
        d_wkv, d_qraw_all = lax.optimization_barrier((d_wkv, d_qraw_all))
        d_wkv = lax.psum(d_wkv, 'dp')

        kv2_q, p2_q, _ = attn_fwd(x_q, order_q, lens_q, Q_MAX, 4, Q_SIZES, w_k2, w_v2, qbd2[:n_q], gk_row, cos_q, sin_q)
        kv2_d, p2_d, _ = attn_fwd(x_d, order_d, len_d, seq_len, 1, D_SIZES, w_k2, w_v2, qbd2[n_q:], gk_row, cos_t, sin_t)
        dkv2_q, _, _ = attn_bwd(lens_q, 4, Q_SIZES, kv2_q, p2_q, qbd2[:n_q], dobd2[:n_q], gk_row, cos_q, sin_q)
        dkv2_d, _, _ = attn_bwd(len_d, 1, D_SIZES, kv2_d, p2_d, qbd2[n_q:], dobd2[n_q:], gk_row, cos_t, sin_t)
        d_hid_q, dgin_q = attn_dx(hid_q, order_q, lens_q, Q_MAX, 4, Q_SIZES, dkv_q, dkv2_q, (w_k, w_v), (w_k2, w_v2), gin_row, d_xlast[:n_q], d_hmid[:n_q])
        d_hid_d, dgin_d = attn_dx(hid_d, order_d, len_d, seq_len, 1, D_SIZES, dkv_d, dkv2_d, (w_k, w_v), (w_k2, w_v2), gin_row, d_xlast[n_q:], d_hmid[n_q:])

        x_last_all, y_all, attn_all = early[:, :width], early[:, width:2 * width], early[:, 2 * width:]
        d_hout_all, d_hmid_all = d_both[:, :width], d_both[:, width:]
        act_all, act_all_pull = jax.vjp(swiglu, dot(y_all, w_gate).astype(BF).astype(F32), dot(y_all, w_up).astype(BF).astype(F32))
        d_gate_all, d_up_all = act_all_pull(dot_nt(d_hout_all, w_down).astype(BF).astype(F32))
        d_wdown = dot_tn(act_all.astype(BF), d_hout_all)
        d_wgate = dot_tn(y_all, d_gate_all.astype(BF))
        d_wup = dot_tn(y_all, d_up_all.astype(BF))
        d_wo = dot_tn(attn_all, d_hmid_all)
        d_wq = dot_tn(x_last_all, d_qraw_all)

        dp_sum = lambda vec: jnp.sum(lax.all_gather(vec, 'dp', axis=0), axis=0)
        d_heads = psum_tp(jnp.concatenate([d_gq, jnp.sum(dgk_q + dgk_d, axis=0)]))
        gains = dp_sum(jnp.concatenate([d_gpost, d_gfinal, d_heads]))
        d_gpost, d_gfinal, d_gq, d_gk = gains[:width], gains[width:2 * width], gains[2 * width:2 * width + HEAD], gains[2 * width + HEAD:]
        d_gin = dp_sum(jnp.sum(dgin_q + dgin_d, axis=0))
        return (loss_rows, d_hid_q, d_hid_d, d_wq, d_wkv[:, :kv_half], d_wkv[:, kv_half:], d_wo, d_wgate, d_wup, d_wdown,
                d_gin, d_gq, d_gk, d_gpost, d_gfinal)

    col_split = P(None, 'tp')
    row_split = P('tp', None)
    in_specs = (P('dp'), P('dp'), P('dp'), P('dp'), P('dp'), col_split, col_split, col_split, row_split, col_split, col_split, row_split, P(), P(), P(), P(), P())
    out_specs = (P('dp'), P('dp'), P('dp'), col_split, col_split, col_split, row_split, col_split, col_split, row_split, P(), P(), P(), P(), P())
    return jax.shard_map(device_step, mesh=mesh, in_specs=in_specs, out_specs=out_specs, check_vma=False)
```

time: 839 us -> 615 us (0.73)
  waiting for transfers between devices: 222 us -> 58.4 us
  Pallas kernels: 292 us -> 262 us
  blocking collectives: 53.2 us -> 28.8 us
    psum x1, waiting for transfers between devices: 91.7 us -> 9.85 us  [device_step(): d_wkv = lax.psum(d_wkv, 'dp')]
    unnamed x8 -> x5, waiting for transfers between devices: 46.2 us -> 0.08 us
    all_gather x4 -> x3, waiting for transfers between devices: 42.2 us -> 0.01 us  [device_step(): lax.all_gather(wide(arr), 'dp', axis=0, tiled=True)]
    psum x1 -> x0, blocking collectives: 38.6 us -> none  [device_step(): lax.psum(jnp.concatenate([d_gin * 0.5, d_gpost * 0.5, d_gfinal * 0.5, d_g...]
    pallas_call x4, Pallas kernels: 106 us -> 85.9 us  [attn_fwd(): pl.pallas_call(functools.partial(fwd_body, do_norm, group, sizes), grid_s...]
    all_gather x0 -> x2, blocking collectives: none -> 18.3 us  [device_step(): dp_sum = lambda vec: jnp.sum(lax.all_gather(vec, 'dp', axis=0), axis=0)]
    pallas_call x2, Pallas kernels: 131 us -> 116 us  [attn_dx(): pl.pallas_call(functools.partial(dx_body, group, sizes), grid_spec=pltpu....]
    ppermute x7 -> x8, waiting for transfers between devices: 42 us -> 42.3 us  [swap_tp(): return lax.ppermute(values, 'tp', SWAP)]
  transfers between devices with their start and end apart: 14 -> 14, of which waited for: 10 -> 7; matrix products, arithmetic and copies ran while one was open for 18% -> 18% of each run, Pallas kernels for 0% -> 43%
where the time goes in v2:
time: 615 us; the launch traced here: 608 us
  Pallas kernels  262 us (43%)
  matrix products  155 us (25%)
  waiting for transfers between devices  58.4 us (9%)
  local copies, waits for them, and re-layouts  38.5 us (6%)
  other arithmetic  33.3 us (5%)
  blocking collectives  28.8 us (5%)
  starting transfers between devices  16.4 us (3%)
  between operations  15 us (2%)
    pallas_call x2, Pallas kernels, attn_dx(): pl.pallas_call(functools.partial(dx_body, group, sizes), grid_spec=pltpu....  116 us
    pallas_call x4, Pallas kernels, attn_fwd(): pl.pallas_call(functools.partial(fwd_body, do_norm, group, sizes), grid_s...  85.9 us
    dot_general x7, matrix products, dot_tn(): return lax.dot_general(a, b, TN, preferred_element_type=F32)  81 us
    pallas_call x4, Pallas kernels, attn_bwd(): pl.pallas_call(functools.partial(bwd_body, group, sizes), grid_spec=pltpu...  60.8 us
    ppermute x8, waiting for transfers between devices, swap_tp(): return lax.ppermute(values, 'tp', SWAP)  42.3 us
    dot_general x7, matrix products, dot(): return jnp.dot(a, b, preferred_element_type=F32)  38.6 us
    dot_general x6, matrix products, dot_nt(): return lax.dot_general(a, b, NT, preferred_element_type=F32)  34.3 us
    all_gather x2, blocking collectives, device_step(): dp_sum = lambda vec: jnp.sum(lax.all_gather(vec, 'dp', axis=0), axis=0)  18.3 us
  transfers between devices with their start and end apart: 14, of which 7 were waited for; matrix products, arithmetic and copies ran while one was open for 18% of the time, Pallas kernels for 43%

profile of v2, /device:TPU:0, one launch (start us, length us, event | category | flops | bytes accessed | tf_op | source)
XLA Modules:
  0.0 607.7 jit_solution(2868222573330015348)
XLA Ops:
  7.3 1.1 constant_dynamic-slice_fusion
  8.5 3.3 collective-permute-start
  11.8 23.2 %collective-permute-done = f32[256,1024]{1,0:T(8,128)S(1)} collective-permute-done((f32[256,1024]{1,0:T(8,128)S(1)}, f32[256,1024]{1,0:T(8,128)S(1)}, u32[]{:S(2)}, u32[]{:S(2)}) %collective-permute-start) | collective-permute-done | bytes 1048608 | tf_op jit(solution)/shard_map/ppermute | solution.py:329
  36.1 1.5 gather_fusion.1
  38.0 1.7 gather_fusion
  39.8 3.1 fusion.18
  44.8 1.0 fusion.54
  45.8 1.0 pad_maximum_fusion.1
  47.8 13.6 %attn_fwd_norm512.1 = (bf16[2,512,2048]{2,1,0:T(8,128)(2,1)}, bf16[2,512,1024]{2,1,0:T(8,128)(2,1)}, f32[2,16,512]{2,1,0:T(8,128)}, f32[2,16,128]{2,1,0:T(8,128)}) custom-call(s32[2]{0:T(128)} %iota.137.order_ref, s32[2]{0:T(128)} %lens_ref.9, bf16[2,512,2048]{2,1,0:T(8,128)(2,1)} %h_ref.3, f32[1,2048]{1,0:T(1,128)} %bitcast.117, bf16[2048,512]{1,0:T(8,128)(2,1)} %wk_ref.3, ...), custom_call_target="tpu_custom_call" | custom-call | flops 4294967296 | bytes 8388608 | tf_op jit(solution)/shard_map/attn_fwd_norm512/pallas_call | solution.py:165
  63.8 40.3 %attn_fwd_norm128.1 = (bf16[32,128,2048]{2,1,0:T(8,128)(2,1)}, bf16[32,128,1024]{2,1,0:T(8,128)(2,1)}, f32[32,16,128]{2,1,0:T(8,128)}, f32[32,16,128]{2,1,0:T(8,128)}) custom-call(s32[32]{0:T(128)} %copy-done.31, s32[32]{0:T(128)} %copy-done.30, bf16[32,512,2048]{2,1,0:T(8,128)(2,1)} %h_ref.2, bf16[32,512,2048]{2,1,0:T(8,128)(2,1)} %h_ref.2, ...), custom_call_target="tpu_custom_call" | custom-call | flops 17179869184 | bytes 33554432 | tf_op jit(solution)/shard_map/attn_fwd_norm128/pallas_call | solution.py:165
  104.1 1.0 convert.16
  105.2 4.8 multiply_convert_fusion
  110.1 2.4 fusion.97
  112.5 1.3 copy-done
  114.6 1.8 collective-permute-start.1
  116.4 5.3 collective-permute-done.1
  122.0 2.3 fusion.1
  125.3 6.8 %fusion.2 = f32[34,3072]{1,0:T(8,128)S(1)} fusion(bf16[34,2048]{1,0:T(8,128)(2,1)S(1)} %multiply_convert_fusion.6, bf16[2048,3072]{1,0:T(8,128)(2,1)} %param.26), kind=kOutput, calls=%fused_computation.21 | convolution fusion | flops 428027904 | bytes 13139968 | tf_op jit(solution)/shard_map/dot_general | solution.py:346
  132.2 6.8 %fusion.42 = f32[34,2048]{1,0:T(8,128)S(1)} fusion(bf16[3072,2048]{1,0:T(8,128)(2,1)} %param.28, f32[34,3072]{1,0:T(8,128)S(1)} %fusion.1, f32[34,3072]{1,0:T(8,128)S(1)} %fusion.2), kind=kOutput, calls=%fused_computation.110 | convolution fusion | flops 428445696 | bytes 13697024 | tf_op jit(solution)/shard_map/dot_general | solution.py:346
  139.0 1.7 collective-permute-start.2
  141.0 5.0 collective-permute-done.2
  146.6 10.4 %all-gather.2 = f32[8,2,2048]{2,1,0:T(2,128)S(1)} all-gather(f32[1,2,2048]{2,1,0:T(2,128)S(1)} %slice_bitcast_fusion.2), channel_id=1, replica_groups=mesh['tp'=2,'dp'=8] {'dp'}, dimensions={0}, use_global_device_ids=true | all-gather | bytes 147456 | tf_op jit(solution)/shard_map/all_gather | solution.py:416
  158.5 3.4 all-to-all-start
  162.8 6.1 %all-to-all-done = f32[8,2,2048]{2,1,0:T(2,128)S(1)} async-done(((f32[8,2,2048]{2,1,0:T(2,128)}), f32[8,2,2048]{2,1,0:T(2,128)S(1)}, u32[]{:S(2)}, u32[]{:S(2)}) %all-to-all-start) | async-done | bytes 131104 | tf_op jit(solution)/shard_map/all_to_all | solution.py:425
  170.3 8.5 %fusion = f32[34,3072]{1,0:T(8,128)S(1)} fusion(bf16[34,2048]{1,0:T(8,128)(2,1)S(1)} %get-tuple-element.97, bf16[3072,2048]{1,0:T(8,128)(2,1)} %param.28), kind=kOutput, calls=%fused_computation.17 | convolution fusion | flops 428027904 | bytes 13139968 | tf_op jit(solution)/shard_map/dot_general | solution.py:350
  178.8 8.6 %fusion.43 = f32[34,2048]{1,0:T(8,128)S(1)} fusion(bf16[2048,3072]{1,0:T(8,128)(2,1)} %param.26, f32[34,3072]{1,0:T(8,128)S(1)} %fusion.2, f32[34,3072]{1,0:T(8,128)S(1)} %fusion, f32[34,3072]{1,0:T(8,128)S(1)} %fusion.1), kind=kOutput, calls=%fused_computation.111 | convolution fusion | flops 428967936 | bytes 14114816 | tf_op jit(solution)/shard_map/dot_general | solution.py:350
  187.5 3.9 convolution_add_fusion
  191.4 1.6 collective-permute-start.3
  193.6 6.3 %collective-permute-done.3 = f32[34,2048]{1,0:T(8,128)S(1)} collective-permute-done((f32[34,2048]{1,0:T(8,128)S(1)}, f32[34,2048]{1,0:T(8,128)S(1)}, u32[]{:S(2)}, u32[]{:S(2)}) %collective-permute-start.3) | collective-permute-done | bytes 278560 | tf_op jit(solution)/shard_map/ppermute | solution.py:329
  200.9 1.0 copy.59.dhm_ref
  202.5 5.1 multiply_convert_fusion.1
  207.6 2.4 reshape.373
  210.0 9.3 %convolution_convert_fusion = bf16[272,3072]{1,0:T(8,128)(2,1)} fusion(bf16[2048,3072]{1,0:T(8,128)(2,1)} %param.26, bf16[272,5120]{1,0:T(8,128)(2,1)S(1)} %reshape.373), kind=kOutput, calls=%fused_computation.13 | convolution fusion | flops 3423387648 | bytes 15368192 | tf_op jit(solution)/shard_map/dot_general | solution.py:346
  219.3 9.4 %convolution_convert_fusion.1 = bf16[272,3072]{1,0:T(8,128)(2,1)} fusion(bf16[2048,3072]{1,0:T(8,128)(2,1)} %param.27, bf16[272,5120]{1,0:T(8,128)(2,1)S(1)} %reshape.373), kind=kOutput, calls=%fused_computation.14 | convolution fusion | flops 3423387648 | bytes 15368192 | tf_op jit(solution)/shard_map/dot_general | solution.py:346
  228.8 1.4 convolution_convert_fusion.6
  230.2 1.6 collective-permute-start.5
  232.8 2.5 collective-permute-done.5
  238.3 6.1 %attn_bwd512.2 = (bf16[2,512,1024]{2,1,0:T(8,128)(2,1)}, f32[2,16,128]{2,1,0:T(8,128)}, f32[8,128]{1,0:T(8,128)}) custom-call(s32[2]{0:T(128)} %lens_ref.9, bf16[2,512,1024]{2,1,0:T(8,128)(2,1)} %get-tuple-element.62.kv_ref, f32[2,16,512]{2,1,0:T(8,128)} %get-tuple-element.63.p_ref, bf16[2,16,512]{2,1,0:T(8,128)(2,1)} %pad_slice_fusion.6.refs_4_.qbd_ref, ...), custom_call_target="tpu_custom_call" | custom-call | flops 2621440000 | bytes 4194304 | tf_op jit(solution)/shard_map/attn_bwd512/pallas_call | solution.py:224
  245.2 24.3 %attn_bwd128.2 = (bf16[32,128,1024]{2,1,0:T(8,128)(2,1)}, f32[32,16,128]{2,1,0:T(8,128)}, f32[8,128]{1,0:T(8,128)}) custom-call(s32[32]{0:T(128)} %copy-done.30, bf16[32,128,1024]{2,1,0:T(8,128)(2,1)} %get-tuple-element.51.kv_ref, f32[32,16,128]{2,1,0:T(8,128)} %get-tuple-element.52.p_ref, bf16[32,16,512]{2,1,0:T(8,128)(2,1)} %pad_slice_fusion.7.refs_7_.qbd_ref, ...), custom_call_target="tpu_custom_call" | custom-call | flops 10485760000 | bytes 16777216 | tf_op jit(solution)/shard_map/attn_bwd128/pallas_call | solution.py:224
  271.6 8.9 %attn_fwd512.1 = (bf16[2,512,1024]{2,1,0:T(8,128)(2,1)}, f32[2,16,512]{2,1,0:T(8,128)}, f32[2,16,128]{2,1,0:T(8,128)}) custom-call(s32[2]{0:T(128)} %iota.139.order_ref, s32[2]{0:T(128)} %lens_ref.9, bf16[2,512,2048]{2,1,0:T(8,128)(2,1)} %get-tuple-element.68.refs_0_, bf16[2048,512]{1,0:T(8,128)(2,1)} %get-tuple-element.56.refs_1_.wk2_ref, ...), custom_call_target="tpu_custom_call" | custom-call | flops 4294967296 | bytes 8388608 | tf_op jit(solution)/shard_map/attn_fwd512/pallas_call | solution.py:165
  281.4 5.9 attn_bwd512.3
  287.3 23.1 %attn_fwd128.1 = (bf16[32,128,1024]{2,1,0:T(8,128)(2,1)}, f32[32,16,128]{2,1,0:T(8,128)}, f32[32,16,128]{2,1,0:T(8,128)}) custom-call(s32[32]{0:T(128)} %copy-done.31, s32[32]{0:T(128)} %copy-done.30, bf16[32,128,2048]{2,1,0:T(8,128)(2,1)} %get-tuple-element.55.refs_0_, bf16[2048,512]{1,0:T(8,128)(2,1)} %get-tuple-element.56.refs_1_.wk2_ref, ...), custom_call_target="tpu_custom_call" | custom-call | flops 17179869184 | bytes 33554432 | tf_op jit(solution)/shard_map/attn_fwd128/pallas_call | solution.py:165
  310.4 24.4 %attn_bwd128.3 = (bf16[32,128,1024]{2,1,0:T(8,128)(2,1)}, f32[32,16,128]{2,1,0:T(8,128)}, f32[8,128]{1,0:T(8,128)}) custom-call(s32[32]{0:T(128)} %copy-done.30, bf16[32,128,1024]{2,1,0:T(8,128)(2,1)} %get-tuple-element.58.kv_ref, f32[32,16,128]{2,1,0:T(8,128)} %get-tuple-element.59.p_ref, bf16[32,16,512]{2,1,0:T(8,128)(2,1)} %pad_slice_fusion.3.refs_3_.qbd_ref, ...), custom_call_target="tpu_custom_call" | custom-call | flops 10485760000 | bytes 16777216 | tf_op jit(solution)/shard_map/attn_bwd128/pallas_call | solution.py:224
  334.9 22.9 %fusion.105 = f32[2048,1024,1]{1,0,2:T(8,128)S(1)} fusion(bf16[32,128,2048]{2,1,0:T(8,128)(2,1)} %get-tuple-element.55.refs_0_, bf16[32,128,1024]{2,1,0:T(8,128)(2,1)} %get-tuple-element.54.dkv_ref), kind=kOutput, calls=%fused_computation.234 | convolution fusion | flops 17179869184 | bytes 33554432 | tf_op jit(solution)/shard_map/dot_general | solution.py:354
  357.8 7.1 %bitcast_add_fusion = f32[2048,1024]{1,0:T(8,128)} fusion(f32[2048,1024,1]{1,0,2:T(8,128)S(1)} %fusion.105, bf16[2,512,2048]{2,1,0:T(8,128)(2,1)S(1)} %copy-done.39, bf16[2,512,1024]{2,1,0:T(8,128)(2,1)S(1)} %copy-done.40), kind=kOutput, calls=%fused_computation.2 | convolution fusion | flops 4297064448 | bytes 23068672 | tf_op jit(solution)/shard_map/dot_general | solution.py:354
  364.9 4.4 multiply_convert_fusion.2
  369.3 3.2 reshape.374
  372.6 7.2 %fusion.19 = f32[1024,2048]{1,0:T(8,128)} fusion(bf16[272,4096]{1,0:T(8,128)(2,1)} %reshape.374, bf16[272,5120]{1,0:T(8,128)(2,1)S(1)} %reshape.373), kind=kOutput, calls=%fused_computation.39 | convolution fusion | flops 1140850688 | bytes 10059776 | tf_op jit(solution)/shard_map/dot_general | solution.py:354
  379.8 8.3 %convolution_convert_fusion.2 = bf16[272,3072]{1,0:T(8,128)(2,1)S(1)} fusion(bf16[3072,2048]{1,0:T(8,128)(2,1)} %param.28, bf16[272,4096]{1,0:T(8,128)(2,1)S(1)} %copy-done.2), kind=kOutput, calls=%fused_computation.15 | convolution fusion | flops 3423387648 | bytes 15368192 | tf_op jit(solution)/shard_map/dot_general | solution.py:350
  388.1 12.5 %fusion.15 = f32[2048,3072]{1,0:T(8,128)} fusion(bf16[272,3072]{1,0:T(8,128)(2,1)S(1)} %convolution_convert_fusion.2, bf16[272,3072]{1,0:T(8,128)(2,1)S(1)} %copy-done.6, bf16[272,5120]{1,0:T(8,128)(2,1)S(1)} %reshape.373), kind=kOutput, calls=%fused_computation.33 | convolution fusion | flops 3429236736 | bytes 29622272 | tf_op jit(solution)/shard_map/dot_general | solution.py:354
  400.7 12.9 %fusion.11 = f32[2048,3072]{1,0:T(8,128)} fusion(bf16[272,3072]{1,0:T(8,128)(2,1)S(1)} %copy-done.6, bf16[272,3072]{1,0:T(8,128)(2,1)S(1)} %copy-done.38, bf16[272,3072]{1,0:T(8,128)(2,1)S(1)} %convolution_convert_fusion.2, bf16[272,5120]{1,0:T(8,128)(2,1)S(1)} %reshape.373), kind=kOutput, calls=%fused_computation.31 | convolution fusion | flops 3434250240 | bytes 31293440 | tf_op jit(solution)/shard_map/dot_general | solution.py:354
  413.6 12.6 %fusion.13 = f32[3072,2048]{1,0:T(8,128)} fusion(bf16[272,3072]{1,0:T(8,128)(2,1)S(1)} %copy-done.38, bf16[272,3072]{1,0:T(8,128)(2,1)S(1)} %copy-done.6, bf16[272,4096]{1,0:T(8,128)(2,1)S(1)} %copy-done.2), kind=kOutput, calls=%fused_computation.32 | convolution fusion | flops 3429236736 | bytes 29622272 | tf_op jit(solution)/shard_map/dot_general | solution.py:354
  427.7 1.6 collective-permute-start.7
  429.3 3.5 fusion.104
  433.4 9.5 %all-gather.6 = f32[8,1,4352]{2,1,0:T(1,128)S(1)} all-gather(f32[1,1,4352]{2,1,0:T(1,128)S(1)} %reshape.364), channel_id=3, replica_groups=mesh['tp'=2,'dp'=8] {'dp'}, dimensions={0}, use_global_device_ids=true | all-gather | bytes 156672 | tf_op jit(solution)/shard_map/all_gather | solution.py:471
  444.1 1.0 add.203
  447.0 21.5 %attn_dx512.1 = (bf16[2,512,2048]{2,1,0:T(8,128)(2,1)}, f32[8,2048]{1,0:T(8,128)}) custom-call(s32[2]{0:T(128)} %iota.138.order_ref, s32[2]{0:T(128)} %lens_ref.9, bf16[2,512,1024]{2,1,0:T(8,128)(2,1)} %get-tuple-element.67.dkv_ref, bf16[2,512,1024]{2,1,0:T(8,128)(2,1)} %get-tuple-element.71.dkv2_ref, bf16[2048,512]{1,0:T(8,128)(2,1)} %wk_ref.3, ...), custom_call_target="tpu_custom_call" | custom-call | flops 8589934592 | bytes 8388608 | tf_op jit(solution)/shard_map/attn_dx512/pallas_call | solution.py:305
  468.5 1.4 multiply_convert_fusion.3
  471.9 1.0 copy.58.dxl_ref
  472.9 94.2 %attn_dx128.1 = (bf16[32,512,2048]{2,1,0:T(8,128)(2,1)}, f32[8,2048]{1,0:T(8,128)}) custom-call(s32[32]{0:T(128)} %copy-done.31, s32[32]{0:T(128)} %copy-done.30, bf16[32,128,1024]{2,1,0:T(8,128)(2,1)} %get-tuple-element.54.dkv_ref, bf16[32,128,1024]{2,1,0:T(8,128)(2,1)} %get-tuple-element.60.dkv2_ref, bf16[2048,512]{1,0:T(8,128)(2,1)} %wk_ref.3, ...), custom_call_target="tpu_custom_call" | custom-call | flops 34359738368 | bytes 134217728 | tf_op jit(solution)/shard_map/attn_dx128/pallas_call | solution.py:305
  568.0 8.9 %all-gather = f32[16384]{0:T(1024)S(1)} all-gather(f32[2048]{0:T(1024)S(1)} %add_reduce_fusion), channel_id=2, replica_groups=mesh['tp'=2,'dp'=8] {'dp'}, dimensions={0}, use_global_device_ids=true | all-gather | bytes 73728 | tf_op jit(solution)/shard_map/all_gather | solution.py:471
  577.5 5.8 fusion.21
  583.3 9.9 %all-reduce.8.cloned.1.call-done = f32[2048,1024]{1,0:T(8,128)} async-done(((f32[2048,1024]{1,0:T(8,128)}), f32[2048,1024]{1,0:T(8,128)}) %all-reduce.8.cloned.1.call-update) | async-done | bytes 8388624 | tf_op jit(solution)/shard_map/psum | solution.py:452
  593.1 7.8 %fusion.96 = (f32[2048,512]{1,0:T(8,128)}, f32[2048,512]{1,0:T(8,128)}) fusion(f32[2048,1024]{1,0:T(8,128)} %all-reduce.8.cloned.1.call-done), kind=kLoop, calls=%fused_computation.225 | loop fusion | bytes 16777216 | tf_op jit(solution)/shard_map/slice | solution.py:476
  (227 shorter events, 32.0 us)
Async XLA Ops:
  7.2 28.9 %copy-start.25 = (bf16[2048]{0:T(1024)(128)(2,1)S(1)}, bf16[2048]{0:T(1024)(128)(2,1)}, u32[]{:S(2)}) copy-start(bf16[2048]{0:T(1024)(128)(2,1)} %param.29) | copy-start | bytes 12292
  7.2 28.9 %copy-start.36 = (s32[2]{0:T(128)S(1)}, s32[2]{0:T(128)}, u32[]{:S(2)}) copy-start(s32[2]{0:T(128)} %lens_ref.9) | copy-start | bytes 28
  7.2 30.4 %copy-start.33 = (s32[32]{0:T(128)S(1)}, s32[32]{0:T(128)}, u32[]{:S(2)}) copy-start(s32[32]{0:T(128)} %param.19) | copy-start | bytes 388
  7.2 30.6 %copy-start.32 = (s32[32]{0:T(128)S(1)}, s32[32]{0:T(128)}, u32[]{:S(2)}) copy-start(s32[32]{0:T(128)} %param.21) | copy-start | bytes 388
  7.2 98.0 %all-gather.12.cloned.1.call-start = ((), (), s32[]{:S(2)}) async-start(), calls=%async_computation.1 | async-start | bytes 9437184 | tf_op jit(solution)/shard_map/all_gather | solution.py:385
  8.5 26.5 %collective-permute-start = (f32[256,1024]{1,0:T(8,128)S(1)}, f32[256,1024]{1,0:T(8,128)S(1)}, u32[]{:S(2)}, u32[]{:S(2)}) collective-permute-start(f32[256,1024]{1,0:T(8,128)S(1)} %maximum_convert_fusion), channel_id=1, source_target_pairs={{0,8},{8,0},{1,9},{9,1},{2,10},{10,2},{3,11},{11,3},{4,12},{12,4},... | collective-permute-start | bytes 3145736 | tf_op jit(solution)/shard_map/ppermute | solution.py:329
  35.0 1.0 copy-start.9
  36.0 7.0 %copy-start.34 = (bf16[128]{0:T(256)(128)(2,1)S(1)}, bf16[128]{0:T(256)(128)(2,1)}, u32[]{:S(2)}) copy-start(bf16[128]{0:T(256)(128)(2,1)} %param.30) | copy-start | bytes 772
  36.0 166.5 %all-gather.14.cloned.1.call-start = ((), (), s32[]{:S(2)}) async-start(), calls=%async_computation.3 | async-start | bytes 7372800 | tf_op jit(solution)/shard_map/all_gather | solution.py:407
  36.1 7.7 %copy-start.16 = (f32[2048]{0:T(1024)}, f32[2048]{0:T(1024)S(1)}, u32[]{:S(2)}) copy-start(f32[2048]{0:T(1024)S(1)} %convert_element_type.188) | copy-start | bytes 24580
  37.9 5.9 copy-start.30
  37.9 5.9 copy-start.31
  42.9 3.9 copy-start.35
  43.0 18.5 %copy-start.3 = (f32[5,8,8,128]{3,2,1,0:T(8,128)}, f32[5,8,8,128]{3,2,1,0:T(8,128)S(1)}, u32[]{:S(2)}) copy-start(f32[5,8,8,128]{3,2,1,0:T(8,128)S(1)} %copy.64) | copy-start | bytes 491524
  43.0 1.2 copy-start.23
  43.2 18.2 %copy-start.19 = (f32[34,8]{0,1:T(8,128)}, f32[34,8]{0,1:T(8,128)S(1)}, u32[]{:S(2)}) copy-start(f32[34,8]{0,1:T(8,128)S(1)} %copy.54) | copy-start | bytes 3268
  43.3 0.9 copy-start.10
  43.7 1.1 copy-start.12
  43.7 2.1 copy-start.14
  63.8 41.4 %copy-start.37 = (s32[2]{0:T(128)S(1)}, s32[2]{0:T(128)}, u32[]{:S(2)}) copy-start(s32[2]{0:T(128)} %lens_ref.9) | copy-start | bytes 28
  105.2 16.8 %slice-start = ((s8[12582912]{0:T(1024)(128)(4,1)}), s8[4194304]{0:T(1024)(128)(4,1)S(1)}, s32[]{:S(2)}) async-start(s8[12582912]{0:T(1024)(128)(4,1)} %bitcast.99), calls=%async_computation.6 | async-start | bytes 8388608
  105.2 16.8 %slice-start.1 = ((s8[12582912]{0:T(1024)(128)(4,1)}), s8[4194304]{0:T(1024)(128)(4,1)S(1)}, s32[]{:S(2)}) async-start(s8[12582912]{0:T(1024)(128)(4,1)} %bitcast.99), calls=%async_computation.7 | async-start | bytes 8388608
  110.1 3.7 copy-start
  110.1 11.9 %slice-start.2 = ((s8[12582912]{0:T(1024)(128)(4,1)}), s8[4194304]{0:T(1024)(128)(4,1)S(1)}, s32[]{:S(2)}) async-start(s8[12582912]{0:T(1024)(128)(4,1)} %bitcast.99), calls=%async_computation.8 | async-start | bytes 8388608
  112.5 3.9 copy-start.26
  112.5 9.2 %copy-start.17 = (f32[2048]{0:T(1024)S(1)}, f32[2048]{0:T(1024)}, u32[]{:S(2)}) copy-start(f32[2048]{0:T(1024)} %copy-done.16) | copy-start | bytes 24580
  114.6 7.1 %collective-permute-start.1 = (f32[34,2048]{1,0:T(8,128)S(1)}, f32[34,2048]{1,0:T(8,128)S(1)}, u32[]{:S(2)}, u32[]{:S(2)}) collective-permute-start(f32[34,2048]{1,0:T(8,128)S(1)} %fusion.103), channel_id=1, source_target_pairs={{0,8},{8,0},{1,9},{9,1},{2,10},{10,2},{3,11},{11,3},{4,12},{12,4},... | collective-permute-start | bytes 835592 | tf_op jit(solution)/shard_map/ppermute | solution.py:329
  132.2 8.9 %copy-start.27 = (bf16[2048]{0:T(1024)(128)(2,1)S(1)}, bf16[2048]{0:T(1024)(128)(2,1)}, u32[]{:S(2)}) copy-start(bf16[2048]{0:T(1024)(128)(2,1)} %param.33) | copy-start | bytes 12292
  139.0 7.1 %collective-permute-start.2 = (f32[34,2048]{1,0:T(8,128)S(1)}, f32[34,2048]{1,0:T(8,128)S(1)}, u32[]{:S(2)}, u32[]{:S(2)}) collective-permute-start(f32[34,2048]{1,0:T(8,128)S(1)} %fusion.42), channel_id=1, source_target_pairs={{0,8},{8,0},{1,9},{9,1},{2,10},{10,2},{3,11},{11,3},{4,12},{12,4},... | collective-permute-start | bytes 835592 | tf_op jit(solution)/shard_map/ppermute | solution.py:329
  140.8 52.3 %collective-permute-start.4 = (f32[34,8,128]{2,1,0:T(8,128)S(1)}, f32[34,8,128]{2,1,0:T(8,128)S(1)}, u32[]{:S(2)}, u32[]{:S(2)}) collective-permute-start(f32[34,8,128]{2,1,0:T(8,128)S(1)} %get-tuple-element.93), channel_id=1, source_target_pairs={{0,8},{8,0},{1,9},{9,1},{2,10},{10,2},{3,11},{11,3},{4,12},{12,4},... | collective-permute-start | bytes 417800 | tf_op jit(solution)/shard_map/ppermute | solution.py:329
  158.5 10.4 %all-to-all-start = ((f32[8,2,2048]{2,1,0:T(2,128)}), f32[8,2,2048]{2,1,0:T(2,128)S(1)}, u32[]{:S(2)}, u32[]{:S(2)}) async-start(f32[8,2,2048]{2,1,0:T(2,128)} %all_to_all.6), calls=%async_computation | async-start | bytes 262144 | tf_op jit(solution)/shard_map/all_to_all | solution.py:425
  161.9 203.0 %all-gather.16.cloned.1.call-start = ((), (), s32[]{:S(2)}) async-start(), calls=%async_computation.4 | async-start | bytes 5898240 | tf_op jit(solution)/shard_map/all_gather | solution.py:407
  170.3 17.2 %slice-start.3 = ((s8[12582912]{0:T(1024)(128)(4,1)}), s8[4194304]{0:T(1024)(128)(4,1)S(1)}, s32[]{:S(2)}) async-start(s8[12582912]{0:T(1024)(128)(4,1)} %bitcast.101), calls=%async_computation.9 | async-start | bytes 8388608
  170.3 17.2 %slice-start.4 = ((s8[12582912]{0:T(1024)(128)(4,1)}), s8[4194304]{0:T(1024)(128)(4,1)S(1)}, s32[]{:S(2)}) async-start(s8[12582912]{0:T(1024)(128)(4,1)} %bitcast.101), calls=%async_computation.10 | async-start | bytes 8388608
  178.8 8.6 %slice-start.5 = ((s8[12582912]{0:T(1024)(128)(4,1)}), s8[4194304]{0:T(1024)(128)(4,1)S(1)}, s32[]{:S(2)}) async-start(s8[12582912]{0:T(1024)(128)(4,1)} %bitcast.101), calls=%async_computation.11 | async-start | bytes 8388608
  191.4 8.6 %collective-permute-start.3 = (f32[34,2048]{1,0:T(8,128)S(1)}, f32[34,2048]{1,0:T(8,128)S(1)}, u32[]{:S(2)}, u32[]{:S(2)}) collective-permute-start(f32[34,2048]{1,0:T(8,128)S(1)} %convolution_add_fusion), channel_id=1, source_target_pairs={{0,8},{8,0},{1,9},{9,1},{2,10},{10,2},{3,11},{11,3},{4,12},{12,4},... | collective-permute-start | bytes 835592 | tf_op jit(solution)/shard_map/ppermute | solution.py:329
  219.3 9.4 %copy-start.1 = (bf16[1024,2048]{1,0:T(8,128)(2,1)S(1)}, bf16[1024,2048]{1,0:T(8,128)(2,1)}, u32[]{:S(2)}) copy-start(bf16[1024,2048]{1,0:T(8,128)(2,1)} %param.25) | copy-start | bytes 12582916
  230.2 5.1 collective-permute-start.5
  232.8 235.8 %all-gather.18.cloned.1.call-start = ((), (), s32[]{:S(2)}) async-start(), calls=%async_computation.5 | async-start | bytes 1474560 | tf_op jit(solution)/shard_map/all_gather | solution.py:407
  271.6 8.9 %copy-start.28 = (f32[8,128]{1,0:T(8,128)S(1)}, f32[8,128]{1,0:T(8,128)}, u32[]{:S(2)}) copy-start(f32[8,128]{1,0:T(8,128)} %get-tuple-element.80) | copy-start | bytes 12292
  271.6 8.9 %copy-start.29 = (f32[8,128]{1,0:T(8,128)S(1)}, f32[8,128]{1,0:T(8,128)}, u32[]{:S(2)}) copy-start(f32[8,128]{1,0:T(8,128)} %get-tuple-element.79) | copy-start | bytes 12292
  334.8 23.0 %copy-start.39 = (bf16[2,512,2048]{2,1,0:T(8,128)(2,1)S(1)}, bf16[2,512,2048]{2,1,0:T(8,128)(2,1)}, u32[]{:S(2)}) copy-start(bf16[2,512,2048]{2,1,0:T(8,128)(2,1)} %get-tuple-element.68.refs_0_) | copy-start | bytes 12582916
  334.9 23.0 %copy-start.40 = (bf16[2,512,1024]{2,1,0:T(8,128)(2,1)S(1)}, bf16[2,512,1024]{2,1,0:T(8,128)(2,1)}, u32[]{:S(2)}) copy-start(bf16[2,512,1024]{2,1,0:T(8,128)(2,1)} %get-tuple-element.67.dkv_ref) | copy-start | bytes 6291460
  372.6 7.2 %copy-start.2 = (bf16[272,4096]{1,0:T(8,128)(2,1)S(1)}, bf16[272,4096]{1,0:T(8,128)(2,1)}, u32[]{:S(2)}) copy-start(bf16[272,4096]{1,0:T(8,128)(2,1)} %reshape.374) | copy-start | bytes 6684676
  379.8 8.4 %copy-start.6 = (bf16[272,3072]{1,0:T(8,128)(2,1)S(1)}, bf16[272,3072]{1,0:T(8,128)(2,1)}, u32[]{:S(2)}) copy-start(bf16[272,3072]{1,0:T(8,128)(2,1)} %convolution_convert_fusion) | copy-start | bytes 5013508
  388.1 12.6 %copy-start.38 = (bf16[272,3072]{1,0:T(8,128)(2,1)S(1)}, bf16[272,3072]{1,0:T(8,128)(2,1)}, u32[]{:S(2)}) copy-start(bf16[272,3072]{1,0:T(8,128)(2,1)} %convolution_convert_fusion.1) | copy-start | bytes 5013508
  413.5 12.6 %copy-start.15 = (f32[34,128]{1,0:T(8,128)S(1)}, f32[34,128]{1,0:T(8,128)}, u32[]{:S(2)}) copy-start(f32[34,128]{1,0:T(8,128)} %copy-done.14) | copy-start | bytes 52228
  413.5 12.8 %copy-start.4 = (f32[5,8,8,128]{3,2,1,0:T(8,128)S(1)}, f32[5,8,8,128]{3,2,1,0:T(8,128)}, u32[]{:S(2)}) copy-start(f32[5,8,8,128]{3,2,1,0:T(8,128)} %copy-done.3) | copy-start | bytes 491524
  413.6 12.8 %copy-start.11 = (f32[34,8]{1,0:T(8,128)S(1)}, f32[34,8]{1,0:T(8,128)}, u32[]{:S(2)}) copy-start(f32[34,8]{1,0:T(8,128)} %copy-done.10) | copy-start | bytes 3268
  413.6 12.8 %copy-start.13 = (f32[34,128]{1,0:T(8,128)S(1)}, f32[34,128]{1,0:T(8,128)}, u32[]{:S(2)}) copy-start(f32[34,128]{1,0:T(8,128)} %copy-done.12) | copy-start | bytes 52228
  413.6 12.8 %copy-start.24 = (f32[128]{0:T(128)S(1)}, f32[128]{0:T(128)}, u32[]{:S(2)}) copy-start(f32[128]{0:T(128)} %copy-done.23) | copy-start | bytes 1540
  413.6 13.1 %copy-start.20 = (f32[34,8]{0,1:T(8,128)S(1)}, f32[34,8]{0,1:T(8,128)}, u32[]{:S(2)}) copy-start(f32[34,8]{0,1:T(8,128)} %copy-done.19) | copy-start | bytes 3268
  426.3 7.1 %copy-start.21 = (f32[2048]{0:T(1024)S(1)}, f32[2048]{0:T(1024)}, u32[]{:S(2)}) copy-start(f32[2048]{0:T(1024)} %get-tuple-element.83) | copy-start | bytes 24580
  426.3 7.1 %copy-start.22 = (f32[2048]{0:T(1024)S(1)}, f32[2048]{0:T(1024)}, u32[]{:S(2)}) copy-start(f32[2048]{0:T(1024)} %get-tuple-element.81) | copy-start | bytes 24580
  427.6 165.5 %all-reduce.8.cloned.1.call-start = ((), (), s32[]{:S(2)}) async-start(), calls=%async_computation.2 | async-start | bytes 16777216 | tf_op jit(solution)/shard_map/psum | solution.py:452
  427.7 5.7 collective-permute-start.7
  432.9 11.2 %collective-permute-start.6 = (f32[34,2048]{1,0:T(8,128)S(1)}, f32[34,2048]{1,0:T(8,128)}, u32[]{:S(2)}, u32[]{:S(2)}) collective-permute-start(f32[34,2048]{1,0:T(8,128)S(1)} %fusion.104), channel_id=1, source_target_pairs={{0,8},{8,0},{1,9},{9,1},{2,10},{10,2},{3,11},{11,3},{4,12},{12,4},... | collective-permute-start | bytes 835592 | tf_op jit(solution)/shard_map/ppermute | solution.py:329
  445.1 0.7 copy-start.7
  470.9 1.0 copy-start.8
  472.9 94.2 %copy-start.18 = (f32[8,2048]{1,0:T(8,128)S(1)}, f32[8,2048]{1,0:T(8,128)}, u32[]{:S(2)}) copy-start(f32[8,2048]{1,0:T(8,128)} %get-tuple-element.78) | copy-start | bytes 196612
  472.9 104.6 %copy-start.5 = (bf16[272,1024]{1,0:T(8,128)(2,1)S(1)}, bf16[272,1024]{1,0:T(8,128)(2,1)}, u32[]{:S(2)}) copy-start(bf16[272,1024]{1,0:T(8,128)(2,1)} %reshape.375) | copy-start | bytes 1671172
Sparse Core Ops, SparseCore 0:
  36.1 51.4 all-gather.11
  125.4 45.5 all-gather.13
  232.9 35.2 all-gather.15
  427.7 20.9 all-gather.17
  471.1 122.0 all-reduce.7

commit v3 on v2

--- a/solution.py
+++ b/solution.py
@@ -103,22 +103,35 @@
     h_refs, refs = refs[:group if do_norm else 1], refs[group if do_norm else 1:]
     if do_norm:
         gin_ref, wk_ref, wv_ref, qbd_ref, gk_ref, cos_ref, sin_ref, x_ref, kv_ref, p_ref, o_ref, rot_ref = refs
-        for g in range(group):
-            def norm_chunk(c, carry, g=g):
-                here = pl.ds(pl.multiple_of(c * 32, 32), 32)
-                hid = h_refs[g][0, here, :].astype(F32)
-                scale = lax.rsqrt(jnp.mean(hid * hid, axis=-1, keepdims=True) + NORM_EPS)
-                x_ref[g, here, :] = (hid * scale * gin_ref[...]).astype(BF)
-                return carry
-
-            lax.fori_loop(0, x_ref.shape[1] // 32, norm_chunk, 0)
     else:
         wk_ref, wv_ref, qbd_ref, gk_ref, cos_ref, sin_ref, kv_ref, p_ref, o_ref, rot_ref = refs
         x_ref = h_refs[0]
     kv_half = wk_ref.shape[1]
     step = pl.program_id(0)
 
+    def norm(size):
+        chunk, model = 32, x_ref.shape[2]
+        tiles = [slice(t, t + HEAD) for t in range(0, model, HEAD)]
+        for g in range(group):
+            def norm_chunk(c, carry, g=g):
+                here = pl.ds(pl.multiple_of(c * chunk, chunk), chunk)
+                squares = jnp.zeros((chunk, HEAD), F32)
+                for t in tiles:
+                    hid = h_refs[g][0, here, t].astype(F32)
+                    squares = squares + hid * hid
+                scale = lax.rsqrt(jnp.sum(squares, axis=-1, keepdims=True) / model + NORM_EPS)
+                for t in tiles:
+                    hid = h_refs[g][0, here, t].astype(F32)
+                    x_ref[g, here, t] = (hid * scale * gin_ref[:, t]).astype(BF)
+                return carry
+
+            lax.fori_loop(0, size // chunk, norm_chunk, 0)
+        if size < x_ref.shape[1]:
+            x_ref[:, size:, :] = jnp.zeros((group, x_ref.shape[1] - size, model), BF)
+
     def run(size):
+        if do_norm:
+            norm(size)
         for at, w_ref in ((0, wk_ref), (kv_half, wv_ref)):
             x_val = x_ref[:, :size, :].reshape(group * size, x_ref.shape[2])
             out = jnp.dot(x_val, w_ref[...], preferred_element_type=F32)
@@ -157,15 +170,14 @@
         in_specs, operands = [by_group(rows, model)], [hid_or_x]
     in_specs += [whole(w_k), whole(w_v), by_group(16, width // 2), whole(g_k), whole(cos_t), whole(sin_t)]
     operands += [w_k, w_v, qbd, g_k, cos_t, sin_t]
-    out_specs = [by_group(rows, width), by_group(16, rows), by_group(16, HEAD)]
-    out_shape = [jax.ShapeDtypeStruct((n_seq, rows, width), BF), jax.ShapeDtypeStruct((n_seq, 16, rows), F32), jax.ShapeDtypeStruct((n_seq, 16, HEAD), F32)]
+    out_specs = [by_group(rows, width), by_group(16, rows), by_group(16, HEAD), by_group(rows, width // 2)]
+    out_shape = [jax.ShapeDtypeStruct((n_seq, rows, width), BF), jax.ShapeDtypeStruct((n_seq, 16, rows), F32), jax.ShapeDtypeStruct((n_seq, 16, HEAD), F32), jax.ShapeDtypeStruct((n_seq, rows, width // 2), BF)]
     if do_norm:
         out_specs.insert(0, by_group(rows, model))
         out_shape.insert(0, jax.ShapeDtypeStruct((n_seq, rows, model), BF))
     return pl.pallas_call(
         functools.partial(fwd_body, do_norm, group, sizes),
-        grid_spec=pltpu.PrefetchScalarGridSpec(num_scalar_prefetch=2, grid=(n_seq // group,), in_specs=in_specs, out_specs=out_specs,
-                                              scratch_shapes=[pltpu.VMEM((group, rows, width // 2), BF)]),
+        grid_spec=pltpu.PrefetchScalarGridSpec(num_scalar_prefetch=2, grid=(n_seq // group,), in_specs=in_specs, out_specs=out_specs),
         out_shape=out_shape,
         compiler_params=pltpu.CompilerParams(dimension_semantics=("arbitrary",), vmem_limit_bytes=VMEM),
         cost_estimate=pl.CostEstimate(flops=2 * n_seq * rows * model * width, bytes_accessed=n_seq * rows * model * 4, transcendentals=0),
@@ -173,7 +185,7 @@
     )(order, lens, *operands)
 
 
-def bwd_body(group, sizes, lens_ref, kv_ref, p_ref, qbd_ref, dobd_ref, gk_ref, cos_ref, sin_ref, dkv_ref, dq_ref, dgk_ref, rot_ref, dkey_ref):
+def bwd_body(group, sizes, lens_ref, kv_ref, rot_ref, p_ref, qbd_ref, dobd_ref, gk_ref, cos_ref, sin_ref, dk_ref, dv_ref, dq_ref, dgk_ref, dkey_ref):
     step = pl.program_id(0)
     rows, width = kv_ref.shape[1], kv_ref.shape[2]
     kv_half = width // 2
@@ -195,28 +207,28 @@
             d_key = lax.dot_general(d_score[g * 16:(g + 1) * 16], qbd_ref[g], TN, preferred_element_type=F32)
             dkey_ref[g, :size, :] = d_key.astype(BF)
             d_val = lax.dot_general(prob[g * 16:(g + 1) * 16], dobd_ref[g], TN, preferred_element_type=F32)
-            dkv_ref[g, :size, kv_half:] = d_val.astype(BF)
+            dv_ref[g, :size, :] = d_val.astype(BF)
         d_gain = jnp.zeros((8, HEAD), F32)
         for g in range(group):
             for head in range(kv_half // HEAD):
                 lanes = slice(head * HEAD, (head + 1) * HEAD)
                 k_hat, scale = key_stats(kv_ref[g, :size, lanes])
-                rot_ref[g, :size, lanes] = turn(k_hat * gk, cos_t, sin_t).astype(BF)
                 d_norm = turn(dkey_ref[g, :size, lanes].astype(F32), cos_t, -sin_t)
                 d_gain = d_gain + jnp.sum((d_norm * k_hat).reshape(size // 8, 8, HEAD), axis=0)
                 d_hat = d_norm * gk
                 d_raw = scale * (d_hat - k_hat * jnp.mean(k_hat * d_hat, axis=-1, keepdims=True))
-                dkv_ref[g, :size, lanes] = d_raw.astype(BF)
+                dk_ref[g, :size, lanes] = d_raw.astype(BF)
         dgk_ref[...] += d_gain
         d_query = stacked([jnp.dot(d_score[g * 16:(g + 1) * 16], rot_ref[g, :size, :], preferred_element_type=F32) for g in range(group)])
         dq_ref[...] = take_diag(d_query).reshape(group, 16, HEAD)
         if size < rows:
-            dkv_ref[:, size:, :] = jnp.zeros((group, rows - size, width), BF)
+            dk_ref[:, size:, :] = jnp.zeros((group, rows - size, kv_half), BF)
+            dv_ref[:, size:, :] = jnp.zeros((group, rows - size, kv_half), BF)
 
     variants(lens_ref[step * group + group - 1], sizes, run)
 
 
-def attn_bwd(lens, group, sizes, kv, prob, qbd, dobd, g_k, cos_t, sin_t):
+def attn_bwd(lens, group, sizes, kv, rot, prob, qbd, dobd, g_k, cos_t, sin_t):
     n_seq, rows, width = kv.shape
     once = dict(pipeline_mode=pl.Buffered(buffer_count=1))
     by_group = lambda *shape: pl.BlockSpec((group,) + shape, lambda i, l: (i,) + (0,) * len(shape))
@@ -225,50 +237,47 @@
         functools.partial(bwd_body, group, sizes),
         grid_spec=pltpu.PrefetchScalarGridSpec(
             num_scalar_prefetch=1, grid=(n_seq // group,),
-            in_specs=[by_group(rows, width), by_group(16, rows), by_group(16, width // 2), by_group(16, width // 2), whole(g_k), whole(cos_t), whole(sin_t)],
-            out_specs=[by_group(rows, width), by_group(16, HEAD), pl.BlockSpec((8, HEAD), lambda i, l: (0, 0))],
-            scratch_shapes=[pltpu.VMEM((group, rows, width // 2), BF)] * 2),
-        out_shape=[jax.ShapeDtypeStruct(kv.shape, BF), jax.ShapeDtypeStruct((n_seq, 16, HEAD), F32), jax.ShapeDtypeStruct((8, HEAD), F32)],
+            in_specs=[by_group(rows, width), by_group(rows, width // 2), by_group(16, rows), by_group(16, width // 2), by_group(16, width // 2), whole(g_k), whole(cos_t), whole(sin_t)],
+            out_specs=[by_group(rows, width // 2), by_group(rows, width // 2), by_group(16, HEAD), pl.BlockSpec((8, HEAD), lambda i, l: (0, 0))],
+            scratch_shapes=[pltpu.VMEM((group, rows, width // 2), BF)]),
+        out_shape=[jax.ShapeDtypeStruct((n_seq, rows, width // 2), BF)] * 2 + [jax.ShapeDtypeStruct((n_seq, 16, HEAD), F32), jax.ShapeDtypeStruct((8, HEAD), F32)],
         compiler_params=pltpu.CompilerParams(dimension_semantics=("arbitrary",), vmem_limit_bytes=VMEM),
         cost_estimate=pl.CostEstimate(flops=20 * 1000 * n_seq * rows * width // 8, bytes_accessed=n_seq * rows * width * 4, transcendentals=0),
         name="attn_bwd" + str(rows),
-    )(lens, kv, prob, qbd, dobd, g_k, cos_t, sin_t)
-
-
-def dx_body(group, sizes, order_ref, lens_ref, dkv_ref, dkv2_ref, wk_ref, wv_ref, wk2_ref, wv2_ref, h_ref, gin_ref, dxl_ref, dhm_ref, out_ref, dgin_ref, dx_ref):
+    )(lens, kv, rot, prob, qbd, dobd, g_k, cos_t, sin_t)
+
+
+def dx_body(group, n_seq, sizes, order_ref, lens_ref, dk_ref, dv_ref, dk2_ref, dv2_ref, wk_ref, wv_ref, wk2_ref, wv2_ref, h_ref, gin_ref, dxl_ref, dhm_ref, out_ref, dgin_ref, dx_ref):
     step = pl.program_id(0)
     rows, model = h_ref.shape[1], h_ref.shape[2]
-    kv_half = wk_ref.shape[1]
-    last = lens_ref[step] - 1
+    kv_half = dk_ref.shape[2]
     inner = lax.rem(step, group)
-    wide_cols = 512
+    turn_in = lax.rem(step // group, 2)
+    part_cols = model // group
+    wide_cols = min(part_cols, 512)
 
     @pl.when(step == 0)
     def _():
         dgin_ref[...] = jnp.zeros_like(dgin_ref)
 
-    def run(size):
-        @pl.when(inner == 0)
-        def _():
-            def project(d_ref, w_refs, add, j, carry):
-                cols = pl.ds(pl.multiple_of(j * wide_cols, wide_cols), wide_cols)
-                part = None
-                for half, w_ref in enumerate(w_refs):
-                    d_half = d_ref[:, :size, half * kv_half:(half + 1) * kv_half].reshape(group * size, kv_half)
-                    term = lax.dot_general(d_half, w_ref[cols, :], NT, preferred_element_type=F32)
-                    part = term if part is None else part + term
-                part = part.reshape(group, size, wide_cols)
-                dx_ref[:, :size, cols] = dx_ref[:, :size, cols] + part if add else part
-                return carry
-
-            lax.fori_loop(0, model // wide_cols, functools.partial(project, dkv_ref, (wk_ref, wv_ref), False), 0)
-            lax.fori_loop(0, model // wide_cols, functools.partial(project, dkv2_ref, (wk2_ref, wv2_ref), True), 0)
-
-        dx_ref[inner, pl.ds(last, 1), :] += dxl_ref[0]
+    def multiply(k_ref, v_ref, key_w, val_w, add, size):
+        for j in range(part_cols // wide_cols):
+            cols = pl.ds(pl.multiple_of(inner * part_cols + j * wide_cols, wide_cols), wide_cols)
+            d_keys = k_ref[:, :size, :].reshape(group * size, kv_half)
+            d_vals = v_ref[:, :size, :].reshape(group * size, kv_half)
+            part = lax.dot_general(d_keys, key_w[cols, :], NT, preferred_element_type=F32)
+            part = part + lax.dot_general(d_vals, val_w[cols, :], NT, preferred_element_type=F32)
+            part = part.reshape(group, size, wide_cols)
+            dx_ref[turn_in, :, :size, cols] = dx_ref[turn_in, :, :size, cols] + part if add else part
+
+    def finish(size):
+        slot = 1 - turn_in
+        last = lens_ref[step - group] - 1
+        dx_ref[slot, inner, pl.ds(last, 1), :] += dxl_ref[0]
         chunk = 32
         tiles = [slice(t, t + HEAD) for t in range(0, model, HEAD)]
 
-        def finish(c, carry):
+        def finish_chunk(c, carry):
             start = pl.multiple_of(c * chunk, chunk)
             here = pl.ds(start, chunk)
             at_last = lax.broadcasted_iota(jnp.int32, (chunk, HEAD), 0) + start == last
@@ -276,45 +285,50 @@
             for t in tiles:
                 hid = h_ref[0, here, t].astype(F32)
                 squares = squares + hid * hid
-                cross = cross + hid * (dx_ref[inner, here, t] * gin_ref[:, t])
+                cross = cross + hid * (dx_ref[slot, inner, here, t] * gin_ref[:, t])
             scale = lax.rsqrt(jnp.sum(squares, axis=-1, keepdims=True) / model + NORM_EPS)
             slope = scale * scale * scale * (jnp.sum(cross, axis=-1, keepdims=True) / model)
             for t in tiles:
                 hid = h_ref[0, here, t].astype(F32)
-                d_x = dx_ref[inner, here, t] * scale
+                d_x = dx_ref[slot, inner, here, t] * scale
                 dgin_ref[:, t] += jnp.sum((d_x * hid).reshape(chunk // 8, 8, HEAD), axis=0)
                 d_hid = d_x * gin_ref[:, t] - hid * slope
                 out_ref[0, here, t] = (d_hid + jnp.where(at_last, dhm_ref[0][:, t], 0.0)).astype(BF)
             return carry
 
-        lax.fori_loop(0, size // chunk, finish, 0)
+        lax.fori_loop(0, size // chunk, finish_chunk, 0)
         if size < out_ref.shape[1]:
             out_ref[0, size:, :] = jnp.zeros((out_ref.shape[1] - size, model), BF)
 
-    variants(lens_ref[step - inner + group - 1], sizes, run)
-
-
-def attn_dx(hid, order, lens, rows, group, sizes, dkv, dkv2, w_own, w_oth, g_in, d_xlast, d_hmid):
+    first = step - inner
+    longest = jnp.where(step < n_seq, lens_ref[jnp.minimum(first, n_seq - group) + group - 1], 0)
+    variants(longest, sizes, functools.partial(multiply, dk_ref, dv_ref, wk_ref, wv_ref, False))
+    variants(longest, sizes, functools.partial(multiply, dk2_ref, dv2_ref, wk2_ref, wv2_ref, True))
+    pl.when(step >= group)(lambda: variants(lens_ref[jnp.maximum(first - group, 0) + group - 1], sizes, finish))
+
+
+def attn_dx(hid, order, lens, rows, group, sizes, d_own, d_oth, w_own, w_oth, g_in, d_xlast, d_hmid):
     n_seq, seq_len, model = hid.shape
-    width = dkv.shape[-1]
+    width = 2 * w_own[0].shape[1]
+    weights = tuple(w_own) + tuple(w_oth)
     once = dict(pipeline_mode=pl.Buffered(buffer_count=1))
-    by_group = lambda *shape: pl.BlockSpec((group,) + shape, lambda i, o, l: (i // group,) + (0,) * len(shape))
+    of_group = pl.BlockSpec((group, rows, width // 2), lambda i, o, l: (jnp.minimum(i // group, n_seq // group - 1), 0, 0))
     whole = lambda arr: pl.BlockSpec(arr.shape, lambda i, o, l: (0,) * arr.ndim, **once)
-    one_row = pl.BlockSpec((1, 1, model), lambda i, o, l: (i, 0, 0))
-    weights = tuple(w_own) + tuple(w_oth)
+    late = lambda i: jnp.maximum(i - group, 0)
+    one_row = pl.BlockSpec((1, 1, model), lambda i, o, l: (late(i), 0, 0))
     return pl.pallas_call(
-        functools.partial(dx_body, group, sizes),
+        functools.partial(dx_body, group, n_seq, sizes),
         grid_spec=pltpu.PrefetchScalarGridSpec(
-            num_scalar_prefetch=2, grid=(n_seq,),
-            in_specs=[by_group(rows, width), by_group(rows, width)] + [whole(w) for w in weights] +
-                     [pl.BlockSpec((1, rows, model), lambda i, o, l: (o[i], 0, 0)), whole(g_in), one_row, one_row],
-            out_specs=[pl.BlockSpec((1, seq_len, model), lambda i, o, l: (o[i], 0, 0)), pl.BlockSpec((8, model), lambda i, o, l: (0, 0))],
-            scratch_shapes=[pltpu.VMEM((group, rows, model), F32)]),
+            num_scalar_prefetch=2, grid=(n_seq + group,),
+            in_specs=[of_group] * 4 + [whole(w) for w in weights] + [pl.BlockSpec((1, rows, model), lambda i, o, l: (o[late(i)], 0, 0)),
+                      whole(g_in), one_row, one_row],
+            out_specs=[pl.BlockSpec((1, seq_len, model), lambda i, o, l: (o[late(i)], 0, 0)), pl.BlockSpec((8, model), lambda i, o, l: (0, 0))],
+            scratch_shapes=[pltpu.VMEM((2, group, rows, model), F32)]),
         out_shape=[jax.ShapeDtypeStruct(hid.shape, BF), jax.ShapeDtypeStruct((8, model), F32)],
         compiler_params=pltpu.CompilerParams(dimension_semantics=("arbitrary",), vmem_limit_bytes=VMEM),
         cost_estimate=pl.CostEstimate(flops=4 * n_seq * rows * model * width, bytes_accessed=hid.size * 4, transcendentals=0),
         name="attn_dx" + str(rows),
-    )(order, lens, dkv, dkv2, *weights, hid, g_in, d_xlast[:, None, :], d_hmid[:, None, :])
+    )(order, lens, *d_own, *d_oth, *weights, hid, g_in, d_xlast[:, None, :], d_hmid[:, None, :])
 
 
 def wide(values):
@@ -382,8 +396,7 @@
         slab_rows = w_k.shape[0] // dp_size
         my_slab = lambda arr: lax.dynamic_slice_in_dim(arr, lax.axis_index('dp') * slab_rows, slab_rows, axis=0)
         slab = jnp.concatenate([my_slab(w_k), my_slab(w_v)], axis=1)
-        w_kv2 = narrow(lax.all_gather(swap_tp(wide(slab)), 'dp', axis=0, tiled=True), unit)
-        w_k2, w_v2 = w_kv2[:, :kv_half], w_kv2[:, kv_half:]
+        slab2 = swap_tp(wide(slab))
 
         h_last = jnp.concatenate([hid_q[order_q, lens_q - 1], hid_d[order_d, len_d - 1]], axis=0).astype(F32)
         x_last = norm_rows(h_last, g_in).astype(BF)
@@ -396,20 +409,26 @@
         cos_t, sin_t = rope_tables(jnp.arange(seq_len))
         cos_q, sin_q = cos_t[:Q_MAX], sin_t[:Q_MAX]
         gin_row, gk_row = g_in[None, :], g_k[None, :]
-        x_q, kv_q, p_q, o_q = attn_fwd(hid_q, order_q, lens_q, Q_MAX, 4, Q_SIZES, w_k, w_v, qbd[:n_q], gk_row, cos_q, sin_q, gin_row)
-        x_d, kv_d, p_d, o_d = attn_fwd(hid_d, order_d, len_d, seq_len, 1, D_SIZES, w_k, w_v, qbd[n_q:], gk_row, cos_t, sin_t, gin_row)
+        x_d, kv_d, p_d, o_d, rot_d = attn_fwd(hid_d, order_d, len_d, seq_len, 1, D_SIZES, w_k, w_v, qbd[n_q:], gk_row, cos_t, sin_t, gin_row)
+        slab2, x_d = lax.optimization_barrier((slab2, x_d))
+        w_kv2 = lax.all_gather(slab2, 'dp', axis=0, tiled=True)
+        x_q, kv_q, p_q, o_q, rot_q = attn_fwd(hid_q, order_q, lens_q, Q_MAX, 4, Q_SIZES, w_k, w_v, qbd[:n_q], gk_row, cos_q, sin_q, gin_row)
         attn_out = jnp.concatenate([o_q, o_d], axis=0)[:, :q_rot.shape[1]].astype(BF).reshape(n_q + n_d, -1)
-        attn_out, w_k2, w_v2 = lax.optimization_barrier((attn_out, w_k2, w_v2))
 
         h_mid = h_last + psum_tp(dot(attn_out, w_o))
         y_norm = norm_rows(h_mid, g_post).astype(BF)
         width = h_last.shape[1]
-        gather = lambda arr: narrow(lax.all_gather(wide(arr), 'dp', axis=0, tiled=True), unit)
-        early = gather(jnp.concatenate([x_last, y_norm, attn_out], axis=1))
+        pad_rows = -(n_q + n_d) % 8
+        gather = lambda arr: narrow(lax.all_gather(wide(jnp.pad(arr, ((0, pad_rows), (0, 0)))), 'dp', axis=0, tiled=True), unit)
+        y_norm, w_kv2 = lax.optimization_barrier((y_norm, w_kv2))
+        w_kv2 = narrow(w_kv2, unit)
+        w_k2, w_v2 = w_kv2[:, :kv_half], w_kv2[:, kv_half:]
         gate_val = dot(y_norm, w_gate).astype(BF)
         up_val = dot(y_norm, w_up).astype(BF)
         hidden_act, act_pull = jax.vjp(swiglu, gate_val.astype(F32), up_val.astype(F32))
-        h_out = h_mid + psum_tp(dot(hidden_act.astype(BF), w_down))
+        hidden_act = hidden_act.astype(BF)
+        early = gather(jnp.concatenate([x_last, y_norm, attn_out, hidden_act], axis=1))
+        h_out = h_mid + psum_tp(dot(hidden_act, w_down))
         emb, head_pull = jax.vjp(final_head, h_out, g_final)
         emb_q, emb_d = emb[:n_q], emb[n_q:]
 
@@ -428,52 +447,54 @@
         d_hout, d_gfinal = head_pull(jnp.concatenate([d_emb_q, d_emb_d], axis=0))
         d_hout_b = d_hout.astype(BF)
         d_act = dot_nt(d_hout_b, w_down).astype(BF)
-        d_gate, d_up = act_pull(d_act.astype(F32))
-        d_y = psum_tp(dot_nt(d_gate.astype(BF), w_gate) + dot_nt(d_up.astype(BF), w_up))
+        d_gate, d_up = (d_in.astype(BF) for d_in in act_pull(d_act.astype(F32)))
+        d_y = psum_tp(dot_nt(d_gate, w_gate) + dot_nt(d_up, w_up))
         d_ymid, d_gpost = norm_back(h_mid, g_post, d_y)
         d_hmid = d_hout + d_ymid
         d_hmid_b = d_hmid.astype(BF)
         d_hmid_b, early = lax.optimization_barrier((d_hmid_b, early))
-        d_both = gather(jnp.concatenate([d_hout_b, d_hmid_b], axis=1))
+        d_both = gather(jnp.concatenate([d_hout_b, d_hmid_b, d_gate, d_up], axis=1))
         d_attn = dot_nt(d_hmid_b, w_o).astype(BF).reshape(q_rot.shape)
         d_attn2 = narrow(swap_tp(wide(d_attn)), unit)
         dobd, dobd2 = block_diag(d_attn), block_diag(d_attn2)
 
-        dkv_q, dq_q, dgk_q = attn_bwd(lens_q, 4, Q_SIZES, kv_q, p_q, qbd[:n_q], dobd[:n_q], gk_row, cos_q, sin_q)
-        dkv_d, dq_d, dgk_d = attn_bwd(len_d, 1, D_SIZES, kv_d, p_d, qbd[n_q:], dobd[n_q:], gk_row, cos_t, sin_t)
+        dk_q, dv_q, dq_q, dgk_q = attn_bwd(lens_q, 4, Q_SIZES, kv_q, rot_q, p_q, qbd[:n_q], dobd[:n_q], gk_row, cos_q, sin_q)
+        dk_d, dv_d, dq_d, dgk_d = attn_bwd(len_d, 1, D_SIZES, kv_d, rot_d, p_d, qbd[n_q:], dobd[n_q:], gk_row, cos_t, sin_t)
         d_qrot = jnp.concatenate([dq_q, dq_d], axis=0)[:, :q_rot.shape[1]].astype(BF)
-        d_qrot, d_both = lax.optimization_barrier((d_qrot, d_both))
         d_qraw, d_gq = q_pull(d_qrot)
         d_xlast = psum_tp(dot_nt(d_qraw, w_q))
+        flat = lambda arr: arr.reshape(-1, arr.shape[-1])
+        d_wk = dot_tn(flat(x_q), flat(dk_q)) + dot_tn(flat(x_d), flat(dk_d))
+        d_wv = dot_tn(flat(x_q), flat(dv_q)) + dot_tn(flat(x_d), flat(dv_d))
+        d_wk, d_wv, d_both = lax.optimization_barrier((d_wk, d_wv, d_both))
+        d_wk, d_wv = lax.psum((d_wk, d_wv), 'dp')
+
+        kv2_q, p2_q, _, rot2_q = attn_fwd(x_q, order_q, lens_q, Q_MAX, 4, Q_SIZES, w_k2, w_v2, qbd2[:n_q], gk_row, cos_q, sin_q)
+        kv2_d, p2_d, _, rot2_d = attn_fwd(x_d, order_d, len_d, seq_len, 1, D_SIZES, w_k2, w_v2, qbd2[n_q:], gk_row, cos_t, sin_t)
+        dk2_q, dv2_q, _, _ = attn_bwd(lens_q, 4, Q_SIZES, kv2_q, rot2_q, p2_q, qbd2[:n_q], dobd2[:n_q], gk_row, cos_q, sin_q)
+        dk2_d, dv2_d, _, _ = attn_bwd(len_d, 1, D_SIZES, kv2_d, rot2_d, p2_d, qbd2[n_q:], dobd2[n_q:], gk_row, cos_t, sin_t)
+        d_hid_q, dgin_q = attn_dx(hid_q, order_q, lens_q, Q_MAX, 4, Q_SIZES, (dk_q, dv_q), (dk2_q, dv2_q), (w_k, w_v), (w_k2, w_v2), gin_row, d_xlast[:n_q], d_hmid[:n_q])
+        d_hid_d, dgin_d = attn_dx(hid_d, order_d, len_d, seq_len, 1, D_SIZES, (dk_d, dv_d), (dk2_d, dv2_d), (w_k, w_v), (w_k2, w_v2), gin_row, d_xlast[n_q:], d_hmid[n_q:])
+
+        d_qraw, d_wk, d_wv, dgin_q = lax.optimization_barrier((d_qraw, d_wk, d_wv, dgin_q))
         d_qraw_all = gather(d_qraw)
-        flat = lambda arr: arr.reshape(-1, arr.shape[-1])
-        d_wkv = dot_tn(flat(x_q), flat(dkv_q)) + dot_tn(flat(x_d), flat(dkv_d))
-        d_wkv, d_qraw_all = lax.optimization_barrier((d_wkv, d_qraw_all))
-        d_wkv = lax.psum(d_wkv, 'dp')
-
-        kv2_q, p2_q, _ = attn_fwd(x_q, order_q, lens_q, Q_MAX, 4, Q_SIZES, w_k2, w_v2, qbd2[:n_q], gk_row, cos_q, sin_q)
-        kv2_d, p2_d, _ = attn_fwd(x_d, order_d, len_d, seq_len, 1, D_SIZES, w_k2, w_v2, qbd2[n_q:], gk_row, cos_t, sin_t)
-        dkv2_q, _, _ = attn_bwd(lens_q, 4, Q_SIZES, kv2_q, p2_q, qbd2[:n_q], dobd2[:n_q], gk_row, cos_q, sin_q)
-        dkv2_d, _, _ = attn_bwd(len_d, 1, D_SIZES, kv2_d, p2_d, qbd2[n_q:], dobd2[n_q:], gk_row, cos_t, sin_t)
-        d_hid_q, dgin_q = attn_dx(hid_q, order_q, lens_q, Q_MAX, 4, Q_SIZES, dkv_q, dkv2_q, (w_k, w_v), (w_k2, w_v2), gin_row, d_xlast[:n_q], d_hmid[:n_q])
-        d_hid_d, dgin_d = attn_dx(hid_d, order_d, len_d, seq_len, 1, D_SIZES, dkv_d, dkv2_d, (w_k, w_v), (w_k2, w_v2), gin_row, d_xlast[n_q:], d_hmid[n_q:])
-
-        x_last_all, y_all, attn_all = early[:, :width], early[:, width:2 * width], early[:, 2 * width:]
-        d_hout_all, d_hmid_all = d_both[:, :width], d_both[:, width:]
-        act_all, act_all_pull = jax.vjp(swiglu, dot(y_all, w_gate).astype(BF).astype(F32), dot(y_all, w_up).astype(BF).astype(F32))
-        d_gate_all, d_up_all = act_all_pull(dot_nt(d_hout_all, w_down).astype(BF).astype(F32))
-        d_wdown = dot_tn(act_all.astype(BF), d_hout_all)
-        d_wgate = dot_tn(y_all, d_gate_all.astype(BF))
-        d_wup = dot_tn(y_all, d_up_all.astype(BF))
+        kv_width = attn_out.shape[1]
+        x_last_all, y_all = early[:, :width], early[:, width:2 * width]
+        attn_all, act_all = early[:, 2 * width:2 * width + kv_width], early[:, 2 * width + kv_width:]
+        d_hout_all, d_hmid_all = d_both[:, :width], d_both[:, width:2 * width]
+        d_gate_all, d_up_all = jnp.split(d_both[:, 2 * width:], 2, axis=1)
+        d_wdown = dot_tn(act_all, d_hout_all)
+        d_wgate = dot_tn(y_all, d_gate_all)
+        d_wup = dot_tn(y_all, d_up_all)
         d_wo = dot_tn(attn_all, d_hmid_all)
         d_wq = dot_tn(x_last_all, d_qraw_all)
 
         dp_sum = lambda vec: jnp.sum(lax.all_gather(vec, 'dp', axis=0), axis=0)
         d_heads = psum_tp(jnp.concatenate([d_gq, jnp.sum(dgk_q + dgk_d, axis=0)]))
-        gains = dp_sum(jnp.concatenate([d_gpost, d_gfinal, d_heads]))
-        d_gpost, d_gfinal, d_gq, d_gk = gains[:width], gains[width:2 * width], gains[2 * width:2 * width + HEAD], gains[2 * width + HEAD:]
-        d_gin = dp_sum(jnp.sum(dgin_q + dgin_d, axis=0))
-        return (loss_rows, d_hid_q, d_hid_d, d_wq, d_wkv[:, :kv_half], d_wkv[:, kv_half:], d_wo, d_wgate, d_wup, d_wdown,
+        gains = dp_sum(jnp.concatenate([d_gpost, d_gfinal, jnp.sum(dgin_q + dgin_d, axis=0), d_heads]))
+        d_gpost, d_gfinal, d_gin, d_heads = jnp.split(gains, (width, 2 * width, 3 * width))
+        d_gq, d_gk = d_heads[:HEAD], d_heads[HEAD:]
+        return (loss_rows, d_hid_q, d_hid_d, d_wq, d_wk, d_wv, d_wo, d_wgate, d_wup, d_wdown,
                 d_gin, d_gq, d_gk, d_gpost, d_gfinal)
 
     col_split = P(None, 'tp')

time: 615 us -> 531 us (0.86)
  Pallas kernels: 262 us -> 217 us
  waiting for transfers between devices: 58.4 us -> 37.5 us
  local copies, waits for them, and re-layouts: 38.5 us -> 26.5 us
  blocking collectives: 28.8 us -> 21 us
    pallas_call x2, Pallas kernels: 116 us -> 94.5 us  [attn_dx(): pl.pallas_call(functools.partial(dx_body, group, n_seq, sizes), grid_spec...]
    pallas_call x4, Pallas kernels: 60.8 us -> 44.5 us  [attn_bwd(): pl.pallas_call(functools.partial(bwd_body, group, sizes), grid_spec=pltpu...]
    dot_general x7 -> x9, matrix products: 81 us -> 96.4 us  [dot_tn(): return lax.dot_general(a, b, TN, preferred_element_type=F32)]
    ppermute x8, waiting for transfers between devices: 42.3 us -> 30.3 us  [swap_tp(): return lax.ppermute(values, 'tp', SWAP)]
    dot_general x7 -> x5, matrix products: 38.6 us -> 26.6 us  [dot(): return jnp.dot(a, b, preferred_element_type=F32)]
    psum x1, waiting for transfers between devices: 9.85 us -> 0.01 us  [device_step(): d_wk, d_wv = lax.psum((d_wk, d_wv), 'dp')]
    slice x3 -> x1, local copies, waits for them, and re-layouts: 8.96 us -> 0.52 us  [device_step(): d_gq, d_gk = (d_heads[:HEAD], d_heads[HEAD:])]
    dot_general x6 -> x5, matrix products: 34.3 us -> 26 us  [dot_nt(): return lax.dot_general(a, b, NT, preferred_element_type=F32)]
  transfers between devices with their start and end apart: 14 -> 14, of which waited for: 7 -> 7; matrix products, arithmetic and copies ran while one was open for 18% -> 32% of each run, Pallas kernels for 43% -> 42%
where the time goes in v3:
time: 531 us; the launch traced here: 522 us
  Pallas kernels  217 us (41%)
  matrix products  150 us (28%)
  other arithmetic  38.8 us (7%)
  waiting for transfers between devices  37.5 us (7%)
  local copies, waits for them, and re-layouts  26.5 us (5%)
  blocking collectives  21 us (4%)
  starting transfers between devices  16.2 us (3%)
  between operations  14.9 us (3%)
    dot_general x9, matrix products, dot_tn(): return lax.dot_general(a, b, TN, preferred_element_type=F32)  96.4 us
    pallas_call x2, Pallas kernels, attn_dx(): pl.pallas_call(functools.partial(dx_body, group, n_seq, sizes), grid_spec...  94.5 us
    pallas_call x4, Pallas kernels, attn_fwd(): pl.pallas_call(functools.partial(fwd_body, do_norm, group, sizes), grid_s...  77.9 us
    pallas_call x4, Pallas kernels, attn_bwd(): pl.pallas_call(functools.partial(bwd_body, group, sizes), grid_spec=pltpu...  44.5 us
    ppermute x8, waiting for transfers between devices, swap_tp(): return lax.ppermute(values, 'tp', SWAP)  30.3 us
    dot_general x5, matrix products, dot(): return jnp.dot(a, b, preferred_element_type=F32)  26.6 us
    dot_general x5, matrix products, dot_nt(): return lax.dot_general(a, b, NT, preferred_element_type=F32)  26 us
    convert_element_type x5, other arithmetic, narrow(): return (values * unit).astype(BF)  20.5 us
  transfers between devices with their start and end apart: 14, of which 7 were waited for; matrix products, arithmetic and copies ran while one was open for 32% of the time, Pallas kernels for 42%

profile of v3, /device:TPU:0, one launch (start us, length us, event | category | flops | bytes accessed | tf_op | source)
XLA Modules:
  0.0 521.8 jit_solution(13236228724065185947)
XLA Ops:
  7.2 1.1 constant_dynamic-slice_fusion
  8.4 3.3 collective-permute-start.1
  11.8 0.9 convert_reduce_fusion
  15.0 1.7 gather_fusion
  16.7 1.5 gather_fusion.1
  19.1 3.1 fusion.24
  23.9 1.0 fusion.51
  24.9 1.0 pad_maximum_fusion.1
  26.9 11.9 %attn_fwd_norm512.1 = (bf16[2,512,2048]{2,1,0:T(8,128)(2,1)}, bf16[2,512,1024]{2,1,0:T(8,128)(2,1)}, f32[2,16,512]{2,1,0:T(8,128)}, f32[2,16,128]{2,1,0:T(8,128)}, bf16[2,512,512]{2,1,0:T(8,128)(2,1)}) custom-call(s32[2]{0:T(128)} %iota.137.order_ref, s32[2]{0:T(128)} %lens_ref.9, bf16[2,512,2048]{2,1,0:T(8,128)(2,1)} %h_ref.3, f32[1,2048]{1,0:T(1,128)} %bitcast.109, ...), custom_call_target="tpu_custom_call" | custom-call | flops 4294967296 | bytes 8388608 | tf_op jit(solution)/shard_map/attn_fwd_norm512/pallas_call | solution.py:178
  41.1 34.6 %attn_fwd_norm128.1 = (bf16[32,128,2048]{2,1,0:T(8,128)(2,1)}, bf16[32,128,1024]{2,1,0:T(8,128)(2,1)}, f32[32,16,128]{2,1,0:T(8,128)}, f32[32,16,128]{2,1,0:T(8,128)}, bf16[32,128,512]{2,1,0:T(8,128)(2,1)}) custom-call(s32[32]{0:T(128)} %copy-done.15, s32[32]{0:T(128)} %copy-done.14, bf16[32,512,2048]{2,1,0:T(8,128)(2,1)} %h_ref.2, ...), custom_call_target="tpu_custom_call" | custom-call | flops 17179869184 | bytes 33554432 | tf_op jit(solution)/shard_map/attn_fwd_norm128/pallas_call | solution.py:178
  75.7 1.0 convert.16
  76.7 3.0 fusion.93
  79.8 8.7 %collective-permute-done = f32[34,2048]{1,0:T(8,128)S(1)} collective-permute-done((f32[34,2048]{1,0:T(8,128)S(1)}, f32[34,2048]{1,0:T(8,128)S(1)}, u32[]{:S(2)}, u32[]{:S(2)}) %collective-permute-start) | collective-permute-done | bytes 278560 | tf_op jit(solution)/shard_map/ppermute | solution.py:343
  89.6 6.8 %fusion.2 = f32[34,3072]{1,0:T(8,128)S(1)} fusion(bf16[34,2048]{1,0:T(8,128)(2,1)S(1)} %multiply_convert_fusion.7, bf16[2048,3072]{1,0:T(8,128)(2,1)} %param.26), kind=kOutput, calls=%fused_computation.12 | convolution fusion | flops 428027904 | bytes 13139968 | tf_op jit(solution)/shard_map/dot_general | solution.py:360
  96.5 6.9 %multiply_convert_fusion.6 = (bf16[34,3072]{1,0:T(8,128)(2,1)S(1)}, f32[34,3072]{1,0:T(8,128)S(1)}) fusion(f32[34,3072]{1,0:T(8,128)S(1)} %fusion.2, bf16[34,2048]{1,0:T(8,128)(2,1)S(1)} %multiply_convert_fusion.7, bf16[2048,3072]{1,0:T(8,128)(2,1)} %param.27), kind=kOutput, calls=%fused_computation.68 | convolution fusion | flops 428654592 | bytes 13766656 | tf_op jit(solution)/shard_map/dot_general | solution.py:360
  103.3 1.1 fusion.32
  104.5 6.8 %fusion.94 = f32[34,2048]{1,0:T(8,128)S(1)} fusion(bf16[34,3072]{1,0:T(8,128)(2,1)S(1)} %get-tuple-element.158, bf16[3072,2048]{1,0:T(8,128)(2,1)} %param.28), kind=kOutput, calls=%fused_computation.220 | convolution fusion | flops 427819008 | bytes 13070336 | tf_op jit(solution)/shard_map/dot_general | solution.py:360
  111.4 1.5 collective-permute-start.2
  112.9 9.0 %collective-permute-done.2 = f32[34,2048]{1,0:T(8,128)S(1)} collective-permute-done((f32[34,2048]{1,0:T(8,128)S(1)}, f32[34,2048]{1,0:T(8,128)S(1)}, u32[]{:S(2)}, u32[]{:S(2)}) %collective-permute-start.2) | collective-permute-done | bytes 278560 | tf_op jit(solution)/shard_map/ppermute | solution.py:343
  122.4 8.7 %all-gather.1 = f32[8,2,2048]{2,1,0:T(2,128)S(1)} all-gather(f32[1,2,2048]{2,1,0:T(2,128)S(1)} %slice_bitcast_fusion.2), channel_id=1, replica_groups=mesh['tp'=2,'dp'=8] {'dp'}, dimensions={0}, use_global_device_ids=true | all-gather | bytes 147456 | tf_op jit(solution)/shard_map/all_gather | solution.py:435
  132.6 3.4 all-to-all-start
  136.7 6.3 %all-to-all-done = f32[8,2,2048]{2,1,0:T(2,128)S(1)} async-done(((f32[8,2,2048]{2,1,0:T(2,128)}), f32[8,2,2048]{2,1,0:T(2,128)S(1)}, u32[]{:S(2)}, u32[]{:S(2)}) %all-to-all-start) | async-done | bytes 131104 | tf_op jit(solution)/shard_map/all_to_all | solution.py:444
  144.3 8.6 %multiply_convert_fusion.5 = (bf16[34,3072]{1,0:T(8,128)(2,1)S(1)}, bf16[34,3072]{1,0:T(8,128)(2,1)S(1)}) fusion(f32[34,3072]{1,0:T(8,128)S(1)} %fusion.2, f32[34,3072]{1,0:T(8,128)S(1)} %get-tuple-element.159, bf16[34,2048]{1,0:T(8,128)(2,1)S(1)} %get-tuple-element.123, bf16[3072,2048]{1,0:T(8,128)(2,1)} %param.28), kind=kOutput, calls=%fused_computation.65 | convolution fusion | flops 429490176 | bytes 13975552 | tf_op jit(solution)/shard_map/dot_general | solution.py:364
  153.0 8.6 %fusion.95 = f32[34,2048]{1,0:T(8,128)S(1)} fusion(bf16[34,3072]{1,0:T(8,128)(2,1)S(1)} %get-tuple-element.134, bf16[2048,3072]{1,0:T(8,128)(2,1)} %param.26), kind=kOutput, calls=%fused_computation.221 | convolution fusion | flops 427819008 | bytes 13070336 | tf_op jit(solution)/shard_map/dot_general | solution.py:364
  161.6 3.9 convolution_add_fusion
  165.5 1.5 collective-permute-start.3
  167.1 7.0 %collective-permute-done.3 = f32[34,2048]{1,0:T(8,128)S(1)} collective-permute-done((f32[34,2048]{1,0:T(8,128)S(1)}, f32[34,2048]{1,0:T(8,128)S(1)}, u32[]{:S(2)}, u32[]{:S(2)}) %collective-permute-start.3) | collective-permute-done | bytes 278560 | tf_op jit(solution)/shard_map/ppermute | solution.py:343
  175.0 7.2 %multiply_convert_fusion.1 = bf16[320,8192]{1,0:T(8,128)(2,1)} fusion(f32[320,8192]{1,0:T(8,128)} %all-gather.10.cloned.1.call-done, f32[]{:T(128)} %bitcast.11), kind=kLoop, calls=%fused_computation.3 | loop fusion | flops 5242880 | bytes 15728644 | tf_op jit(solution)/shard_map/convert_element_type | solution.py:339
  182.2 1.3 fusion.28
  184.0 1.5 collective-permute-start.4
  185.5 3.6 collective-permute-done.4
  189.1 4.6 multiply_convert_fusion.2
  193.7 2.4 fusion.87
  197.4 1.4 convolution_convert_fusion.3
  198.8 1.5 collective-permute-start.5
  200.4 1.0 copy.63.dhm_ref
  202.0 2.0 collective-permute-done.5
  204.6 6.0 %attn_bwd512.2 = (bf16[2,512,512]{2,1,0:T(8,128)(2,1)}, bf16[2,512,512]{2,1,0:T(8,128)(2,1)}, f32[2,16,128]{2,1,0:T(8,128)}, f32[8,128]{1,0:T(8,128)}) custom-call(s32[2]{0:T(128)} %lens_ref.9, bf16[2,512,1024]{2,1,0:T(8,128)(2,1)} %get-tuple-element.79.kv_ref, bf16[2,512,512]{2,1,0:T(8,128)(2,1)} %get-tuple-element.80.rot_ref, ...), custom_call_target="tpu_custom_call" | custom-call | flops 2621440000 | bytes 4194304 | tf_op jit(solution)/shard_map/attn_bwd512/pallas_call | solution.py:236
  212.2 16.0 %attn_bwd128.2 = (bf16[32,128,512]{2,1,0:T(8,128)(2,1)}, bf16[32,128,512]{2,1,0:T(8,128)(2,1)}, f32[32,16,128]{2,1,0:T(8,128)}, f32[8,128]{1,0:T(8,128)}) custom-call(s32[32]{0:T(128)} %copy-done.14, bf16[32,128,1024]{2,1,0:T(8,128)(2,1)} %get-tuple-element.65.kv_ref, bf16[32,128,512]{2,1,0:T(8,128)(2,1)} %get-tuple-element.66.rot_ref, ...), custom_call_target="tpu_custom_call" | custom-call | flops 10485760000 | bytes 16777216 | tf_op jit(solution)/shard_map/attn_bwd128/pallas_call | solution.py:236
  228.3 1.0 convert.18
  229.9 3.5 fusion.96
  233.5 1.5 collective-permute-start.6
  237.7 0.9 pad_slice_fusion.1.dobd_ref
  239.1 8.9 %attn_fwd512.1 = (bf16[2,512,1024]{2,1,0:T(8,128)(2,1)}, f32[2,16,512]{2,1,0:T(8,128)}, f32[2,16,128]{2,1,0:T(8,128)}, bf16[2,512,512]{2,1,0:T(8,128)(2,1)}) custom-call(s32[2]{0:T(128)} %iota.139.order_ref, s32[2]{0:T(128)} %lens_ref.9, bf16[2,512,2048]{2,1,0:T(8,128)(2,1)} %get-tuple-element.86.refs_0_, ...), custom_call_target="tpu_custom_call" | custom-call | flops 4294967296 | bytes 8388608 | tf_op jit(solution)/shard_map/attn_fwd512/pallas_call | solution.py:178
  248.1 13.9 %fusion.98 = f32[2048,512,1]{1,0,2:T(8,128)S(1)} fusion(bf16[32,128,2048]{2,1,0:T(8,128)(2,1)} %get-tuple-element.71.refs_0_, bf16[32,128,512]{2,1,0:T(8,128)(2,1)} %get-tuple-element.70.dv_ref), kind=kOutput, calls=%fused_computation.224 | convolution fusion | flops 8589934592 | bytes 25165824 | tf_op jit(solution)/shard_map/dot_general | solution.py:368
  262.0 4.6 bitcast_add_fusion
  266.6 16.2 %fusion.97 = f32[2048,512,1]{1,0,2:T(8,128)S(1)} fusion(bf16[32,128,2048]{2,1,0:T(8,128)(2,1)S(1)} %bitcast.114, bf16[32,128,512]{2,1,0:T(8,128)(2,1)} %get-tuple-element.69.dk_ref), kind=kOutput, calls=%fused_computation.223 | convolution fusion | flops 8589934592 | bytes 25165824 | tf_op jit(solution)/shard_map/dot_general | solution.py:368
  282.8 4.5 bitcast_add_fusion.1
  287.3 22.5 %attn_fwd128.1 = (bf16[32,128,1024]{2,1,0:T(8,128)(2,1)}, f32[32,16,128]{2,1,0:T(8,128)}, f32[32,16,128]{2,1,0:T(8,128)}, bf16[32,128,512]{2,1,0:T(8,128)(2,1)}) custom-call(s32[32]{0:T(128)} %copy-done.15, s32[32]{0:T(128)} %copy-done.14, bf16[32,128,2048]{2,1,0:T(8,128)(2,1)} %get-tuple-element.71.refs_0_, ...), custom_call_target="tpu_custom_call" | custom-call | flops 17179869184 | bytes 33554432 | tf_op jit(solution)/shard_map/attn_fwd128/pallas_call | solution.py:178
  309.8 16.0 %attn_bwd128.3 = (bf16[32,128,512]{2,1,0:T(8,128)(2,1)}, bf16[32,128,512]{2,1,0:T(8,128)(2,1)}, f32[32,16,128]{2,1,0:T(8,128)}, f32[8,128]{1,0:T(8,128)}) custom-call(s32[32]{0:T(128)} %copy-done.14, bf16[32,128,1024]{2,1,0:T(8,128)(2,1)} %get-tuple-element.73.kv_ref, bf16[32,128,512]{2,1,0:T(8,128)(2,1)} %get-tuple-element.74.rot_ref, ...), custom_call_target="tpu_custom_call" | custom-call | flops 10485760000 | bytes 16777216 | tf_op jit(solution)/shard_map/attn_bwd128/pallas_call | solution.py:236
  325.8 6.4 %attn_bwd512.3 = (bf16[2,512,512]{2,1,0:T(8,128)(2,1)}, bf16[2,512,512]{2,1,0:T(8,128)(2,1)}, f32[2,16,128]{2,1,0:T(8,128)}, f32[8,128]{1,0:T(8,128)}) custom-call(s32[2]{0:T(128)} %lens_ref.9, bf16[2,512,1024]{2,1,0:T(8,128)(2,1)} %get-tuple-element.87.kv_ref, bf16[2,512,512]{2,1,0:T(8,128)(2,1)} %get-tuple-element.88.rot_ref, ...), custom_call_target="tpu_custom_call" | custom-call | flops 2621440000 | bytes 4194304 | tf_op jit(solution)/shard_map/attn_bwd512/pallas_call | solution.py:236
  332.3 1.0 copy.62.dxl_ref
  333.3 8.6 %multiply_convert_fusion = bf16[320,10240]{1,0:T(8,128)(2,1)} fusion(f32[320,10240]{1,0:T(8,128)} %all-gather.12.cloned.1.call-done, f32[]{:T(128)} %bitcast.11), kind=kLoop, calls=%fused_computation.2 | loop fusion | flops 6553600 | bytes 19660804 | tf_op jit(solution)/shard_map/convert_element_type | solution.py:339
  342.0 75.1 %attn_dx128.1 = (bf16[32,512,2048]{2,1,0:T(8,128)(2,1)}, f32[8,2048]{1,0:T(8,128)}) custom-call(s32[32]{0:T(128)} %copy-done.15, s32[32]{0:T(128)} %copy-done.14, bf16[32,128,512]{2,1,0:T(8,128)(2,1)} %get-tuple-element.69.dk_ref, bf16[32,128,512]{2,1,0:T(8,128)(2,1)} %get-tuple-element.70.dv_ref, bf16[32,128,512]{2,1,0:T(8,128)(2,1)} %get-tuple-element.76.dk2_ref, ...), custom_call_target="tpu_custom_call" | custom-call | flops 34359738368 | bytes 134217728 | tf_op jit(solution)/shard_map/attn_dx128/pallas_call | solution.py:319
  418.2 19.4 %attn_dx512.1 = (bf16[2,512,2048]{2,1,0:T(8,128)(2,1)}, f32[8,2048]{1,0:T(8,128)}) custom-call(s32[2]{0:T(128)} %iota.138.order_ref, s32[2]{0:T(128)} %lens_ref.9, bf16[2,512,512]{2,1,0:T(8,128)(2,1)} %get-tuple-element.84.dk_ref, bf16[2,512,512]{2,1,0:T(8,128)(2,1)} %get-tuple-element.85.dv_ref, bf16[2,512,512]{2,1,0:T(8,128)(2,1)} %get-tuple-element.90.dk2_ref, ...), custom_call_target="tpu_custom_call" | custom-call | flops 8589934592 | bytes 8388608 | tf_op jit(solution)/shard_map/attn_dx512/pallas_call | solution.py:319
  437.6 14.2 %fusion.5 = f32[2048,3072]{1,0:T(8,128)} fusion(bf16[320,10240]{1,0:T(8,128)(2,1)} %multiply_convert_fusion, bf16[320,8192]{1,0:T(8,128)(2,1)} %multiply_convert_fusion.1), kind=kOutput, calls=%fused_computation.16 | convolution fusion | flops 4026531840 | bytes 28442624 | tf_op jit(solution)/shard_map/dot_general | solution.py:368
  451.9 14.0 %fusion.7 = f32[2048,3072]{1,0:T(8,128)} fusion(bf16[320,10240]{1,0:T(8,128)(2,1)} %multiply_convert_fusion, bf16[320,8192]{1,0:T(8,128)(2,1)} %multiply_convert_fusion.1), kind=kOutput, calls=%fused_computation.18 | convolution fusion | flops 4026531840 | bytes 28442624 | tf_op jit(solution)/shard_map/dot_general | solution.py:368
  466.6 7.3 %fusion.18 = f32[1024,2048]{1,0:T(8,128)} fusion(bf16[320,10240]{1,0:T(8,128)(2,1)} %multiply_convert_fusion, bf16[320,8192]{1,0:T(8,128)(2,1)} %multiply_convert_fusion.1), kind=kOutput, calls=%fused_computation.31 | convolution fusion | flops 1342177280 | bytes 10354688 | tf_op jit(solution)/shard_map/dot_general | solution.py:368
  473.9 14.0 %fusion.3 = f32[3072,2048]{1,0:T(8,128)} fusion(bf16[320,8192]{1,0:T(8,128)(2,1)} %multiply_convert_fusion.1, bf16[320,10240]{1,0:T(8,128)(2,1)} %multiply_convert_fusion), kind=kOutput, calls=%fused_computation.14 | convolution fusion | flops 4026531840 | bytes 28442624 | tf_op jit(solution)/shard_map/dot_general | solution.py:368
  488.0 12.3 %all-gather.2 = f32[8,1,6400]{2,1,0:T(1,128)S(1)} all-gather(f32[1,1,6400]{2,1,0:T(1,128)S(1)} %reshape.361), channel_id=2, replica_groups=mesh['tp'=2,'dp'=8] {'dp'}, dimensions={0}, use_global_device_ids=true | all-gather | bytes 230400 | tf_op jit(solution)/shard_map/all_gather | solution.py:492
  501.6 7.7 %fusion.20 = f32[2048,1024]{1,0:T(8,128)} fusion(bf16[320,8192]{1,0:T(8,128)(2,1)} %multiply_convert_fusion.1, f32[320,1024]{1,0:T(8,128)} %all-gather.14.cloned.1.call-done, f32[]{:T(128)} %bitcast.11), kind=kOutput, calls=%fused_computation.34 | convolution fusion | flops 1342832640 | bytes 11010560 | tf_op jit(solution)/shard_map/dot_general | solution.py:368
  509.3 2.1 copy.78
  511.4 1.6 copy-done.1
  513.0 2.0 copy.79
  (183 shorter events, 26.3 us)
Async XLA Ops:
  7.2 82.5 %all-gather.8.cloned.1.call-start = ((), (), s32[]{:S(2)}) async-start(), calls=%async_computation.1 | async-start | bytes 9437184 | tf_op jit(solution)/shard_map/all_gather | solution.py:414
  8.3 14.2 %copy-start.16 = (bf16[128]{0:T(256)(128)(2,1)S(1)}, bf16[128]{0:T(256)(128)(2,1)}, u32[]{:S(2)}) copy-start(bf16[128]{0:T(256)(128)(2,1)} %param.30) | copy-start | bytes 772
  8.4 30.4 %collective-permute-start.1 = (f32[256,1024]{1,0:T(8,128)S(1)}, f32[256,1024]{1,0:T(8,128)}, u32[]{:S(2)}, u32[]{:S(2)}) collective-permute-start(f32[256,1024]{1,0:T(8,128)S(1)} %maximum_convert_fusion), channel_id=1, source_target_pairs={{0,8},{8,0},{1,9},{9,1},{2,10},{10,2},{3,11},{11,3},{4,12},{12,4},... | collective-permute-start | bytes 3145736 | tf_op jit(solution)/shard_map/ppermute | solution.py:343
  14.2 9.0 %copy-start.14 = (s32[32]{0:T(128)}, s32[32]{0:T(128)S(1)}, u32[]{:S(2)}) copy-start(s32[32]{0:T(128)S(1)} %get-tuple-element.114.lens_ref) | copy-start | bytes 388
  14.2 9.0 %copy-start.15 = (s32[32]{0:T(128)}, s32[32]{0:T(128)S(1)}, u32[]{:S(2)}) copy-start(s32[32]{0:T(128)S(1)} %get-tuple-element.115.order_ref) | copy-start | bytes 388
  19.1 6.8 %copy-start.3 = (f32[2048]{0:T(1024)}, f32[2048]{0:T(1024)S(1)}, u32[]{:S(2)}) copy-start(f32[2048]{0:T(1024)S(1)} %convert_element_type.167) | copy-start | bytes 24580
  19.1 6.8 %copy-start.17 = (bf16[128]{0:T(256)(128)(2,1)S(1)}, bf16[128]{0:T(256)(128)(2,1)}, u32[]{:S(2)}) copy-start(bf16[128]{0:T(256)(128)(2,1)} %param.31) | copy-start | bytes 772
  38.9 136.1 %all-gather.10.cloned.1.call-start = ((), (), s32[]{:S(2)}) async-start(), calls=%async_computation.2 | async-start | bytes 11796480 | tf_op jit(solution)/shard_map/all_gather | solution.py:422
  41.1 35.6 %copy-start.9 = (f32[2,16,128]{2,1,0:T(8,128)S(1)}, f32[2,16,128]{2,1,0:T(8,128)}, u32[]{:S(2)}) copy-start(f32[2,16,128]{2,1,0:T(8,128)} %get-tuple-element.61) | copy-start | bytes 49156
  75.7 4.1 copy-start.10
  75.7 12.9 %copy-start.4 = (f32[2048]{0:T(1024)S(1)}, f32[2048]{0:T(1024)}, u32[]{:S(2)}) copy-start(f32[2048]{0:T(1024)} %copy-done.3) | copy-start | bytes 24580
  79.8 8.8 %collective-permute-start = (f32[34,2048]{1,0:T(8,128)S(1)}, f32[34,2048]{1,0:T(8,128)S(1)}, u32[]{:S(2)}, u32[]{:S(2)}) collective-permute-start(f32[34,2048]{1,0:T(8,128)S(1)} %fusion.93), channel_id=1, source_target_pairs={{0,8},{8,0},{1,9},{9,1},{2,10},{10,2},{3,11},{11,3},{4,12},{12,4},... | collective-permute-start | bytes 835592 | tf_op jit(solution)/shard_map/ppermute | solution.py:343
  104.5 8.3 %copy-start.11 = (bf16[2048]{0:T(1024)(128)(2,1)S(1)}, bf16[2048]{0:T(1024)(128)(2,1)}, u32[]{:S(2)}) copy-start(bf16[2048]{0:T(1024)(128)(2,1)} %param.33) | copy-start | bytes 12292
  111.4 10.5 %collective-permute-start.2 = (f32[34,2048]{1,0:T(8,128)S(1)}, f32[34,2048]{1,0:T(8,128)S(1)}, u32[]{:S(2)}, u32[]{:S(2)}) collective-permute-start(f32[34,2048]{1,0:T(8,128)S(1)} %fusion.94), channel_id=1, source_target_pairs={{0,8},{8,0},{1,9},{9,1},{2,10},{10,2},{3,11},{11,3},{4,12},{12,4},... | collective-permute-start | bytes 835592 | tf_op jit(solution)/shard_map/ppermute | solution.py:343
  132.6 10.4 %all-to-all-start = ((f32[8,2,2048]{2,1,0:T(2,128)}), f32[8,2,2048]{2,1,0:T(2,128)S(1)}, u32[]{:S(2)}, u32[]{:S(2)}) async-start(f32[8,2,2048]{2,1,0:T(2,128)} %all_to_all.6), calls=%async_computation | async-start | bytes 262144 | tf_op jit(solution)/shard_map/all_to_all | solution.py:444
  136.0 197.4 %all-gather.12.cloned.1.call-start = ((), (), s32[]{:S(2)}) async-start(), calls=%async_computation.3 | async-start | bytes 14745600 | tf_op jit(solution)/shard_map/all_gather | solution.py:422
  144.3 17.3 %slice-start = ((s8[12582912]{0:T(1024)(128)(4,1)}), s8[4194304]{0:T(1024)(128)(4,1)S(1)}, s32[]{:S(2)}) async-start(s8[12582912]{0:T(1024)(128)(4,1)} %bitcast.93), calls=%async_computation.6 | async-start | bytes 8388608
  144.3 17.3 %slice-start.1 = ((s8[12582912]{0:T(1024)(128)(4,1)}), s8[4194304]{0:T(1024)(128)(4,1)S(1)}, s32[]{:S(2)}) async-start(s8[12582912]{0:T(1024)(128)(4,1)} %bitcast.93), calls=%async_computation.7 | async-start | bytes 8388608
  152.9 8.6 %slice-start.2 = ((s8[12582912]{0:T(1024)(128)(4,1)}), s8[4194304]{0:T(1024)(128)(4,1)S(1)}, s32[]{:S(2)}) async-start(s8[12582912]{0:T(1024)(128)(4,1)} %bitcast.93), calls=%async_computation.8 | async-start | bytes 8388608
  161.6 5.4 %copy-start.18 = (s32[2]{0:T(128)S(1)}, s32[2]{0:T(128)}, u32[]{:S(2)}) copy-start(s32[2]{0:T(128)} %lens_ref.9) | copy-start | bytes 28
  165.5 8.6 %collective-permute-start.3 = (f32[34,2048]{1,0:T(8,128)S(1)}, f32[34,2048]{1,0:T(8,128)S(1)}, u32[]{:S(2)}, u32[]{:S(2)}) collective-permute-start(f32[34,2048]{1,0:T(8,128)S(1)} %convolution_add_fusion), channel_id=1, source_target_pairs={{0,8},{8,0},{1,9},{9,1},{2,10},{10,2},{3,11},{11,3},{4,12},{12,4},... | collective-permute-start | bytes 835592 | tf_op jit(solution)/shard_map/ppermute | solution.py:343
  183.5 282.4 %all-reduce.12.cloned.1.call-start = ((), (), s32[]{:S(2)}) async-start(), calls=%async_computation.5 | async-start | bytes 16777216 | tf_op jit(solution)/shard_map/psum | solution.py:470
  184.0 5.1 collective-permute-start.4
  193.7 3.7 copy-start
  198.8 5.1 collective-permute-start.5
  228.2 6.8 %copy-start.12 = (f32[8,128]{1,0:T(8,128)S(1)}, f32[8,128]{1,0:T(8,128)}, u32[]{:S(2)}) copy-start(f32[8,128]{1,0:T(8,128)} %get-tuple-element.104) | copy-start | bytes 12292
  228.2 6.8 %copy-start.13 = (f32[8,128]{1,0:T(8,128)S(1)}, f32[8,128]{1,0:T(8,128)}, u32[]{:S(2)}) copy-start(f32[8,128]{1,0:T(8,128)} %get-tuple-element.103) | copy-start | bytes 12292
  233.5 98.8 %collective-permute-start.6 = (f32[34,2048]{1,0:T(8,128)S(1)}, f32[34,2048]{1,0:T(8,128)S(1)}, u32[]{:S(2)}, u32[]{:S(2)}) collective-permute-start(f32[34,2048]{1,0:T(8,128)S(1)} %fusion.96), channel_id=1, source_target_pairs={{0,8},{8,0},{1,9},{9,1},{2,10},{10,2},{3,11},{11,3},{4,12},{12,4},... | collective-permute-start | bytes 835592 | tf_op jit(solution)/shard_map/ppermute | solution.py:343
  235.0 97.2 %collective-permute-start.7 = (f32[256]{0:T(256)S(1)}, f32[256]{0:T(256)S(1)}, u32[]{:S(2)}, u32[]{:S(2)}) collective-permute-start(f32[256]{0:T(256)S(1)} %pad_maximum_fusion.9), channel_id=1, source_target_pairs={{0,8},{8,0},{1,9},{9,1},{2,10},{10,2},{3,11},{11,3},{4,12},{12,4},... | collective-permute-start | bytes 3080 | tf_op jit(solution)/shard_map/ppermute | solution.py:343
  248.0 13.9 %copy-start.19 = (bf16[2,512,2048]{2,1,0:T(8,128)(2,1)S(1)}, bf16[2,512,2048]{2,1,0:T(8,128)(2,1)}, u32[]{:S(2)}) copy-start(bf16[2,512,2048]{2,1,0:T(8,128)(2,1)} %get-tuple-element.86.refs_0_) | copy-start | bytes 12582916
  248.0 14.0 %copy-start.21 = (bf16[2,512,512]{2,1,0:T(8,128)(2,1)S(1)}, bf16[2,512,512]{2,1,0:T(8,128)(2,1)}, u32[]{:S(2)}) copy-start(bf16[2,512,512]{2,1,0:T(8,128)(2,1)} %get-tuple-element.85.dv_ref) | copy-start | bytes 3145732
  248.0 18.5 %slice-start.3 = ((s8[16777216]{0:T(1024)(128)(4,1)}), s8[4194304]{0:T(1024)(128)(4,1)S(1)}, s32[]{:S(2)}) async-start(s8[16777216]{0:T(1024)(128)(4,1)} %bitcast.113), calls=%async_computation.9 | async-start | bytes 8388608
  248.0 18.5 %slice-start.4 = ((s8[16777216]{0:T(1024)(128)(4,1)}), s8[4194304]{0:T(1024)(128)(4,1)S(1)}, s32[]{:S(2)}) async-start(s8[16777216]{0:T(1024)(128)(4,1)} %bitcast.113), calls=%async_computation.10 | async-start | bytes 8388608
  248.1 18.5 %slice-start.5 = ((s8[16777216]{0:T(1024)(128)(4,1)}), s8[4194304]{0:T(1024)(128)(4,1)S(1)}, s32[]{:S(2)}) async-start(s8[16777216]{0:T(1024)(128)(4,1)} %bitcast.113), calls=%async_computation.11 | async-start | bytes 8388608
  262.0 4.6 slice-start.6
  266.6 16.2 %copy-start.20 = (bf16[2,512,512]{2,1,0:T(8,128)(2,1)S(1)}, bf16[2,512,512]{2,1,0:T(8,128)(2,1)}, u32[]{:S(2)}) copy-start(bf16[2,512,512]{2,1,0:T(8,128)(2,1)} %get-tuple-element.84.dk_ref) | copy-start | bytes 3145732
  342.0 159.6 %all-gather.14.cloned.1.call-start = ((), (), s32[]{:S(2)}) async-start(), calls=%async_computation.4 | async-start | bytes 1474560 | tf_op jit(solution)/shard_map/all_gather | solution.py:422
  473.9 14.1 %copy-start.5 = (f32[8,2048]{1,0:T(8,128)S(1)}, f32[8,2048]{1,0:T(8,128)}, u32[]{:S(2)}) copy-start(f32[8,2048]{1,0:T(8,128)} %get-tuple-element.101) | copy-start | bytes 196612
  473.9 14.1 %copy-start.6 = (f32[8,2048]{1,0:T(8,128)S(1)}, f32[8,2048]{1,0:T(8,128)}, u32[]{:S(2)}) copy-start(f32[8,2048]{1,0:T(8,128)} %get-tuple-element.102) | copy-start | bytes 196612
  473.9 14.1 %copy-start.7 = (f32[2048]{0:T(1024)S(1)}, f32[2048]{0:T(1024)}, u32[]{:S(2)}) copy-start(f32[2048]{0:T(1024)} %get-tuple-element.107) | copy-start | bytes 24580
  473.9 14.1 %copy-start.8 = (f32[2048]{0:T(1024)S(1)}, f32[2048]{0:T(1024)}, u32[]{:S(2)}) copy-start(f32[2048]{0:T(1024)} %get-tuple-element.105) | copy-start | bytes 24580
  501.6 7.7 %copy-start.2 = (f32[2048,512]{1,0:T(8,128)S(1)}, f32[2048,512]{1,0:T(8,128)}, u32[]{:S(2)}) copy-start(f32[2048,512]{1,0:T(8,128)} %get-tuple-element.178) | copy-start | bytes 12582916
  509.3 3.7 copy-start.1
Sparse Core Ops, SparseCore 0:
  39.0 50.5 all-gather.7
  104.6 61.0 all-gather.9
  183.6 69.5 all-gather.11
  342.1 117.4 all-reduce.11
  466.7 23.5 all-gather.13
